TPU v7x, 256 devices: a whole 4x4x8 slice. The times are simulated.
256 devices in a mesh: dp: 32 (over z, y), mp: 8 (over x, core).
Axes of the slice: x: 4, y: 4, z: 8, core: 2. Of those that a mesh axis runs over, the one named last changes fastest.
Arguments:
- embedded: bfloat16 [128, 64, 4096], P('dp', None, 'mp'), may hold values from -6 to 6
- targets: int32 [128, 64], P('dp'), may hold values from 0 to 65535
- labels: int32 [128], P('dp'), may hold values from 0 to 21
- counts: int32 [32], replicated, may hold values from 0 to 4, as said below
- destinations: int32 [128], P('dp'), may hold values from 0 to 63, as said below
- gain_in: float32 [4096], replicated, may hold values from 0.1 to 1.9
- w_query: bfloat16 [4096, 2048], P(None, 'mp'), may hold values from -40 to 40
- w_key: bfloat16 [4096, 1024], P(None, 'mp'), may hold values from -0.09375 to 0.09375
- w_value: bfloat16 [4096, 1024], P(None, 'mp'), may hold values from -0.09375 to 0.09375
- w_out: bfloat16 [2048, 4096], P('mp'), may hold values from -0.5 to 0.5
- gain_out: float32 [4096], replicated, may hold values from 0.1 to 1.9
- w_vocab: bfloat16 [4096, 65536], P('mp', 'dp'), may hold values from -40 to 40
- prev_probs: float32 [22], replicated, may hold values from 0.03 to 0.2
- log_weights: float32 [22], replicated, may hold values from -200 to 21000
Outputs:
- token_loss: float32 [4096], P(('dp', 'mp'))
- new_weights: float32 [22], replicated
- probs: float32 [22], replicated
Inputs may be any that keep to these rules, and one draw needn't show every extreme that they name: The counts sum to 64. `destinations`: each value from 0 to 63 is held by exactly one live slot; entries of slots that are not live are meaningless.
All inputs are finite; a program needn't handle non-finite values.
Results may differ from a plain program's by a relative error of at most 0.015.
The roundings to bfloat16 on the way count: a program that leaves them out, or rounds other values in their place, can miss the bound.
Values may be sent and summed in bfloat16 or wider, within the bound.
No kernel may reach another device: no remote copies, remote signals or barrier semaphores. Data moves between devices by JAX's collectives and lax.ppermute only.
A program may use at most 128 MiB of HBM per device.

v0:
```python
import functools

import jax
import jax.numpy as jnp
import numpy as np
from jax import lax
from jax.experimental import pallas as pl
from jax.experimental.pallas import tpu as pltpu
from jax.sharding import Mesh
from jax.sharding import PartitionSpec as P


HEAD_DIM = 128
DOMAINS = 22
SEQ_LEN = 64
DP = ("z", "y")
MP = ("x", "c")
ALL = ("z", "y", "x", "c")
NZ, NY, NX, NC = 8, 4, 4, 2

norm_eps = 1e-05
rope_base = 500000.0
memory_rate = 0.9
step_rate = 0.02
explore_mass = 0.005


bf16 = jnp.bfloat16
f32 = jnp.float32
i32 = jnp.int32


def shift(array, axis, by):
    n = {"z": NZ, "y": NY, "x": NX, "c": NC}[axis]
    return lax.ppermute(array, axis, [(i, (i + by) % n) for i in range(n)])


def call(kernel, out_shape, args, scalars=None, scratch=(), flops=0, vmem=None):
    spec = pl.BlockSpec(memory_space=pltpu.VMEM)
    many = isinstance(out_shape, (list, tuple))
    params = {} if vmem is None else {"vmem_limit_bytes": vmem}
    return pl.pallas_call(
        kernel,
        out_shape=out_shape,
        in_specs=([pl.BlockSpec(memory_space=pltpu.SMEM)] if scalars is not None else [])
        + [spec] * len(args),
        out_specs=[spec] * len(out_shape) if many else spec,
        scratch_shapes=scratch,
        compiler_params=pltpu.CompilerParams(**params),
        cost_estimate=pl.CostEstimate(flops=flops, bytes_accessed=0, transcendentals=0)
        if flops
        else None,
    )(*(() if scalars is None else (scalars,)), *args)


def sds(shape, dtype):
    return jax.ShapeDtypeStruct(shape, dtype)


def pack_kernel(embedded, targets, labels, destinations, out_ref, meta_ref):
    ids = targets[...]
    meta_ref[...] = jnp.zeros((8, 128), f32)
    meta_ref[0:4, 0:64] = (ids // 256).astype(f32)
    meta_ref[0:4, 64:128] = (ids % 256).astype(f32)
    meta_ref[4:5, 0:4] = labels[...].astype(f32)
    meta_ref[5:6, 0:4] = destinations[...].astype(f32)
    meta = meta_ref[...].astype(bf16)
    for r in range(8):
        for col in range(4):
            for s in range(4):
                out_ref[r * 4 + col, s] = embedded[
                    s, r * 8 : r * 8 + 8, col * 128 : col * 128 + 128
                ]
            out_ref[r * 4 + col, 4] = meta


def select_kernel(row_ref, got_ref, out_ref):
    for g in range(64):
        out_ref[g] = got_ref[row_ref[g]]


def rope_tables():
    half = HEAD_DIM // 2
    frequency = np.power(rope_base, -np.arange(half) * 2.0 / HEAD_DIM)
    angle = np.arange(SEQ_LEN)[:, None] * frequency[None, :]
    cosine = np.concatenate([np.cos(angle), np.cos(angle)], axis=1)
    sine = np.concatenate([-np.sin(angle), np.sin(angle)], axis=1)
    both = [np.concatenate([t, t], axis=0).astype(np.float32) for t in (cosine, sine)]
    return both


def attention_kernel(
    at_ref, same, other, gain, wq, wk, wv, wo, cos, sin, keep_ref, send_ref, resid_ref, mixed_ref
):
    x, c = at_ref[0], at_ref[1]
    m = x * 2 + c
    blocks = [same.at[t] for t in range(4)] + [other.at[t] for t in range(4)]

    def feature_block(k):
        return (k % 4) * 2 + (c if k < 4 else 1 - c)

    def piece(ref, col):
        return jnp.concatenate([ref[r * 4 + col] for r in range(8)], axis=0).astype(f32)

    squares = jnp.zeros((128, 128), f32)
    for ref in blocks:
        for col in range(4):
            v = piece(ref, col)
            squares = squares + v * v
    inv_rms = lax.rsqrt(jnp.sum(squares, axis=1, keepdims=True) * (1.0 / 4096.0) + norm_eps)

    query = jnp.zeros((128, 256), f32)
    key = jnp.zeros((128, 128), f32)
    value = jnp.zeros((128, 128), f32)
    for k, ref in enumerate(blocks):
        fb = feature_block(k)
        g = gain[fb]
        normed = jnp.concatenate(
            [
                (piece(ref, col) * inv_rms * g[:, col * 128 : col * 128 + 128]).astype(bf16)
                for col in range(4)
            ],
            axis=1,
        )
        rows = pl.ds(pl.multiple_of(fb * 512, 512), 512)
        query = query + jnp.dot(normed, wq[rows, :], preferred_element_type=f32)
        key = key + jnp.dot(normed, wk[rows, :], preferred_element_type=f32)
        value = value + jnp.dot(normed, wv[rows, :], preferred_element_type=f32)

    def in_order(t):
        return jnp.concatenate(
            [t[r * 16 + s * 8 : r * 16 + s * 8 + 8] for s in range(2) for r in range(8)], axis=0
        )

    cosine, sine = cos[...], sin[...]

    def rotated(t):
        return (t * cosine + pltpu.roll(t, 64, axis=1) * sine).astype(bf16)

    query, key, value = in_order(query), rotated(in_order(key)), in_order(value).astype(bf16)
    row = lax.broadcasted_iota(i32, (128, 128), 0)
    column = lax.broadcasted_iota(i32, (128, 128), 1)
    seen = (row // SEQ_LEN == column // SEQ_LEN) & (column <= row)
    for h in range(2):
        q = rotated(query[:, h * 128 : h * 128 + 128])
        scores = lax.dot_general(q, key, (((1,), (1,)), ((), ())), preferred_element_type=f32)
        scores = jnp.where(seen, scores * HEAD_DIM ** (-0.5), -jnp.inf)
        top = jnp.max(scores, axis=1, keepdims=True)
        e = jnp.exp(scores - top)
        weights = (e / jnp.sum(e, axis=1, keepdims=True)).astype(bf16)
        mixed = jnp.dot(weights, value, preferred_element_type=f32).astype(bf16)
        mixed_ref[:, :, h * 128 : h * 128 + 128] = mixed.reshape(8, 16, 128)
    left = jnp.concatenate(
        [mixed_ref[t * 2 + c] for t in range(4)] + [mixed_ref[t * 2 + 1 - c] for t in range(4)],
        axis=0,
    )
    for fb in range(8):
        part = jnp.dot(left, wo[:, fb * 512 : fb * 512 + 512], preferred_element_type=f32)
        part = part.astype(bf16).reshape(8, 16, 512)
        keep_ref[:, fb] = part[:4]
        send_ref[:, fb] = part[4:]

    first = m < 4
    r0 = lax.rem(m, 4) * 2
    for k, ref in enumerate(blocks):
        fb = feature_block(k)
        rows = []
        for r in range(2):
            cols = []
            for col in range(4):
                v = ref[(r0 + r) * 4 + col].astype(f32)
                cols.append(jnp.where(first, v[:8], v[8:]))
            rows.append(jnp.concatenate(cols, axis=1))
        resid_ref[fb] = jnp.concatenate(rows, axis=0).astype(bf16)


def pair_kernel(keep_ref, got_ref, out_ref):
    out_ref[...] = (keep_ref[...].astype(f32) + got_ref[...].astype(f32)).astype(bf16)


def final_kernel(at_ref, resid, sums, gain, fa_ref, fb_ref, hidden_ref):
    x, c = at_ref[0], at_ref[1]
    squares = jnp.zeros((16, 512), f32)
    for k in range(8):
        h = resid[k].astype(f32) + (
            (sums[0, k].astype(f32) + sums[1, k].astype(f32))
            + (sums[2, k].astype(f32) + sums[3, k].astype(f32))
        )
        hidden_ref[k] = h
        squares = squares + h * h
    inv_rms = lax.rsqrt(jnp.sum(squares, axis=1, keepdims=True) * (1.0 / 4096.0) + norm_eps)
    for s in range(4):
        base = lax.rem(x + (4 - s), 4) * 2
        fa_ref[s] = (hidden_ref[base + c] * inv_rms * gain[base + c]).astype(bf16)
        other = base + 1 - c
        rows = (hidden_ref[other] * inv_rms * gain[other]).astype(bf16)
        for t in range(8):
            fb_ref[t, s] = rows


BLOCKS = 4
WIDTH = 512


def fetch(pieces, buffer, sems):
    copies = [
        [
            pltpu.make_async_copy(
                ref.at[pl.ds(lo, 256), pl.ds(j * WIDTH, WIDTH)],
                buffer.at[j, pl.ds(p * 256, 256)],
                sems.at[j, p],
            )
            for p, (ref, lo) in enumerate(pieces)
        ]
        for j in range(BLOCKS)
    ]
    for block in copies:
        for copy in block:
            copy.start()
    return copies


def lay_rows(rows_ref, parts):
    for to, take in parts:
        at = pl.ds(pl.multiple_of(to * 16, 16), 16)
        for k in range(4):
            rows_ref[at, k * 512 : k * 512 + 512] = take(k)


def first_kernel(at_ref, own, f1, f2, f3, g1, g2, g3, *refs):
    rows = refs[:8]
    out_ref, buffer, rows_ref, sems = refs[8:]
    pieces = [(own, 0), (own, 256), (f1, 0), (g1, 0), (f2, 0), (g2, 0), (f3, 0), (g3, 0)]
    copies = fetch(pieces, buffer, sems)
    z, y = at_ref[2], at_ref[3]
    parts = []
    for dz in range(8):
        for dy in range(4):
            to = lax.rem(z + (8 - dz), 8) * 4 + lax.rem(y + (4 - dy), 4)
            parts.append((to, functools.partial(lambda dz, dy, k: rows[dz][dy, k], dz, dy)))
    lay_rows(rows_ref, parts)
    for j in range(BLOCKS):
        for copy in copies[j]:
            copy.wait()
        out_ref[j] = jnp.dot(rows_ref[...], buffer[j], preferred_element_type=f32)


def second_kernel(at_ref, own, first, second, *refs):
    rows = refs[:4]
    part_ref, goal_ref, out_ref, buffer, rows_ref, sems = refs[4:]
    pieces = [(own, 0), (own, 256)]
    for s in range(3):
        pieces += [(first, s * 256), (second, s * 256)]
    copies = fetch(pieces, buffer, sems)
    y = at_ref[3]
    parts = []
    for dz in range(8):
        for dy in range(4):
            to = dz * 4 + lax.rem(y + (4 - dy), 4)
            parts.append((to, functools.partial(lambda dz, dy, k: rows[dy][dz, k], dz, dy)))
    lay_rows(rows_ref, parts)
    top = jnp.full((512, 1), -jnp.inf, f32)
    total = jnp.zeros((512, 1), f32)
    picked = jnp.zeros((512, 1), f32)
    goal = goal_ref[...]
    for j in range(BLOCKS):
        for copy in copies[j]:
            copy.wait()
        logits = part_ref[j] + jnp.dot(rows_ref[...], buffer[j], preferred_element_type=f32)
        column = lax.broadcasted_iota(i32, logits.shape, 1) + j * WIDTH
        new = jnp.maximum(top, jnp.max(logits, axis=1, keepdims=True))
        total = total * jnp.exp(top - new) + jnp.sum(
            jnp.exp(logits - new), axis=1, keepdims=True
        )
        picked = picked + jnp.sum(jnp.where(column == goal, logits, 0.0), axis=1, keepdims=True)
        top = new
    eye = lax.broadcasted_iota(i32, (128, 128), 0) == lax.broadcasted_iota(i32, (128, 128), 1)
    lines = []
    for values in (top + jnp.log(total), picked):
        for q in range(4):
            block = jnp.where(eye, values[q * 128 : q * 128 + 128], 0.0)
            lines.append(jnp.sum(block, axis=0, keepdims=True))
    lines = jnp.concatenate(lines, axis=0)
    for t in range(32):
        out_ref[t] = lines


def logits_call(kernel, at, weights, rest, out_shape):
    vmem = pl.BlockSpec(memory_space=pltpu.VMEM)
    return pl.pallas_call(
        kernel,
        out_shape=out_shape,
        in_specs=[pl.BlockSpec(memory_space=pltpu.SMEM)]
        + [pl.BlockSpec(memory_space=pltpu.HBM)] * len(weights)
        + [vmem] * len(rest),
        out_specs=vmem,
        scratch_shapes=[
            pltpu.VMEM((BLOCKS, 2048, WIDTH), bf16),
            pltpu.VMEM((512, 2048), bf16),
            pltpu.SemaphoreType.DMA((BLOCKS, 8)),
        ],
        cost_estimate=pl.CostEstimate(
            flops=2 * 512 * 2048 * 2048, bytes_accessed=12 << 20, transcendentals=0
        ),
        compiler_params=pltpu.CompilerParams(vmem_limit_bytes=40 << 20),
    )(at, *weights, *rest)


def merge_kernel(got_ref, label_ref, loss_ref, sums_ref):
    lse = [got_ref[k][:4] for k in range(32)]
    top = functools.reduce(jnp.maximum, lse)
    total = functools.reduce(lambda a, b: a + b, [jnp.exp(v - top) for v in lse])
    picked = functools.reduce(lambda a, b: a + b, [got_ref[k][4:] for k in range(32)])
    loss = top + jnp.log(total) - picked
    loss_ref[...] = loss
    domain = lax.broadcasted_iota(i32, (128, 128), 0)
    by_domain = jnp.zeros((128, 128), f32)
    for q in range(4):
        same = domain == label_ref[q : q + 1, :]
        by_domain = by_domain + jnp.where(same, loss[q : q + 1, :], 0.0)
    column = jnp.sum(by_domain, axis=1, keepdims=True)
    eye = domain == lax.broadcasted_iota(i32, (128, 128), 1)
    line = jnp.sum(jnp.where(eye, column, 0.0), axis=0, keepdims=True)
    for t in range(8):
        sums_ref[t] = jnp.broadcast_to(line, (8, 128))


def output_kernel(sums_ref, tally, prev, old, new_ref, probs_ref):
    sums = sums_ref[0]
    for t in range(1, 8):
        sums = sums + sums_ref[t]
    sums = sums[0:1]
    reward = sums / jnp.maximum(tally[...], 1.0) / prev[...]
    new = memory_rate * old[...] + (1.0 - memory_rate) * reward
    real = lax.broadcasted_iota(i32, (1, 128), 1) < DOMAINS
    scaled = jnp.where(real, step_rate * new, -jnp.inf)
    e = jnp.exp(scaled - jnp.max(scaled, axis=1, keepdims=True))
    soft = e / jnp.sum(e, axis=1, keepdims=True)
    new_ref[...] = new
    probs_ref[...] = (1.0 - DOMAINS * explore_mass) * soft + explore_mass


def program(
    embedded, targets, labels, counts, destinations, gain_in, w_query, w_key, w_value, w_out,
    gain_out, w_vocab, prev_probs, log_weights,
):
    z, y, x, c = (lax.axis_index(a) for a in ALL)
    d, m = z * NY + y, x * NC + c
    at = jnp.stack([x, c, z, y]).astype(i32)

    w_other = shift(w_vocab, "c", 1)
    rows = w_vocab[:256]
    w_first = [shift(rows, "x", s) for s in (1, 2, 3)]

    packed = call(
        pack_kernel, sds((32, 5, 8, 128), bf16),
        (embedded, targets, labels.reshape(1, 4), destinations.reshape(1, 4)),
        scratch=[pltpu.VMEM((8, 128), f32)],
    )
    got = lax.all_to_all(packed, DP, 0, 0, tiled=True)

    meta = got[:, 4]
    label_of = meta[:, 4, 0:4].reshape(128).astype(i32)
    goes_to = meta[:, 5, 0:4].reshape(128).astype(i32)
    slot = jnp.arange(128, dtype=i32)
    live = slot % 4 < jnp.repeat(counts, 4)
    chosen = live[None, :] & (goes_to[None, :] == jnp.arange(64, dtype=i32)[:, None])
    source_row = jnp.sum(jnp.where(chosen, (slot // 4) * 5 + slot % 4, 0), axis=1)
    picked = call(select_kernel, sds((64, 8, 128), bf16), (got.reshape(160, 8, 128),), source_row)
    block = lax.all_to_all(picked.reshape(32, 16, 128), DP, 0, 0, tiled=True)

    same = lax.all_gather(block, "x", axis=0, tiled=False)
    other = shift(same, "c", 1)

    cosine, sine = rope_tables()
    keep, send, resid = call(
        attention_kernel,
        [sds((4, 8, 16, 512), bf16), sds((4, 8, 16, 512), bf16), sds((8, 16, 512), bf16)],
        (
            same, other, gain_in.reshape(8, 1, 512), w_query, w_key, w_value, w_out,
            jnp.asarray(cosine), jnp.asarray(sine),
        ),
        at,
        scratch=[pltpu.VMEM((8, 16, 256), bf16)],
        flops=1 << 30,
    )
    got_part = shift(send, "c", 1)
    pair = call(pair_kernel, sds((4, 8, 16, 512), bf16), (keep, got_part))
    sums = lax.all_to_all(pair, "x", 0, 0, tiled=True)

    (_, first_w, own_w) = lax.optimization_barrier((pair, tuple(w_first), w_vocab))
    rows = own_w[256:]
    w_second = [shift(rows, "x", s) for s in (1, 2, 3)]
    w_first_other = shift(jnp.concatenate(first_w, axis=0), "c", 1)

    fa, fb = call(
        final_kernel, [sds((4, 16, 512), bf16), sds((8, 4, 16, 512), bf16)],
        (resid, sums, gain_out.reshape(8, 1, 512)), at,
        scratch=[pltpu.VMEM((8, 16, 512), f32)],
    )

    parts = [shift(fa, "y", s) for s in (1, 2, 3)]
    column = lax.all_to_all(fb, "z", 0, 0, tiled=True)
    group = jnp.stack([fa, *parts])
    up, down = [group], [group]
    for _ in range(3):
        up.append(shift(up[-1], "z", 1))
        down.append(shift(down[-1], "z", NZ - 1))
    rows_b = [column] + [shift(column, "y", s) for s in (1, 2, 3)]
    up.append(shift(up[-1], "z", 1))
    rows_a = [*up, down[3], down[2], down[1]]
    w_second_other = shift(jnp.concatenate(w_second, axis=0), "c", 1)

    seq_ids = jnp.dot(
        chosen.astype(bf16), meta[:, :4].reshape(128, 128), preferred_element_type=f32
    ).astype(i32)
    seq_goals = seq_ids[:, :64] * 256 + seq_ids[:, 64:]
    seq_labels = jnp.sum(jnp.where(chosen, label_of[None, :], 0), axis=1)
    mine = lax.dynamic_slice(
        seq_goals.reshape(32, 2, 4, 16), (0, m // 4, m % 4, 0), (32, 1, 1, 16)
    ).reshape(512)
    kinds = lax.dynamic_slice(seq_labels.reshape(32, 2), (0, m // 4), (32, 1))
    kinds = jnp.broadcast_to(kinds, (32, 16)).reshape(4, 128)
    goals = (mine - d * 2048).reshape(512, 1)
    domain = jnp.arange(128, dtype=i32)
    tally = SEQ_LEN * jnp.sum(
        (live[:, None] & (label_of[:, None] == domain[None, :])).astype(f32), axis=0
    )

    partial = logits_call(
        first_kernel, at, (w_vocab, *w_first, *w_second), rows_a,
        sds((BLOCKS, 512, WIDTH), f32),
    )
    pieces = logits_call(
        second_kernel, at, (w_other, w_first_other, w_second_other), (*rows_b, partial, goals),
        sds((32, 8, 128), f32),
    )
    merged = lax.all_to_all(pieces, DP, 0, 0, tiled=True)
    losses, sums_here = call(
        merge_kernel, [sds((4, 128), f32), sds((8, 8, 128), f32)], (merged, kinds)
    )
    own_loss = lax.dynamic_slice_in_dim(losses.reshape(512), d * 16, 16, 0)
    all_sums = lax.all_to_all(sums_here, MP, 0, 0, tiled=True)
    line = lambda v, fill: jnp.pad(v, (0, 128 - DOMAINS), constant_values=fill).reshape(1, 128)
    new_weights, probs = call(
        output_kernel, [sds((1, 128), f32)] * 2,
        (all_sums, tally.reshape(1, 128), line(prev_probs, 1.0), line(log_weights, 0.0)),
    )
    return own_loss, new_weights[0, :DOMAINS], probs[0, :DOMAINS]


def solution(mesh):
    torus = Mesh(mesh.devices.reshape(NZ, NY, NX, NC), ALL)
    in_specs = (
        P(DP, None, MP), P(DP, None), P(DP), P(), P(DP), P(), P(None, MP), P(None, MP),
        P(None, MP), P(MP, None), P(), P(MP, DP), P(), P(),
    )
    return jax.shard_map(
        program, mesh=torus, in_specs=in_specs, out_specs=(P(ALL), P(), P()), check_vma=False
    )
```

profile of v0, /device:TPU:1, one launch (start us, length us, event | category | flops | bytes accessed | tf_op | source)
XLA Modules:
  0.0 295.0 jit_solution(7877206272867476593)
XLA Ops:
  0.6 1.9 shard_map.175
  2.6 12.0 %all-to-all-start = ((bf16[32,5,8,128]{3,2,1,0:T(8,128)(2,1)}), bf16[32,5,8,128]{3,2,1,0:T(8,128)(2,1)S(1)}, u32[]{:S(2)}, u32[]{:S(2)}) async-start(bf16[32,5,8,128]{3,2,1,0:T(8,128)(2,1)} %shard_map.175), calls=%async_computation | async-start | bytes 655360 | tf_op jit(solution)/shard_map/all_to_all | solution.py:360
  15.5 11.8 %all-to-all-done = bf16[32,5,8,128]{3,2,1,0:T(8,128)(2,1)S(1)} async-done(((bf16[32,5,8,128]{3,2,1,0:T(8,128)(2,1)}), bf16[32,5,8,128]{3,2,1,0:T(8,128)(2,1)S(1)}, u32[]{:S(2)}, u32[]{:S(2)}) %all-to-all-start) | async-done | bytes 327712 | tf_op jit(solution)/shard_map/all_to_all | solution.py:360
  28.3 1.7 shard_map.176
  30.0 14.2 %all_to_all.30 = bf16[32,16,128]{2,1,0:T(8,128)(2,1)S(1)} all-to-all(bf16[32,16,128]{2,1,0:T(8,128)(2,1)} %bitcast.31), channel_id=1, replica_groups=mesh['z'=8,'y'=4,'x'=4,'c'=2] {'z','y'}, dimensions={0} | all-to-all | bytes 262144 | tf_op jit(solution)/shard_map/all_to_all | solution.py:370
  44.1 11.0 %all-gather = bf16[128,16,128]{2,1,0:T(8,128)(2,1)} all-gather(bf16[32,16,128]{2,1,0:T(8,128)(2,1)S(1)} %all_to_all.30), channel_id=2, replica_groups=mesh['z'=8,'y'=4,'x'=4,'c'=2] {'x'}, dimensions={0}, use_global_device_ids=true | all-gather | bytes 655360 | tf_op jit(solution)/shard_map/all_gather | solution.py:372
  55.2 6.2 %collective-permute-start.1 = (bf16[4,32,16,128]{3,2,1,0:T(8,128)(2,1)}, bf16[4,32,16,128]{3,2,1,0:T(8,128)(2,1)}, u32[]{:S(2)}, u32[]{:S(2)}) collective-permute-start(bf16[4,32,16,128]{3,2,1,0:T(8,128)(2,1)} %bitcast.9.same), channel_id=1, source_target_pairs={{0,1},{1,0},{2,3},{3,2},{4,5},{5,4},{6,7},{7,6},{8,9},{9,8},{10,11... | collective-permute-start | bytes 1572872 | tf_op jit(solution)/shard_map/ppermute | solution.py:35
  62.8 2.4 collective-permute-start.4
  66.4 6.4 %shard_map.177 = (bf16[4,8,16,512]{3,2,1,0:T(8,128)(2,1)}, bf16[4,8,16,512]{3,2,1,0:T(8,128)(2,1)}, bf16[8,16,512]{2,1,0:T(8,128)(2,1)}) custom-call(s32[4]{0:T(128)} %pad_add_fusion.at_ref, bf16[4,32,16,128]{3,2,1,0:T(8,128)(2,1)} %bitcast.9.same, bf16[4,32,16,128]{3,2,1,0:T(8,128)(2,1)} %collective-permute-done.1.other, f32[8,1,512]{2,1,0:T(1,128)} %bitcast.37, ...), custom_call_target="tpu_custom_call" | custom-call | flops 1073741824 | tf_op jit(solution)/shard_map/pallas_call | solution.py:42
  73.6 1.9 collective-permute-done.2.got_ref
  75.5 2.1 shard_map.178
  77.6 11.1 %collective-permute-done.3.f1 = bf16[256,2048]{1,0:T(8,128)(2,1)S(1)} collective-permute-done((bf16[256,2048]{1,0:T(8,128)(2,1)}, bf16[256,2048]{1,0:T(8,128)(2,1)S(1)}, u32[]{:S(2)}, u32[]{:S(2)}) %collective-permute-start.3) | collective-permute-done | bytes 1048608 | tf_op jit(solution)/shard_map/ppermute | solution.py:35
  88.6 22.6 %collective-permute-done.4.f2 = bf16[256,2048]{1,0:T(8,128)(2,1)} collective-permute-done((bf16[256,2048]{1,0:T(8,128)(2,1)}, bf16[256,2048]{1,0:T(8,128)(2,1)}, u32[]{:S(2)}, u32[]{:S(2)}) %collective-permute-start.4) | collective-permute-done | bytes 1048608 | tf_op jit(solution)/shard_map/ppermute | solution.py:35
  111.6 1.3 collective-permute-start.7
  112.9 3.0 %collective-permute-start.8 = (bf16[256,2048]{1,0:T(8,128)(2,1)S(1)}, bf16[256,2048]{1,0:T(8,128)(2,1)S(1)}, u32[]{:S(2)}, u32[]{:S(2)}) collective-permute-start(bf16[256,2048]{1,0:T(8,128)(2,1)S(1)} %slice.33), channel_id=1, source_target_pairs={{0,4},{2,6},{4,0},{6,2},{1,5},{3,7},{5,1},{7,3},{8,12},{10,14},{12... | collective-permute-start | bytes 3145736 | tf_op jit(solution)/shard_map/ppermute | solution.py:35
  115.9 3.1 %pad_maximum_fusion = bf16[768,2048]{1,0:T(8,128)(2,1)} fusion(bf16[256,2048]{1,0:T(8,128)(2,1)} %collective-permute-done.5.f3, bf16[256,2048]{1,0:T(8,128)(2,1)} %collective-permute-done.4.f2, bf16[256,2048]{1,0:T(8,128)(2,1)S(1)} %collective-permute-done.3.f1), kind=kLoop, calls=%fused_computation | loop fusion | flops 9437184 | bytes 6291456 | tf_op jit(solution)/shard_map/concatenate | solution.py:394
  120.0 17.1 %collective-permute-done.7.g1 = bf16[256,2048]{1,0:T(8,128)(2,1)S(1)} collective-permute-done((bf16[256,2048]{1,0:T(8,128)(2,1)S(1)}, bf16[256,2048]{1,0:T(8,128)(2,1)S(1)}, u32[]{:S(2)}, u32[]{:S(2)}) %collective-permute-start.7) | collective-permute-done | bytes 1048608 | tf_op jit(solution)/shard_map/ppermute | solution.py:35
  137.1 24.0 %collective-permute-done.8.g2 = bf16[256,2048]{1,0:T(8,128)(2,1)S(1)} collective-permute-done((bf16[256,2048]{1,0:T(8,128)(2,1)S(1)}, bf16[256,2048]{1,0:T(8,128)(2,1)S(1)}, u32[]{:S(2)}, u32[]{:S(2)}) %collective-permute-start.8) | collective-permute-done | bytes 1048608 | tf_op jit(solution)/shard_map/ppermute | solution.py:35
  161.1 1.9 pad_maximum_fusion.1
  163.4 1.3 collective-permute-start.10
  164.8 12.1 %all_to_all.31.sums = bf16[4,8,16,512]{3,2,1,0:T(8,128)(2,1)} all-to-all(bf16[4,8,16,512]{3,2,1,0:T(8,128)(2,1)S(1)} %copy-done.13), channel_id=1, replica_groups=mesh['z'=8,'y'=4,'x'=4,'c'=2] {'x'}, dimensions={0} | all-to-all | bytes 1048576 | tf_op jit(solution)/shard_map/all_to_all | solution.py:389
  176.9 2.1 shard_map.179
  179.0 2.3 collective-permute-start.15
  181.3 3.0 %collective-permute-done.14 = bf16[4,16,512]{2,1,0:T(8,128)(2,1)S(1)} collective-permute-done((bf16[4,16,512]{2,1,0:T(8,128)(2,1)}, bf16[4,16,512]{2,1,0:T(8,128)(2,1)S(1)}, u32[]{:S(2)}, u32[]{:S(2)}) %collective-permute-start.14) | collective-permute-done | bytes 65568 | tf_op jit(solution)/shard_map/ppermute | solution.py:35
  184.2 3.3 %collective-permute-done.16 = bf16[4,16,512]{2,1,0:T(8,128)(2,1)S(1)} collective-permute-done((bf16[4,16,512]{2,1,0:T(8,128)(2,1)}, bf16[4,16,512]{2,1,0:T(8,128)(2,1)S(1)}, u32[]{:S(2)}, u32[]{:S(2)}) %collective-permute-start.16) | collective-permute-done | bytes 65568 | tf_op jit(solution)/shard_map/ppermute | solution.py:35
  188.5 4.2 %all-to-all-start.3 = ((bf16[8,4,16,512]{3,2,1,0:T(8,128)(2,1)}), bf16[8,4,16,512]{3,2,1,0:T(8,128)(2,1)}, u32[]{:S(2)}, u32[]{:S(2)}) async-start(bf16[8,4,16,512]{3,2,1,0:T(8,128)(2,1)} %get-tuple-element.23), calls=%async_computation.3 | async-start | bytes 1048576 | tf_op jit(solution)/shard_map/all_to_all | solution.py:403
  192.7 2.7 collective-permute-start.21
  195.4 14.2 %collective-permute-done.21.refs_7_ = bf16[4,4,16,512]{3,2,1,0:T(8,128)(2,1)S(1)} collective-permute-done((bf16[4,4,16,512]{3,2,1,0:T(8,128)(2,1)S(1)}, bf16[4,4,16,512]{3,2,1,0:T(8,128)(2,1)S(1)}, u32[]{:S(2)}, u32[]{:S(2)}) %collective-permute-start.21) | collective-permute-done | bytes 262176 | tf_op jit(solution)/shard_map/ppermute | solution.py:35
  211.4 2.2 collective-permute-done.18.refs_2_
  215.2 2.1 collective-permute-start.23
  217.3 2.9 collective-permute-done.19.refs_3_
  220.4 1.8 collective-permute-done.23.refs_5_
  222.2 1.9 collective-permute-start.12
  224.1 2.8 collective-permute-done.20.refs_4_
  226.9 2.6 collective-permute-start.13
  231.6 1.6 sub.32.refs_5_
  233.3 1.2 copy-done.2
  234.5 1.2 copy-done.4
  235.7 1.2 copy-done.6
  238.9 9.7 %shard_map.180.refs_4_ = f32[4,512,512]{2,1,0:T(8,128)} custom-call(s32[4]{0:T(128)S(1)} %copy-done.8, bf16[512,2048]{1,0:T(8,128)(2,1)S(1)} %copy-done, bf16[256,2048]{1,0:T(8,128)(2,1)S(1)} %collective-permute-done.3.f1, bf16[256,2048]{1,0:T(8,128)(2,1)} %collective-permute-done.4.f2, bf16[256,2048]{1,0:T(8,128)(2,1)} %collective-permute-done.5.f3, ...), custom_call_target="tpu_custom_call" | custom-call | flops 4294967296 | bytes 12582912 | tf_op jit(solution)/shard_map/pallas_call | solution.py:290
  248.7 11.5 %shard_map.181 = f32[32,8,128]{2,1,0:T(8,128)} custom-call(s32[4]{0:T(128)S(1)} %copy-done.8, bf16[512,2048]{1,0:T(8,128)(2,1)} %collective-permute-done.own, bf16[768,2048]{1,0:T(8,128)(2,1)} %collective-permute-done.6.first, bf16[768,2048]{1,0:T(8,128)(2,1)} %collective-permute-done.10.second, bf16[8,4,16,512]{3,2,1,0:T(8,128)(2,1)} %all-to-all-done.3.refs_0_, ...), custom_call_target="tpu_custom_call" | custom-call | flops 4294967296 | bytes 12582912 | tf_op jit(solution)/shard_map/pallas_call | solution.py:290
  260.2 9.4 %all-to-all-start.4 = ((f32[32,8,128]{2,1,0:T(8,128)}), f32[32,8,128]{2,1,0:T(8,128)S(1)}, u32[]{:S(2)}, u32[]{:S(2)}) async-start(f32[32,8,128]{2,1,0:T(8,128)} %shard_map.181), calls=%async_computation.4 | async-start | bytes 262144 | tf_op jit(solution)/shard_map/all_to_all | solution.py:438
  271.9 7.1 %all-to-all-done.4.got_ref = f32[32,8,128]{2,1,0:T(8,128)S(1)} async-done(((f32[32,8,128]{2,1,0:T(8,128)}), f32[32,8,128]{2,1,0:T(8,128)S(1)}, u32[]{:S(2)}, u32[]{:S(2)}) %all-to-all-start.4) | async-done | bytes 131104 | tf_op jit(solution)/shard_map/all_to_all | solution.py:438
  279.7 1.7 shard_map.182
  281.4 5.6 %all-to-all-start.5 = ((f32[8,8,128]{2,1,0:T(8,128)}), f32[8,8,128]{2,1,0:T(8,128)S(1)}, u32[]{:S(2)}, u32[]{:S(2)}) async-start(f32[8,8,128]{2,1,0:T(8,128)} %get-tuple-element.26), calls=%async_computation.5 | async-start | bytes 65536 | tf_op jit(solution)/shard_map/all_to_all | solution.py:443
  287.5 1.3 dynamic_slice.11
  288.7 3.0 %all-to-all-done.5.sums_ref = f32[8,8,128]{2,1,0:T(8,128)S(1)} async-done(((f32[8,8,128]{2,1,0:T(8,128)}), f32[8,8,128]{2,1,0:T(8,128)S(1)}, u32[]{:S(2)}, u32[]{:S(2)}) %all-to-all-start.5) | async-done | bytes 32800 | tf_op jit(solution)/shard_map/all_to_all | solution.py:443
  292.3 1.5 shard_map.183
  (90 shorter events, 21.0 us)
Async XLA Ops:
  0.6 60.8 %copy-start = (bf16[512,2048]{1,0:T(8,128)(2,1)S(1)}, bf16[512,2048]{1,0:T(8,128)(2,1)}, u32[]{:S(2)}) copy-start(bf16[512,2048]{1,0:T(8,128)(2,1)} %own.1) | copy-start | bytes 6291460
  2.6 24.7 %all-to-all-start = ((bf16[32,5,8,128]{3,2,1,0:T(8,128)(2,1)}), bf16[32,5,8,128]{3,2,1,0:T(8,128)(2,1)S(1)}, u32[]{:S(2)}, u32[]{:S(2)}) async-start(bf16[32,5,8,128]{3,2,1,0:T(8,128)(2,1)} %shard_map.175), calls=%async_computation | async-start | bytes 655360 | tf_op jit(solution)/shard_map/all_to_all | solution.py:360
  27.3 1.0 copy-start.14
  55.2 11.2 %collective-permute-start.1 = (bf16[4,32,16,128]{3,2,1,0:T(8,128)(2,1)}, bf16[4,32,16,128]{3,2,1,0:T(8,128)(2,1)}, u32[]{:S(2)}, u32[]{:S(2)}) collective-permute-start(bf16[4,32,16,128]{3,2,1,0:T(8,128)(2,1)} %bitcast.9.same), channel_id=1, source_target_pairs={{0,1},{1,0},{2,3},{3,2},{4,5},{5,4},{6,7},{7,6},{8,9},{9,8},{10,11... | collective-permute-start | bytes 1572872 | tf_op jit(solution)/shard_map/ppermute | solution.py:35
  62.5 26.1 %collective-permute-start.3 = (bf16[256,2048]{1,0:T(8,128)(2,1)}, bf16[256,2048]{1,0:T(8,128)(2,1)S(1)}, u32[]{:S(2)}, u32[]{:S(2)}) collective-permute-start(bf16[256,2048]{1,0:T(8,128)(2,1)} %slice.32), channel_id=1, source_target_pairs={{0,2},{2,4},{4,6},{6,0},{1,3},{3,5},{5,7},{7,1},{8,10},{10,12},{12... | collective-permute-start | bytes 3145736 | tf_op jit(solution)/shard_map/ppermute | solution.py:35
  62.8 48.4 %collective-permute-start.4 = (bf16[256,2048]{1,0:T(8,128)(2,1)}, bf16[256,2048]{1,0:T(8,128)(2,1)}, u32[]{:S(2)}, u32[]{:S(2)}) collective-permute-start(bf16[256,2048]{1,0:T(8,128)(2,1)} %slice.32), channel_id=1, source_target_pairs={{0,4},{2,6},{4,0},{6,2},{1,5},{3,7},{5,1},{7,3},{8,12},{10,14},{12... | collective-permute-start | bytes 3145736 | tf_op jit(solution)/shard_map/ppermute | solution.py:35
  65.2 46.3 %collective-permute-start.5 = (bf16[256,2048]{1,0:T(8,128)(2,1)}, bf16[256,2048]{1,0:T(8,128)(2,1)}, u32[]{:S(2)}, u32[]{:S(2)}) collective-permute-start(bf16[256,2048]{1,0:T(8,128)(2,1)} %slice.32), channel_id=1, source_target_pairs={{0,6},{2,0},{4,2},{6,4},{1,7},{3,1},{5,3},{7,5},{8,14},{10,8},{12,... | collective-permute-start | bytes 3145736 | tf_op jit(solution)/shard_map/ppermute | solution.py:35
  72.7 2.7 collective-permute-start.2
  111.6 25.5 %collective-permute-start.7 = (bf16[256,2048]{1,0:T(8,128)(2,1)S(1)}, bf16[256,2048]{1,0:T(8,128)(2,1)S(1)}, u32[]{:S(2)}, u32[]{:S(2)}) collective-permute-start(bf16[256,2048]{1,0:T(8,128)(2,1)S(1)} %slice.33), channel_id=1, source_target_pairs={{0,2},{2,4},{4,6},{6,0},{1,3},{3,5},{5,7},{7,1},{8,10},{10,12},{12... | collective-permute-start | bytes 3145736 | tf_op jit(solution)/shard_map/ppermute | solution.py:35
  112.9 48.2 %collective-permute-start.8 = (bf16[256,2048]{1,0:T(8,128)(2,1)S(1)}, bf16[256,2048]{1,0:T(8,128)(2,1)S(1)}, u32[]{:S(2)}, u32[]{:S(2)}) collective-permute-start(bf16[256,2048]{1,0:T(8,128)(2,1)S(1)} %slice.33), channel_id=1, source_target_pairs={{0,4},{2,6},{4,0},{6,2},{1,5},{3,7},{5,1},{7,3},{8,12},{10,14},{12... | collective-permute-start | bytes 3145736 | tf_op jit(solution)/shard_map/ppermute | solution.py:35
  115.9 45.2 %collective-permute-start.9 = (bf16[256,2048]{1,0:T(8,128)(2,1)S(1)}, bf16[256,2048]{1,0:T(8,128)(2,1)S(1)}, u32[]{:S(2)}, u32[]{:S(2)}) collective-permute-start(bf16[256,2048]{1,0:T(8,128)(2,1)S(1)} %slice.33), channel_id=1, source_target_pairs={{0,6},{2,0},{4,2},{6,4},{1,7},{3,1},{5,3},{7,5},{8,14},{10,8},{12,... | collective-permute-start | bytes 3145736 | tf_op jit(solution)/shard_map/ppermute | solution.py:35
  119.0 45.8 %copy-start.13 = (bf16[4,8,16,512]{3,2,1,0:T(8,128)(2,1)S(1)}, bf16[4,8,16,512]{3,2,1,0:T(8,128)(2,1)}, u32[]{:S(2)}) copy-start(bf16[4,8,16,512]{3,2,1,0:T(8,128)(2,1)} %shard_map.178) | copy-start | bytes 1572868
  119.0 129.7 %collective-permute-start.6 = (bf16[768,2048]{1,0:T(8,128)(2,1)}, bf16[768,2048]{1,0:T(8,128)(2,1)}, u32[]{:S(2)}, u32[]{:S(2)}) collective-permute-start(bf16[768,2048]{1,0:T(8,128)(2,1)} %pad_maximum_fusion), channel_id=1, source_target_pairs={{0,1},{1,0},{2,3},{3,2},{4,5},{5,4},{6,7},{7,6},{8,9},{9,8},{10,11... | collective-permute-start | bytes 9437192 | tf_op jit(solution)/shard_map/ppermute | solution.py:35
  137.1 25.9 %copy-start.1 = (bf16[256,2048]{1,0:T(8,128)(2,1)}, bf16[256,2048]{1,0:T(8,128)(2,1)S(1)}, u32[]{:S(2)}) copy-start(bf16[256,2048]{1,0:T(8,128)(2,1)S(1)} %collective-permute-done.7.g1) | copy-start | bytes 3145732
  161.1 2.0 copy-start.3
  161.1 2.3 copy-start.5
  163.4 69.9 %copy-start.8 = (s32[4]{0:T(128)S(1)}, s32[4]{0:T(128)}, u32[]{:S(2)}) copy-start(s32[4]{0:T(128)} %pad_add_fusion.at_ref) | copy-start | bytes 52
  163.4 85.2 %collective-permute-start.10 = (bf16[768,2048]{1,0:T(8,128)(2,1)}, bf16[768,2048]{1,0:T(8,128)(2,1)}, u32[]{:S(2)}, u32[]{:S(2)}) collective-permute-start(bf16[768,2048]{1,0:T(8,128)(2,1)} %pad_maximum_fusion.1), channel_id=1, source_target_pairs={{0,1},{1,0},{2,3},{3,2},{4,5},{5,4},{6,7},{7,6},{8,9},{9,8},{10,11... | collective-permute-start | bytes 9437192 | tf_op jit(solution)/shard_map/ppermute | solution.py:35
  164.8 55.5 %collective-permute-start = (bf16[512,2048]{1,0:T(8,128)(2,1)S(1)}, bf16[512,2048]{1,0:T(8,128)(2,1)}, u32[]{:S(2)}, u32[]{:S(2)}) collective-permute-start(bf16[512,2048]{1,0:T(8,128)(2,1)S(1)} %copy-done), channel_id=1, source_target_pairs={{0,1},{1,0},{2,3},{3,2},{4,5},{5,4},{6,7},{7,6},{8,9},{9,8},{10,11... | collective-permute-start | bytes 6291464 | tf_op jit(solution)/shard_map/ppermute | solution.py:35
  179.0 5.2 %collective-permute-start.14 = (bf16[4,16,512]{2,1,0:T(8,128)(2,1)}, bf16[4,16,512]{2,1,0:T(8,128)(2,1)S(1)}, u32[]{:S(2)}, u32[]{:S(2)}) collective-permute-start(bf16[4,16,512]{2,1,0:T(8,128)(2,1)} %get-tuple-element.24), channel_id=1, source_target_pairs={{0,8},{8,16},{16,24},{24,0},{1,9},{9,17},{17,25},{25,1},{2,10},{10... | collective-permute-start | bytes 196616 | tf_op jit(solution)/shard_map/ppermute | solution.py:35
  179.0 5.2 %collective-permute-start.15 = (bf16[4,16,512]{2,1,0:T(8,128)(2,1)}, bf16[4,16,512]{2,1,0:T(8,128)(2,1)S(1)}, u32[]{:S(2)}, u32[]{:S(2)}) collective-permute-start(bf16[4,16,512]{2,1,0:T(8,128)(2,1)} %get-tuple-element.24), channel_id=1, source_target_pairs={{0,16},{8,24},{16,0},{24,8},{1,17},{9,25},{17,1},{25,9},{2,18},{10... | collective-permute-start | bytes 196616 | tf_op jit(solution)/shard_map/ppermute | solution.py:35
  184.2 3.3 %collective-permute-start.16 = (bf16[4,16,512]{2,1,0:T(8,128)(2,1)}, bf16[4,16,512]{2,1,0:T(8,128)(2,1)S(1)}, u32[]{:S(2)}, u32[]{:S(2)}) collective-permute-start(bf16[4,16,512]{2,1,0:T(8,128)(2,1)} %get-tuple-element.24), channel_id=1, source_target_pairs={{0,24},{8,0},{16,8},{24,16},{1,25},{9,1},{17,9},{25,17},{2,26},{10... | collective-permute-start | bytes 196616 | tf_op jit(solution)/shard_map/ppermute | solution.py:35
  188.4 6.9 %collective-permute-start.17 = (bf16[4,4,16,512]{3,2,1,0:T(8,128)(2,1)S(1)}, bf16[4,4,16,512]{3,2,1,0:T(8,128)(2,1)}, u32[]{:S(2)}, u32[]{:S(2)}) collective-permute-start(bf16[4,4,16,512]{3,2,1,0:T(8,128)(2,1)S(1)} %pad_maximum_fusion.2.refs_0_), channel_id=1, source_target_pairs={{0,32},{32,64},{64,96},{96,128},{128,160},{160,192},{192,224},{224... | collective-permute-start | bytes 786440 | tf_op jit(solution)/shard_map/ppermute | solution.py:35
  188.5 31.8 %all-to-all-start.3 = ((bf16[8,4,16,512]{3,2,1,0:T(8,128)(2,1)}), bf16[8,4,16,512]{3,2,1,0:T(8,128)(2,1)}, u32[]{:S(2)}, u32[]{:S(2)}) async-start(bf16[8,4,16,512]{3,2,1,0:T(8,128)(2,1)} %get-tuple-element.23), calls=%async_computation.3 | async-start | bytes 1048576 | tf_op jit(solution)/shard_map/all_to_all | solution.py:403
  192.7 16.9 %collective-permute-start.21 = (bf16[4,4,16,512]{3,2,1,0:T(8,128)(2,1)S(1)}, bf16[4,4,16,512]{3,2,1,0:T(8,128)(2,1)S(1)}, u32[]{:S(2)}, u32[]{:S(2)}) collective-permute-start(bf16[4,4,16,512]{3,2,1,0:T(8,128)(2,1)S(1)} %pad_maximum_fusion.2.refs_0_), channel_id=1, source_target_pairs={{0,224},{32,0},{64,32},{96,64},{128,96},{160,128},{192,160},{224,1... | collective-permute-start | bytes 786440 | tf_op jit(solution)/shard_map/ppermute | solution.py:35
  195.4 18.2 %collective-permute-start.18 = (bf16[4,4,16,512]{3,2,1,0:T(8,128)(2,1)}, bf16[4,4,16,512]{3,2,1,0:T(8,128)(2,1)S(1)}, u32[]{:S(2)}, u32[]{:S(2)}) collective-permute-start(bf16[4,4,16,512]{3,2,1,0:T(8,128)(2,1)} %collective-permute-done.17.refs_1_), channel_id=1, source_target_pairs={{0,32},{32,64},{64,96},{96,128},{128,160},{160,192},{192,224},{224... | collective-permute-start | bytes 786440 | tf_op jit(solution)/shard_map/ppermute | solution.py:35
  209.6 5.6 %collective-permute-start.22 = (bf16[4,4,16,512]{3,2,1,0:T(8,128)(2,1)S(1)}, bf16[4,4,16,512]{3,2,1,0:T(8,128)(2,1)}, u32[]{:S(2)}, u32[]{:S(2)}) collective-permute-start(bf16[4,4,16,512]{3,2,1,0:T(8,128)(2,1)S(1)} %collective-permute-done.21.refs_7_), channel_id=1, source_target_pairs={{0,224},{32,0},{64,32},{96,64},{128,96},{160,128},{192,160},{224,1... | collective-permute-start | bytes 786440 | tf_op jit(solution)/shard_map/ppermute | solution.py:35
  210.7 0.7 copy-start.9
  213.6 6.5 %collective-permute-start.19 = (bf16[4,4,16,512]{3,2,1,0:T(8,128)(2,1)S(1)}, bf16[4,4,16,512]{3,2,1,0:T(8,128)(2,1)}, u32[]{:S(2)}, u32[]{:S(2)}) collective-permute-start(bf16[4,4,16,512]{3,2,1,0:T(8,128)(2,1)S(1)} %collective-permute-done.18.refs_2_), channel_id=1, source_target_pairs={{0,32},{32,64},{64,96},{96,128},{128,160},{160,192},{192,224},{224... | collective-permute-start | bytes 786440 | tf_op jit(solution)/shard_map/ppermute | solution.py:35
  213.6 0.7 copy-start.11
  215.2 7.1 %collective-permute-start.23 = (bf16[4,4,16,512]{3,2,1,0:T(8,128)(2,1)}, bf16[4,4,16,512]{3,2,1,0:T(8,128)(2,1)}, u32[]{:S(2)}, u32[]{:S(2)}) collective-permute-start(bf16[4,4,16,512]{3,2,1,0:T(8,128)(2,1)} %collective-permute-done.22.refs_6_), channel_id=1, source_target_pairs={{0,224},{32,0},{64,32},{96,64},{128,96},{160,128},{192,160},{224,1... | collective-permute-start | bytes 786440 | tf_op jit(solution)/shard_map/ppermute | solution.py:35
  220.1 6.7 %collective-permute-start.20 = (bf16[4,4,16,512]{3,2,1,0:T(8,128)(2,1)}, bf16[4,4,16,512]{3,2,1,0:T(8,128)(2,1)}, u32[]{:S(2)}, u32[]{:S(2)}) collective-permute-start(bf16[4,4,16,512]{3,2,1,0:T(8,128)(2,1)} %collective-permute-done.19.refs_3_), channel_id=1, source_target_pairs={{0,32},{32,64},{64,96},{96,128},{128,160},{160,192},{192,224},{224... | collective-permute-start | bytes 786440 | tf_op jit(solution)/shard_map/ppermute | solution.py:35
  220.3 28.3 %collective-permute-start.11 = (bf16[8,4,16,512]{3,2,1,0:T(8,128)(2,1)}, bf16[8,4,16,512]{3,2,1,0:T(8,128)(2,1)}, u32[]{:S(2)}, u32[]{:S(2)}) collective-permute-start(bf16[8,4,16,512]{3,2,1,0:T(8,128)(2,1)} %all-to-all-done.3.refs_0_), channel_id=1, source_target_pairs={{0,8},{8,16},{16,24},{24,0},{1,9},{9,17},{17,25},{25,1},{2,10},{10... | collective-permute-start | bytes 1572872 | tf_op jit(solution)/shard_map/ppermute | solution.py:35
  222.2 26.4 %collective-permute-start.12 = (bf16[8,4,16,512]{3,2,1,0:T(8,128)(2,1)}, bf16[8,4,16,512]{3,2,1,0:T(8,128)(2,1)}, u32[]{:S(2)}, u32[]{:S(2)}) collective-permute-start(bf16[8,4,16,512]{3,2,1,0:T(8,128)(2,1)} %all-to-all-done.3.refs_0_), channel_id=1, source_target_pairs={{0,16},{8,24},{16,0},{24,8},{1,17},{9,25},{17,1},{25,9},{2,18},{10... | collective-permute-start | bytes 1572872 | tf_op jit(solution)/shard_map/ppermute | solution.py:35
  226.9 21.8 %collective-permute-start.13 = (bf16[8,4,16,512]{3,2,1,0:T(8,128)(2,1)}, bf16[8,4,16,512]{3,2,1,0:T(8,128)(2,1)}, u32[]{:S(2)}, u32[]{:S(2)}) collective-permute-start(bf16[8,4,16,512]{3,2,1,0:T(8,128)(2,1)} %all-to-all-done.3.refs_0_), channel_id=1, source_target_pairs={{0,24},{8,0},{16,8},{24,16},{1,25},{9,1},{17,9},{25,17},{2,26},{10... | collective-permute-start | bytes 1572872 | tf_op jit(solution)/shard_map/ppermute | solution.py:35
  233.3 1.2 copy-start.2
  234.5 1.2 copy-start.4
  235.7 1.2 copy-start.6
  237.0 0.9 copy-start.10
  237.9 0.9 copy-start.12
  238.9 9.8 %copy-start.7 = (s32[512,1]{1,0:T(8,128)S(1)}, s32[512,1]{1,0:T(8,128)}, u32[]{:S(2)}) copy-start(s32[512,1]{1,0:T(8,128)} %sub.32.refs_5_) | copy-start | bytes 6148
  248.6 21.0 %copy-start.17 = (f32[22]{0:T(128)S(1)}, f32[22]{0:T(128)}, u32[]{:S(2)}) copy-start(f32[22]{0:T(128)} %param.29) | copy-start | bytes 268
  248.6 21.6 %copy-start.18 = (f32[22]{0:T(128)S(1)}, f32[22]{0:T(128)}, u32[]{:S(2)}) copy-start(f32[22]{0:T(128)} %param.28) | copy-start | bytes 268
  260.2 18.8 %all-to-all-start.4 = ((f32[32,8,128]{2,1,0:T(8,128)}), f32[32,8,128]{2,1,0:T(8,128)S(1)}, u32[]{:S(2)}, u32[]{:S(2)}) async-start(f32[32,8,128]{2,1,0:T(8,128)} %shard_map.181), calls=%async_computation.4 | async-start | bytes 262144 | tf_op jit(solution)/shard_map/all_to_all | solution.py:438
  279.0 0.6 copy-start.15
  281.4 10.3 %all-to-all-start.5 = ((f32[8,8,128]{2,1,0:T(8,128)}), f32[8,8,128]{2,1,0:T(8,128)S(1)}, u32[]{:S(2)}, u32[]{:S(2)}) async-start(f32[8,8,128]{2,1,0:T(8,128)} %get-tuple-element.26), calls=%async_computation.5 | async-start | bytes 65536 | tf_op jit(solution)/shard_map/all_to_all | solution.py:443
  291.7 0.6 copy-start.16
where the time goes:
time: 296 us; the launch traced here: 295 us
  waiting for transfers between devices  130 us (44%)
  starting transfers between devices  61 us (21%)
  Pallas kernels  38.6 us (13%)
  blocking collectives  37.3 us (13%)
  local copies, waits for them, and re-layouts  18 us (6%)
  other arithmetic  9.23 us (3%)
    ppermute x24, waiting for transfers between devices, shift(): return lax.ppermute(array, axis, [(i, (i + by) % n) for i in range(n)])  108 us
    ppermute x24, starting transfers between devices, shift(): return lax.ppermute(array, axis, [(i, (i + by) % n) for i in range(n)])  29.8 us
    pallas_call x2, Pallas kernels, logits_call(): pl.pallas_call(kernel, out_shape=out_shape, in_specs=[pl.BlockSpec(memory...  21.2 us
    pallas_call x7, Pallas kernels, call(): pl.pallas_call(kernel, out_shape=out_shape, in_specs=([pl.BlockSpec(memor...  17.4 us
    all_to_all x1, blocking collectives, program(): block = lax.all_to_all(picked.reshape(32, 16, 128), DP, 0, 0, tiled=True)  14.2 us
    all_to_all x1, blocking collectives, program(): sums = lax.all_to_all(pair, 'x', 0, 0, tiled=True)  12.1 us
    all_to_all x1, starting transfers between devices, program(): got = lax.all_to_all(packed, DP, 0, 0, tiled=True)  12 us
    all_to_all x1, waiting for transfers between devices, program(): got = lax.all_to_all(packed, DP, 0, 0, tiled=True)  11.8 us
  transfers between devices with their start and end apart: 28, of which 17 were waited for; matrix products, arithmetic and copies ran while one was open for 6% of the time, Pallas kernels for 7%

commit v1 on v0

--- a/solution.py
+++ b/solution.py
@@ -202,81 +202,70 @@
 WIDTH = 512
 
 
-def fetch(pieces, buffer, sems):
-    copies = [
-        [
-            pltpu.make_async_copy(
-                ref.at[pl.ds(lo, 256), pl.ds(j * WIDTH, WIDTH)],
-                buffer.at[j, pl.ds(p * 256, 256)],
-                sems.at[j, p],
+FIRST = 192
+
+
+def logits_kernel(at_ref, *refs):
+    own, f1, f2, f3, g1, g2, g3, w_other, first, second = refs[:10]
+    rows_a, rows_b = refs[10:18], refs[18:22]
+    goal_ref, out_ref, buffer, rows_ref, top_ref, sum_ref, pick_ref, sems = refs[22:]
+    late = 512 - FIRST
+    pieces = []
+    for f, g in ((own, own), (f1, g1), (f2, g2), (f3, g3)):
+        pieces += [(f, 0, FIRST), (g, FIRST if g is own else 0, late)]
+    pieces += [(w_other, 0, FIRST), (w_other, FIRST, late)]
+    for s in range(3):
+        pieces += [(first, s * FIRST, FIRST), (second, s * late, late)]
+
+    def copies(j):
+        found, at = [], 0
+        for p, (ref, lo, n) in enumerate(pieces):
+            found.append(
+                pltpu.make_async_copy(
+                    ref.at[pl.ds(lo, n), pl.ds(pl.multiple_of(j * WIDTH, WIDTH), WIDTH)],
+                    buffer.at[j, pl.ds(at, n)],
+                    sems.at[j, p],
+                )
             )
-            for p, (ref, lo) in enumerate(pieces)
-        ]
-        for j in range(BLOCKS)
-    ]
-    for block in copies:
-        for copy in block:
+            at += n
+        return found
+
+    @pl.loop(0, BLOCKS)
+    def _(j):
+        for copy in copies(j):
             copy.start()
-    return copies
-
-
-def lay_rows(rows_ref, parts):
-    for to, take in parts:
-        at = pl.ds(pl.multiple_of(to * 16, 16), 16)
-        for k in range(4):
-            rows_ref[at, k * 512 : k * 512 + 512] = take(k)
-
-
-def first_kernel(at_ref, own, f1, f2, f3, g1, g2, g3, *refs):
-    rows = refs[:8]
-    out_ref, buffer, rows_ref, sems = refs[8:]
-    pieces = [(own, 0), (own, 256), (f1, 0), (g1, 0), (f2, 0), (g2, 0), (f3, 0), (g3, 0)]
-    copies = fetch(pieces, buffer, sems)
+
     z, y = at_ref[2], at_ref[3]
-    parts = []
     for dz in range(8):
         for dy in range(4):
-            to = lax.rem(z + (8 - dz), 8) * 4 + lax.rem(y + (4 - dy), 4)
-            parts.append((to, functools.partial(lambda dz, dy, k: rows[dz][dy, k], dz, dy)))
-    lay_rows(rows_ref, parts)
-    for j in range(BLOCKS):
-        for copy in copies[j]:
+            in_y = lax.rem(y + (4 - dy), 4)
+            a_rows = pl.ds(pl.multiple_of((lax.rem(z + (8 - dz), 8) * 4 + in_y) * 16, 16), 16)
+            b_rows = pl.ds(pl.multiple_of((dz * 4 + in_y) * 16, 16), 16)
+            for k in range(4):
+                rows_ref[a_rows, k * 512 : k * 512 + 512] = rows_a[dz][dy, k]
+                rows_ref[b_rows, 2048 + k * 512 : 2048 + k * 512 + 512] = rows_b[dy][dz, k]
+    top_ref[...] = jnp.full((512, 1), -jnp.inf, f32)
+    sum_ref[...] = jnp.zeros((512, 1), f32)
+    pick_ref[...] = jnp.zeros((512, 1), f32)
+
+    @pl.loop(0, BLOCKS)
+    def _(j):
+        for copy in copies(j):
             copy.wait()
-        out_ref[j] = jnp.dot(rows_ref[...], buffer[j], preferred_element_type=f32)
-
-
-def second_kernel(at_ref, own, first, second, *refs):
-    rows = refs[:4]
-    part_ref, goal_ref, out_ref, buffer, rows_ref, sems = refs[4:]
-    pieces = [(own, 0), (own, 256)]
-    for s in range(3):
-        pieces += [(first, s * 256), (second, s * 256)]
-    copies = fetch(pieces, buffer, sems)
-    y = at_ref[3]
-    parts = []
-    for dz in range(8):
-        for dy in range(4):
-            to = dz * 4 + lax.rem(y + (4 - dy), 4)
-            parts.append((to, functools.partial(lambda dz, dy, k: rows[dy][dz, k], dz, dy)))
-    lay_rows(rows_ref, parts)
-    top = jnp.full((512, 1), -jnp.inf, f32)
-    total = jnp.zeros((512, 1), f32)
-    picked = jnp.zeros((512, 1), f32)
-    goal = goal_ref[...]
-    for j in range(BLOCKS):
-        for copy in copies[j]:
-            copy.wait()
-        logits = part_ref[j] + jnp.dot(rows_ref[...], buffer[j], preferred_element_type=f32)
-        column = lax.broadcasted_iota(i32, logits.shape, 1) + j * WIDTH
+        logits = jnp.dot(rows_ref[...], buffer[j], preferred_element_type=f32)
+        column = lax.broadcasted_iota(i32, logits.shape, 1)
+        top = top_ref[...]
         new = jnp.maximum(top, jnp.max(logits, axis=1, keepdims=True))
-        total = total * jnp.exp(top - new) + jnp.sum(
+        sum_ref[...] = sum_ref[...] * jnp.exp(top - new) + jnp.sum(
             jnp.exp(logits - new), axis=1, keepdims=True
         )
-        picked = picked + jnp.sum(jnp.where(column == goal, logits, 0.0), axis=1, keepdims=True)
-        top = new
+        hit = column == goal_ref[...] - j * WIDTH
+        pick_ref[...] += jnp.sum(jnp.where(hit, logits, 0.0), axis=1, keepdims=True)
+        top_ref[...] = new
+
     eye = lax.broadcasted_iota(i32, (128, 128), 0) == lax.broadcasted_iota(i32, (128, 128), 1)
     lines = []
-    for values in (top + jnp.log(total), picked):
+    for values in (top_ref[...] + jnp.log(sum_ref[...]), pick_ref[...]):
         for q in range(4):
             block = jnp.where(eye, values[q * 128 : q * 128 + 128], 0.0)
             lines.append(jnp.sum(block, axis=0, keepdims=True))
@@ -285,24 +274,28 @@
         out_ref[t] = lines
 
 
-def logits_call(kernel, at, weights, rest, out_shape):
+def logits_call(at, weights, rest):
     vmem = pl.BlockSpec(memory_space=pltpu.VMEM)
     return pl.pallas_call(
-        kernel,
-        out_shape=out_shape,
+        logits_kernel,
+        out_shape=sds((32, 8, 128), f32),
         in_specs=[pl.BlockSpec(memory_space=pltpu.SMEM)]
         + [pl.BlockSpec(memory_space=pltpu.HBM)] * len(weights)
         + [vmem] * len(rest),
         out_specs=vmem,
         scratch_shapes=[
-            pltpu.VMEM((BLOCKS, 2048, WIDTH), bf16),
-            pltpu.VMEM((512, 2048), bf16),
-            pltpu.SemaphoreType.DMA((BLOCKS, 8)),
+            pltpu.VMEM((BLOCKS, 4096, WIDTH), bf16),
+            pltpu.VMEM((512, 4096), bf16),
+            pltpu.VMEM((512, 1), f32),
+            pltpu.VMEM((512, 1), f32),
+            pltpu.VMEM((512, 1), f32),
+            pltpu.SemaphoreType.DMA((BLOCKS, 16)),
         ],
+        name="logits",
         cost_estimate=pl.CostEstimate(
-            flops=2 * 512 * 2048 * 2048, bytes_accessed=12 << 20, transcendentals=0
+            flops=2 * 512 * 4096 * 2048, bytes_accessed=20 << 20, transcendentals=0
         ),
-        compiler_params=pltpu.CompilerParams(vmem_limit_bytes=40 << 20),
+        compiler_params=pltpu.CompilerParams(vmem_limit_bytes=44 << 20),
     )(at, *weights, *rest)
 
 
@@ -336,8 +329,8 @@
     scaled = jnp.where(real, step_rate * new, -jnp.inf)
     e = jnp.exp(scaled - jnp.max(scaled, axis=1, keepdims=True))
     soft = e / jnp.sum(e, axis=1, keepdims=True)
-    new_ref[...] = new
-    probs_ref[...] = (1.0 - DOMAINS * explore_mass) * soft + explore_mass
+    new_ref[...] = new[:, :DOMAINS]
+    probs_ref[...] = ((1.0 - DOMAINS * explore_mass) * soft + explore_mass)[:, :DOMAINS]
 
 
 def program(
@@ -349,7 +342,7 @@
     at = jnp.stack([x, c, z, y]).astype(i32)
 
     w_other = shift(w_vocab, "c", 1)
-    rows = w_vocab[:256]
+    rows = w_vocab[:FIRST]
     w_first = [shift(rows, "x", s) for s in (1, 2, 3)]
 
     packed = call(
@@ -389,27 +382,9 @@
     sums = lax.all_to_all(pair, "x", 0, 0, tiled=True)
 
     (_, first_w, own_w) = lax.optimization_barrier((pair, tuple(w_first), w_vocab))
-    rows = own_w[256:]
+    rows = own_w[FIRST:]
     w_second = [shift(rows, "x", s) for s in (1, 2, 3)]
     w_first_other = shift(jnp.concatenate(first_w, axis=0), "c", 1)
-
-    fa, fb = call(
-        final_kernel, [sds((4, 16, 512), bf16), sds((8, 4, 16, 512), bf16)],
-        (resid, sums, gain_out.reshape(8, 1, 512)), at,
-        scratch=[pltpu.VMEM((8, 16, 512), f32)],
-    )
-
-    parts = [shift(fa, "y", s) for s in (1, 2, 3)]
-    column = lax.all_to_all(fb, "z", 0, 0, tiled=True)
-    group = jnp.stack([fa, *parts])
-    up, down = [group], [group]
-    for _ in range(3):
-        up.append(shift(up[-1], "z", 1))
-        down.append(shift(down[-1], "z", NZ - 1))
-    rows_b = [column] + [shift(column, "y", s) for s in (1, 2, 3)]
-    up.append(shift(up[-1], "z", 1))
-    rows_a = [*up, down[3], down[2], down[1]]
-    w_second_other = shift(jnp.concatenate(w_second, axis=0), "c", 1)
 
     seq_ids = jnp.dot(
         chosen.astype(bf16), meta[:, :4].reshape(128, 128), preferred_element_type=f32
@@ -426,14 +401,29 @@
     tally = SEQ_LEN * jnp.sum(
         (live[:, None] & (label_of[:, None] == domain[None, :])).astype(f32), axis=0
     )
-
-    partial = logits_call(
-        first_kernel, at, (w_vocab, *w_first, *w_second), rows_a,
-        sds((BLOCKS, 512, WIDTH), f32),
-    )
+    sums, goals = lax.optimization_barrier((sums, goals))
+
+    fa, fb = call(
+        final_kernel, [sds((4, 16, 512), bf16), sds((8, 4, 16, 512), bf16)],
+        (resid, sums, gain_out.reshape(8, 1, 512)), at,
+        scratch=[pltpu.VMEM((8, 16, 512), f32)],
+    )
+
+    parts = [shift(fa, "y", s) for s in (1, 2, 3)]
+    column = lax.all_to_all(fb, "z", 0, 0, tiled=True)
+    group = jnp.stack([fa, *parts])
+    up, down = [group], [group]
+    for _ in range(3):
+        up.append(shift(up[-1], "z", 1))
+        down.append(shift(down[-1], "z", NZ - 1))
+    rows_b = [column] + [shift(column, "y", s) for s in (1, 2, 3)]
+    up.append(shift(up[-1], "z", 1))
+    rows_a = [*up, down[3], down[2], down[1]]
+    w_second_other = shift(jnp.concatenate(w_second, axis=0), "c", 1)
+
     pieces = logits_call(
-        second_kernel, at, (w_other, w_first_other, w_second_other), (*rows_b, partial, goals),
-        sds((32, 8, 128), f32),
+        at, (w_vocab, *w_first, *w_second, w_other, w_first_other, w_second_other),
+        (*rows_a, *rows_b, goals),
     )
     merged = lax.all_to_all(pieces, DP, 0, 0, tiled=True)
     losses, sums_here = call(
@@ -443,10 +433,10 @@
     all_sums = lax.all_to_all(sums_here, MP, 0, 0, tiled=True)
     line = lambda v, fill: jnp.pad(v, (0, 128 - DOMAINS), constant_values=fill).reshape(1, 128)
     new_weights, probs = call(
-        output_kernel, [sds((1, 128), f32)] * 2,
+        output_kernel, [sds((1, DOMAINS), f32)] * 2,
         (all_sums, tally.reshape(1, 128), line(prev_probs, 1.0), line(log_weights, 0.0)),
     )
-    return own_loss, new_weights[0, :DOMAINS], probs[0, :DOMAINS]
+    return own_loss, new_weights.reshape(DOMAINS), probs.reshape(DOMAINS)
 
 
 def solution(mesh):

time: 296 us -> 314 us (1.061)
  waiting for transfers between devices: 130 us -> 153 us
  blocking collectives: 37.3 us -> 24.6 us
  starting transfers between devices: 61 us -> 68.4 us
    ppermute x24, waiting for transfers between devices: 108 us -> 125 us  [shift(): return lax.ppermute(array, axis, [(i, (i + by) % n) for i in range(n)])]
    all_to_all x1 -> x0, blocking collectives: 12.1 us -> none  [program(): sums = lax.all_to_all(pair, 'x', 0, 0, tiled=True)]
    all_to_all x0 -> x1, waiting for transfers between devices: none -> 6.47 us  [program(): sums = lax.all_to_all(pair, 'x', 0, 0, tiled=True)]
    all_to_all x1, starting transfers between devices: 9.42 us -> 13.7 us  [program(): merged = lax.all_to_all(pieces, DP, 0, 0, tiled=True)]
    all_to_all x0 -> x1, starting transfers between devices: none -> 4.16 us  [program(): sums = lax.all_to_all(pair, 'x', 0, 0, tiled=True)]
    pallas_call x2 -> x1, Pallas kernels: 21.2 us -> 18.6 us  [logits_call(): pl.pallas_call(logits_kernel, out_shape=sds((32, 8, 128), f32), in_specs=...]
    unnamed x38 -> x42, local copies, waits for them, and re-layouts: 8.67 us -> 10.8 us
  transfers between devices with their start and end apart: 28 -> 29, of which waited for: 17 -> 21; matrix products, arithmetic and copies ran while one was open for 6% -> 5% of each run, Pallas kernels for 7% -> 3%
where the time goes in v1:
time: 314 us; the launch traced here: 313 us
  waiting for transfers between devices  153 us (49%)
  starting transfers between devices  68.4 us (22%)
  Pallas kernels  35.8 us (11%)
  blocking collectives  24.6 us (8%)
  local copies, waits for them, and re-layouts  20.9 us (7%)
  other arithmetic  9.03 us (3%)
    ppermute x24, waiting for transfers between devices, shift(): return lax.ppermute(array, axis, [(i, (i + by) % n) for i in range(n)])  125 us
    ppermute x24, starting transfers between devices, shift(): return lax.ppermute(array, axis, [(i, (i + by) % n) for i in range(n)])  29 us
    pallas_call x1, Pallas kernels, logits_call(): pl.pallas_call(logits_kernel, out_shape=sds((32, 8, 128), f32), in_specs=...  18.6 us
    pallas_call x7, Pallas kernels, call(): pl.pallas_call(kernel, out_shape=out_shape, in_specs=([pl.BlockSpec(memor...  17.2 us
    all_to_all x1, blocking collectives, program(): block = lax.all_to_all(picked.reshape(32, 16, 128), DP, 0, 0, tiled=True)  14.2 us
    all_to_all x1, starting transfers between devices, program(): merged = lax.all_to_all(pieces, DP, 0, 0, tiled=True)  13.7 us
    all_to_all x1, starting transfers between devices, program(): got = lax.all_to_all(packed, DP, 0, 0, tiled=True)  12 us
    all_to_all x1, waiting for transfers between devices, program(): got = lax.all_to_all(packed, DP, 0, 0, tiled=True)  11.8 us
  transfers between devices with their start and end apart: 29, of which 21 were waited for; matrix products, arithmetic and copies ran while one was open for 5% of the time, Pallas kernels for 3%

profile of v1, /device:TPU:1, one launch (start us, length us, event | category | flops | bytes accessed | tf_op | source)
XLA Modules:
  0.0 313.2 jit_solution(7959226065617509049)
XLA Ops:
  0.6 1.8 shard_map.175
  2.4 12.0 %all-to-all-start = ((bf16[32,5,8,128]{3,2,1,0:T(8,128)(2,1)}), bf16[32,5,8,128]{3,2,1,0:T(8,128)(2,1)S(1)}, u32[]{:S(2)}, u32[]{:S(2)}) async-start(bf16[32,5,8,128]{3,2,1,0:T(8,128)(2,1)} %shard_map.175), calls=%async_computation | async-start | bytes 655360 | tf_op jit(solution)/shard_map/all_to_all | solution.py:353
  15.3 11.8 %all-to-all-done = bf16[32,5,8,128]{3,2,1,0:T(8,128)(2,1)S(1)} async-done(((bf16[32,5,8,128]{3,2,1,0:T(8,128)(2,1)}), bf16[32,5,8,128]{3,2,1,0:T(8,128)(2,1)S(1)}, u32[]{:S(2)}, u32[]{:S(2)}) %all-to-all-start) | async-done | bytes 327712 | tf_op jit(solution)/shard_map/all_to_all | solution.py:353
  28.1 1.7 shard_map.176
  29.8 14.2 %all_to_all.30 = bf16[32,16,128]{2,1,0:T(8,128)(2,1)S(1)} all-to-all(bf16[32,16,128]{2,1,0:T(8,128)(2,1)} %bitcast.31), channel_id=1, replica_groups=mesh['z'=8,'y'=4,'x'=4,'c'=2] {'z','y'}, dimensions={0} | all-to-all | bytes 262144 | tf_op jit(solution)/shard_map/all_to_all | solution.py:363
  44.0 10.4 %all-gather = bf16[128,16,128]{2,1,0:T(8,128)(2,1)S(1)} all-gather(bf16[32,16,128]{2,1,0:T(8,128)(2,1)S(1)} %all_to_all.30), channel_id=2, replica_groups=mesh['z'=8,'y'=4,'x'=4,'c'=2] {'x'}, dimensions={0}, use_global_device_ids=true | all-gather | bytes 655360 | tf_op jit(solution)/shard_map/all_gather | solution.py:365
  54.4 6.2 %collective-permute-start.3 = (bf16[4,32,16,128]{3,2,1,0:T(8,128)(2,1)S(1)}, bf16[4,32,16,128]{3,2,1,0:T(8,128)(2,1)S(1)}, u32[]{:S(2)}, u32[]{:S(2)}) collective-permute-start(bf16[4,32,16,128]{3,2,1,0:T(8,128)(2,1)S(1)} %bitcast.28), channel_id=1, source_target_pairs={{0,1},{1,0},{2,3},{3,2},{4,5},{5,4},{6,7},{7,6},{8,9},{9,8},{10,11... | collective-permute-start | bytes 1572872 | tf_op jit(solution)/shard_map/ppermute | solution.py:35
  60.6 2.1 slice.24
  63.0 2.4 collective-permute-start.1
  67.4 6.4 %shard_map.177 = (bf16[4,8,16,512]{3,2,1,0:T(8,128)(2,1)}, bf16[4,8,16,512]{3,2,1,0:T(8,128)(2,1)}, bf16[8,16,512]{2,1,0:T(8,128)(2,1)}) custom-call(s32[4]{0:T(128)} %pad_add_fusion.at_ref, bf16[4,32,16,128]{3,2,1,0:T(8,128)(2,1)} %bitcast.29, bf16[4,32,16,128]{3,2,1,0:T(8,128)(2,1)} %copy-done.15, f32[8,1,512]{2,1,0:T(1,128)} %bitcast.37, ...), custom_call_target="tpu_custom_call" | custom-call | flops 1073741824 | tf_op jit(solution)/shard_map/pallas_call | solution.py:42
  74.8 1.7 collective-permute-done.4.got_ref
  77.3 2.1 shard_map.178
  79.5 3.6 %collective-permute-done.refs_1_ = bf16[192,2048]{1,0:T(8,128)(2,1)S(1)} collective-permute-done((bf16[192,2048]{1,0:T(8,128)(2,1)}, bf16[192,2048]{1,0:T(8,128)(2,1)S(1)}, u32[]{:S(2)}, u32[]{:S(2)}) %collective-permute-start) | collective-permute-done | bytes 786464 | tf_op jit(solution)/shard_map/ppermute | solution.py:35
  83.1 16.8 %collective-permute-done.1.refs_2_ = bf16[192,2048]{1,0:T(8,128)(2,1)S(1)} collective-permute-done((bf16[192,2048]{1,0:T(8,128)(2,1)}, bf16[192,2048]{1,0:T(8,128)(2,1)S(1)}, u32[]{:S(2)}, u32[]{:S(2)}) %collective-permute-start.1) | collective-permute-done | bytes 786464 | tf_op jit(solution)/shard_map/ppermute | solution.py:35
  101.6 1.4 slice.27
  104.1 3.0 collective-permute-start.6
  107.1 26.6 %collective-permute-done.5.refs_4_ = bf16[320,2048]{1,0:T(8,128)(2,1)S(1)} collective-permute-done((bf16[320,2048]{1,0:T(8,128)(2,1)S(1)}, bf16[320,2048]{1,0:T(8,128)(2,1)S(1)}, u32[]{:S(2)}, u32[]{:S(2)}) %collective-permute-start.5) | collective-permute-done | bytes 1310752 | tf_op jit(solution)/shard_map/ppermute | solution.py:35
  133.7 29.9 %collective-permute-done.6.refs_5_ = bf16[320,2048]{1,0:T(8,128)(2,1)S(1)} collective-permute-done((bf16[320,2048]{1,0:T(8,128)(2,1)S(1)}, bf16[320,2048]{1,0:T(8,128)(2,1)S(1)}, u32[]{:S(2)}, u32[]{:S(2)}) %collective-permute-start.6) | collective-permute-done | bytes 1310752 | tf_op jit(solution)/shard_map/ppermute | solution.py:35
  163.5 2.3 pad_maximum_fusion
  165.9 1.3 collective-permute-start.10
  167.2 1.7 pad_maximum_fusion.1
  169.5 4.2 %all-to-all-start.2 = ((bf16[4,8,16,512]{3,2,1,0:T(8,128)(2,1)}), bf16[4,8,16,512]{3,2,1,0:T(8,128)(2,1)}, u32[]{:S(2)}, u32[]{:S(2)}) async-start(bf16[4,8,16,512]{3,2,1,0:T(8,128)(2,1)} %shard_map.178), calls=%async_computation.2 | async-start | bytes 1048576 | tf_op jit(solution)/shard_map/all_to_all | solution.py:382
  176.8 6.5 %all-to-all-done.2.sums = bf16[4,8,16,512]{3,2,1,0:T(8,128)(2,1)} async-done(((bf16[4,8,16,512]{3,2,1,0:T(8,128)(2,1)}), bf16[4,8,16,512]{3,2,1,0:T(8,128)(2,1)}, u32[]{:S(2)}, u32[]{:S(2)}) %all-to-all-start.2) | async-done | bytes 524320 | tf_op jit(solution)/shard_map/all_to_all | solution.py:382
  183.3 2.1 shard_map.179
  185.4 2.3 collective-permute-start.12
  187.7 3.3 %collective-permute-done.11 = bf16[4,16,512]{2,1,0:T(8,128)(2,1)S(1)} collective-permute-done((bf16[4,16,512]{2,1,0:T(8,128)(2,1)}, bf16[4,16,512]{2,1,0:T(8,128)(2,1)S(1)}, u32[]{:S(2)}, u32[]{:S(2)}) %collective-permute-start.11) | collective-permute-done | bytes 65568 | tf_op jit(solution)/shard_map/ppermute | solution.py:35
  191.0 3.3 %collective-permute-done.13 = bf16[4,16,512]{2,1,0:T(8,128)(2,1)S(1)} collective-permute-done((bf16[4,16,512]{2,1,0:T(8,128)(2,1)}, bf16[4,16,512]{2,1,0:T(8,128)(2,1)S(1)}, u32[]{:S(2)}, u32[]{:S(2)}) %collective-permute-start.13) | collective-permute-done | bytes 65568 | tf_op jit(solution)/shard_map/ppermute | solution.py:35
  194.3 1.6 pad_maximum_fusion.2.refs_10_
  195.9 4.1 %all-to-all-start.3 = ((bf16[8,4,16,512]{3,2,1,0:T(8,128)(2,1)}), bf16[8,4,16,512]{3,2,1,0:T(8,128)(2,1)}, u32[]{:S(2)}, u32[]{:S(2)}) async-start(bf16[8,4,16,512]{3,2,1,0:T(8,128)(2,1)} %get-tuple-element.27), calls=%async_computation.3 | async-start | bytes 1048576 | tf_op jit(solution)/shard_map/all_to_all | solution.py:413
  200.1 2.7 collective-permute-start.18
  202.8 14.2 %collective-permute-done.18.refs_17_ = bf16[4,4,16,512]{3,2,1,0:T(8,128)(2,1)S(1)} collective-permute-done((bf16[4,4,16,512]{3,2,1,0:T(8,128)(2,1)}, bf16[4,4,16,512]{3,2,1,0:T(8,128)(2,1)S(1)}, u32[]{:S(2)}, u32[]{:S(2)}) %collective-permute-start.18) | collective-permute-done | bytes 262176 | tf_op jit(solution)/shard_map/ppermute | solution.py:35
  216.9 1.4 collective-permute-start.19
  219.0 1.9 collective-permute-done.15.refs_12_
  222.5 2.4 collective-permute-start.20
  224.9 2.6 collective-permute-done.16.refs_13_
  229.0 1.7 collective-permute-start.22
  230.7 3.5 %collective-permute-done.17.refs_14_ = bf16[4,4,16,512]{3,2,1,0:T(8,128)(2,1)} collective-permute-done((bf16[4,4,16,512]{3,2,1,0:T(8,128)(2,1)}, bf16[4,4,16,512]{3,2,1,0:T(8,128)(2,1)}, u32[]{:S(2)}, u32[]{:S(2)}) %collective-permute-start.17) | collective-permute-done | bytes 262176 | tf_op jit(solution)/shard_map/ppermute | solution.py:35
  234.2 2.0 collective-permute-start.23
  237.1 1.9 collective-permute-done.21.refs_19_
  239.0 12.4 %collective-permute-done.22.refs_20_ = bf16[8,4,16,512]{3,2,1,0:T(8,128)(2,1)} collective-permute-done((bf16[8,4,16,512]{3,2,1,0:T(8,128)(2,1)}, bf16[8,4,16,512]{3,2,1,0:T(8,128)(2,1)}, u32[]{:S(2)}, u32[]{:S(2)}) %collective-permute-start.22) | collective-permute-done | bytes 524320 | tf_op jit(solution)/shard_map/ppermute | solution.py:35
  257.0 18.6 %logits.1 = f32[32,8,128]{2,1,0:T(8,128)} custom-call(s32[4]{0:T(128)S(1)} %copy-done.7, bf16[512,2048]{1,0:T(8,128)(2,1)} %refs_0_.1, bf16[192,2048]{1,0:T(8,128)(2,1)S(1)} %collective-permute-done.refs_1_, bf16[192,2048]{1,0:T(8,128)(2,1)S(1)} %copy-done.2, bf16[192,2048]{1,0:T(8,128)(2,1)S(1)} %copy-done.5, ...), custom_call_target="tpu_custom_call" | custom-call | flops 8589934592 | bytes 20971520 | tf_op jit(solution)/shard_map/logits/pallas_call | solution.py:279
  275.6 13.7 %all-to-all-start.4 = ((f32[32,8,128]{2,1,0:T(8,128)}), f32[32,8,128]{2,1,0:T(8,128)S(1)}, u32[]{:S(2)}, u32[]{:S(2)}) async-start(f32[32,8,128]{2,1,0:T(8,128)} %logits.1), calls=%async_computation.4 | async-start | bytes 262144 | tf_op jit(solution)/shard_map/all_to_all | solution.py:428
  291.2 7.5 %all-to-all-done.4.got_ref = f32[32,8,128]{2,1,0:T(8,128)S(1)} async-done(((f32[32,8,128]{2,1,0:T(8,128)}), f32[32,8,128]{2,1,0:T(8,128)S(1)}, u32[]{:S(2)}, u32[]{:S(2)}) %all-to-all-start.4) | async-done | bytes 131104 | tf_op jit(solution)/shard_map/all_to_all | solution.py:428
  299.4 1.7 shard_map.180
  301.1 5.3 %all-to-all-start.5 = ((f32[8,8,128]{2,1,0:T(8,128)}), f32[8,8,128]{2,1,0:T(8,128)S(1)}, u32[]{:S(2)}, u32[]{:S(2)}) async-start(f32[8,8,128]{2,1,0:T(8,128)} %get-tuple-element.30), calls=%async_computation.5 | async-start | bytes 65536 | tf_op jit(solution)/shard_map/all_to_all | solution.py:433
  306.9 1.3 dynamic_slice.11
  308.2 3.0 all-to-all-done.5.sums_ref
  311.7 1.5 shard_map.181
  (93 shorter events, 26.2 us)
Async XLA Ops:
  2.4 24.7 %all-to-all-start = ((bf16[32,5,8,128]{3,2,1,0:T(8,128)(2,1)}), bf16[32,5,8,128]{3,2,1,0:T(8,128)(2,1)S(1)}, u32[]{:S(2)}, u32[]{:S(2)}) async-start(bf16[32,5,8,128]{3,2,1,0:T(8,128)(2,1)} %shard_map.175), calls=%async_computation | async-start | bytes 655360 | tf_op jit(solution)/shard_map/all_to_all | solution.py:353
  27.2 1.0 copy-start.13
  54.4 12.2 %copy-start.12 = (bf16[128,16,128]{2,1,0:T(8,128)(2,1)}, bf16[128,16,128]{2,1,0:T(8,128)(2,1)S(1)}, u32[]{:S(2)}) copy-start(bf16[128,16,128]{2,1,0:T(8,128)(2,1)S(1)} %all-gather) | copy-start | bytes 1572868
  54.4 12.2 %collective-permute-start.3 = (bf16[4,32,16,128]{3,2,1,0:T(8,128)(2,1)S(1)}, bf16[4,32,16,128]{3,2,1,0:T(8,128)(2,1)S(1)}, u32[]{:S(2)}, u32[]{:S(2)}) collective-permute-start(bf16[4,32,16,128]{3,2,1,0:T(8,128)(2,1)S(1)} %bitcast.28), channel_id=1, source_target_pairs={{0,1},{1,0},{2,3},{3,2},{4,5},{5,4},{6,7},{7,6},{8,9},{9,8},{10,11... | collective-permute-start | bytes 1572872 | tf_op jit(solution)/shard_map/ppermute | solution.py:35
  62.7 20.4 %collective-permute-start = (bf16[192,2048]{1,0:T(8,128)(2,1)}, bf16[192,2048]{1,0:T(8,128)(2,1)S(1)}, u32[]{:S(2)}, u32[]{:S(2)}) collective-permute-start(bf16[192,2048]{1,0:T(8,128)(2,1)} %slice.24), channel_id=1, source_target_pairs={{0,2},{2,4},{4,6},{6,0},{1,3},{3,5},{5,7},{7,1},{8,10},{10,12},{12... | collective-permute-start | bytes 2359304 | tf_op jit(solution)/shard_map/ppermute | solution.py:35
  63.0 36.9 %collective-permute-start.1 = (bf16[192,2048]{1,0:T(8,128)(2,1)}, bf16[192,2048]{1,0:T(8,128)(2,1)S(1)}, u32[]{:S(2)}, u32[]{:S(2)}) collective-permute-start(bf16[192,2048]{1,0:T(8,128)(2,1)} %slice.24), channel_id=1, source_target_pairs={{0,4},{2,6},{4,0},{6,2},{1,5},{3,7},{5,1},{7,3},{8,12},{10,14},{12... | collective-permute-start | bytes 2359304 | tf_op jit(solution)/shard_map/ppermute | solution.py:35
  65.3 34.9 %collective-permute-start.2 = (bf16[192,2048]{1,0:T(8,128)(2,1)}, bf16[192,2048]{1,0:T(8,128)(2,1)S(1)}, u32[]{:S(2)}, u32[]{:S(2)}) collective-permute-start(bf16[192,2048]{1,0:T(8,128)(2,1)} %slice.24), channel_id=1, source_target_pairs={{0,6},{2,0},{4,2},{6,4},{1,7},{3,1},{5,3},{7,5},{8,14},{10,8},{12,... | collective-permute-start | bytes 2359304 | tf_op jit(solution)/shard_map/ppermute | solution.py:35
  66.6 0.8 copy-start.15
  73.7 2.8 collective-permute-start.4
  76.5 0.8 copy-start.16
  99.8 0.9 copy-start
  100.7 0.9 copy-start.3
  103.1 64.1 %copy-start.1 = (bf16[192,2048]{1,0:T(8,128)(2,1)S(1)}, bf16[192,2048]{1,0:T(8,128)(2,1)}, u32[]{:S(2)}) copy-start(bf16[192,2048]{1,0:T(8,128)(2,1)} %copy-done) | copy-start | bytes 2359300
  103.1 64.1 %copy-start.4 = (bf16[192,2048]{1,0:T(8,128)(2,1)S(1)}, bf16[192,2048]{1,0:T(8,128)(2,1)}, u32[]{:S(2)}) copy-start(bf16[192,2048]{1,0:T(8,128)(2,1)} %copy-done.3) | copy-start | bytes 2359300
  103.1 30.6 %collective-permute-start.5 = (bf16[320,2048]{1,0:T(8,128)(2,1)S(1)}, bf16[320,2048]{1,0:T(8,128)(2,1)S(1)}, u32[]{:S(2)}, u32[]{:S(2)}) collective-permute-start(bf16[320,2048]{1,0:T(8,128)(2,1)S(1)} %slice.27), channel_id=1, source_target_pairs={{0,2},{2,4},{4,6},{6,0},{1,3},{3,5},{5,7},{7,1},{8,10},{10,12},{12... | collective-permute-start | bytes 3932168 | tf_op jit(solution)/shard_map/ppermute | solution.py:35
  104.1 59.5 %collective-permute-start.6 = (bf16[320,2048]{1,0:T(8,128)(2,1)S(1)}, bf16[320,2048]{1,0:T(8,128)(2,1)S(1)}, u32[]{:S(2)}, u32[]{:S(2)}) collective-permute-start(bf16[320,2048]{1,0:T(8,128)(2,1)S(1)} %slice.27), channel_id=1, source_target_pairs={{0,4},{2,6},{4,0},{6,2},{1,5},{3,7},{5,1},{7,3},{8,12},{10,14},{12... | collective-permute-start | bytes 3932168 | tf_op jit(solution)/shard_map/ppermute | solution.py:35
  107.1 56.5 %collective-permute-start.7 = (bf16[320,2048]{1,0:T(8,128)(2,1)S(1)}, bf16[320,2048]{1,0:T(8,128)(2,1)S(1)}, u32[]{:S(2)}, u32[]{:S(2)}) collective-permute-start(bf16[320,2048]{1,0:T(8,128)(2,1)S(1)} %slice.27), channel_id=1, source_target_pairs={{0,6},{2,0},{4,2},{6,4},{1,7},{3,1},{5,3},{7,5},{8,14},{10,8},{12,... | collective-permute-start | bytes 3932168 | tf_op jit(solution)/shard_map/ppermute | solution.py:35
  163.5 2.3 copy-start.14
  165.9 86.0 %collective-permute-start.10 = (bf16[960,2048]{1,0:T(8,128)(2,1)}, bf16[960,2048]{1,0:T(8,128)(2,1)}, u32[]{:S(2)}, u32[]{:S(2)}) collective-permute-start(bf16[960,2048]{1,0:T(8,128)(2,1)} %pad_maximum_fusion), channel_id=1, source_target_pairs={{0,1},{1,0},{2,3},{3,2},{4,5},{5,4},{6,7},{7,6},{8,9},{9,8},{10,11... | collective-permute-start | bytes 11796488 | tf_op jit(solution)/shard_map/ppermute | solution.py:35
  167.2 60.3 %collective-permute-start.8 = (bf16[512,2048]{1,0:T(8,128)(2,1)}, bf16[512,2048]{1,0:T(8,128)(2,1)}, u32[]{:S(2)}, u32[]{:S(2)}) collective-permute-start(bf16[512,2048]{1,0:T(8,128)(2,1)} %refs_0_.1), channel_id=1, source_target_pairs={{0,1},{1,0},{2,3},{3,2},{4,5},{5,4},{6,7},{7,6},{8,9},{9,8},{10,11... | collective-permute-start | bytes 6291464 | tf_op jit(solution)/shard_map/ppermute | solution.py:35
  169.0 82.9 %copy-start.7 = (s32[4]{0:T(128)S(1)}, s32[4]{0:T(128)}, u32[]{:S(2)}) copy-start(s32[4]{0:T(128)} %pad_add_fusion.at_ref) | copy-start | bytes 52
  169.0 82.9 %collective-permute-start.9 = (bf16[576,2048]{1,0:T(8,128)(2,1)}, bf16[576,2048]{1,0:T(8,128)(2,1)}, u32[]{:S(2)}, u32[]{:S(2)}) collective-permute-start(bf16[576,2048]{1,0:T(8,128)(2,1)} %pad_maximum_fusion.1), channel_id=1, source_target_pairs={{0,1},{1,0},{2,3},{3,2},{4,5},{5,4},{6,7},{7,6},{8,9},{9,8},{10,11... | collective-permute-start | bytes 7077896 | tf_op jit(solution)/shard_map/ppermute | solution.py:35
  169.5 13.8 %all-to-all-start.2 = ((bf16[4,8,16,512]{3,2,1,0:T(8,128)(2,1)}), bf16[4,8,16,512]{3,2,1,0:T(8,128)(2,1)}, u32[]{:S(2)}, u32[]{:S(2)}) async-start(bf16[4,8,16,512]{3,2,1,0:T(8,128)(2,1)} %shard_map.178), calls=%async_computation.2 | async-start | bytes 1048576 | tf_op jit(solution)/shard_map/all_to_all | solution.py:382
  185.4 5.6 %collective-permute-start.11 = (bf16[4,16,512]{2,1,0:T(8,128)(2,1)}, bf16[4,16,512]{2,1,0:T(8,128)(2,1)S(1)}, u32[]{:S(2)}, u32[]{:S(2)}) collective-permute-start(bf16[4,16,512]{2,1,0:T(8,128)(2,1)} %get-tuple-element.26), channel_id=1, source_target_pairs={{0,8},{8,16},{16,24},{24,0},{1,9},{9,17},{17,25},{25,1},{2,10},{10... | collective-permute-start | bytes 196616 | tf_op jit(solution)/shard_map/ppermute | solution.py:35
  185.4 5.6 %collective-permute-start.12 = (bf16[4,16,512]{2,1,0:T(8,128)(2,1)}, bf16[4,16,512]{2,1,0:T(8,128)(2,1)S(1)}, u32[]{:S(2)}, u32[]{:S(2)}) collective-permute-start(bf16[4,16,512]{2,1,0:T(8,128)(2,1)} %get-tuple-element.26), channel_id=1, source_target_pairs={{0,16},{8,24},{16,0},{24,8},{1,17},{9,25},{17,1},{25,9},{2,18},{10... | collective-permute-start | bytes 196616 | tf_op jit(solution)/shard_map/ppermute | solution.py:35
  191.0 3.3 %collective-permute-start.13 = (bf16[4,16,512]{2,1,0:T(8,128)(2,1)}, bf16[4,16,512]{2,1,0:T(8,128)(2,1)S(1)}, u32[]{:S(2)}, u32[]{:S(2)}) collective-permute-start(bf16[4,16,512]{2,1,0:T(8,128)(2,1)} %get-tuple-element.26), channel_id=1, source_target_pairs={{0,24},{8,0},{16,8},{24,16},{1,25},{9,1},{17,9},{25,17},{2,26},{10... | collective-permute-start | bytes 196616 | tf_op jit(solution)/shard_map/ppermute | solution.py:35
  195.9 6.9 %collective-permute-start.14 = (bf16[4,4,16,512]{3,2,1,0:T(8,128)(2,1)}, bf16[4,4,16,512]{3,2,1,0:T(8,128)(2,1)}, u32[]{:S(2)}, u32[]{:S(2)}) collective-permute-start(bf16[4,4,16,512]{3,2,1,0:T(8,128)(2,1)} %pad_maximum_fusion.2.refs_10_), channel_id=1, source_target_pairs={{0,32},{32,64},{64,96},{96,128},{128,160},{160,192},{192,224},{224... | collective-permute-start | bytes 786440 | tf_op jit(solution)/shard_map/ppermute | solution.py:35
  195.9 31.6 %all-to-all-start.3 = ((bf16[8,4,16,512]{3,2,1,0:T(8,128)(2,1)}), bf16[8,4,16,512]{3,2,1,0:T(8,128)(2,1)}, u32[]{:S(2)}, u32[]{:S(2)}) async-start(bf16[8,4,16,512]{3,2,1,0:T(8,128)(2,1)} %get-tuple-element.27), calls=%async_computation.3 | async-start | bytes 1048576 | tf_op jit(solution)/shard_map/all_to_all | solution.py:413
  200.1 16.9 %collective-permute-start.18 = (bf16[4,4,16,512]{3,2,1,0:T(8,128)(2,1)}, bf16[4,4,16,512]{3,2,1,0:T(8,128)(2,1)S(1)}, u32[]{:S(2)}, u32[]{:S(2)}) collective-permute-start(bf16[4,4,16,512]{3,2,1,0:T(8,128)(2,1)} %pad_maximum_fusion.2.refs_10_), channel_id=1, source_target_pairs={{0,224},{32,0},{64,32},{96,64},{128,96},{160,128},{192,160},{224,1... | collective-permute-start | bytes 786440 | tf_op jit(solution)/shard_map/ppermute | solution.py:35
  202.8 18.2 %collective-permute-start.15 = (bf16[4,4,16,512]{3,2,1,0:T(8,128)(2,1)}, bf16[4,4,16,512]{3,2,1,0:T(8,128)(2,1)S(1)}, u32[]{:S(2)}, u32[]{:S(2)}) collective-permute-start(bf16[4,4,16,512]{3,2,1,0:T(8,128)(2,1)} %collective-permute-done.14.refs_11_), channel_id=1, source_target_pairs={{0,32},{32,64},{64,96},{96,128},{128,160},{160,192},{192,224},{224... | collective-permute-start | bytes 786440 | tf_op jit(solution)/shard_map/ppermute | solution.py:35
  216.9 5.6 %collective-permute-start.19 = (bf16[4,4,16,512]{3,2,1,0:T(8,128)(2,1)S(1)}, bf16[4,4,16,512]{3,2,1,0:T(8,128)(2,1)}, u32[]{:S(2)}, u32[]{:S(2)}) collective-permute-start(bf16[4,4,16,512]{3,2,1,0:T(8,128)(2,1)S(1)} %collective-permute-done.18.refs_17_), channel_id=1, source_target_pairs={{0,224},{32,0},{64,32},{96,64},{128,96},{160,128},{192,160},{224,1... | collective-permute-start | bytes 786440 | tf_op jit(solution)/shard_map/ppermute | solution.py:35
  218.4 0.7 copy-start.8
  221.0 6.5 %collective-permute-start.16 = (bf16[4,4,16,512]{3,2,1,0:T(8,128)(2,1)S(1)}, bf16[4,4,16,512]{3,2,1,0:T(8,128)(2,1)}, u32[]{:S(2)}, u32[]{:S(2)}) collective-permute-start(bf16[4,4,16,512]{3,2,1,0:T(8,128)(2,1)S(1)} %collective-permute-done.15.refs_12_), channel_id=1, source_target_pairs={{0,32},{32,64},{64,96},{96,128},{128,160},{160,192},{192,224},{224... | collective-permute-start | bytes 786440 | tf_op jit(solution)/shard_map/ppermute | solution.py:35
  221.0 0.7 copy-start.10
  222.5 6.5 %collective-permute-start.20 = (bf16[4,4,16,512]{3,2,1,0:T(8,128)(2,1)}, bf16[4,4,16,512]{3,2,1,0:T(8,128)(2,1)}, u32[]{:S(2)}, u32[]{:S(2)}) collective-permute-start(bf16[4,4,16,512]{3,2,1,0:T(8,128)(2,1)} %collective-permute-done.19.refs_16_), channel_id=1, source_target_pairs={{0,224},{32,0},{64,32},{96,64},{128,96},{160,128},{192,160},{224,1... | collective-permute-start | bytes 786440 | tf_op jit(solution)/shard_map/ppermute | solution.py:35
  227.5 6.7 %collective-permute-start.17 = (bf16[4,4,16,512]{3,2,1,0:T(8,128)(2,1)}, bf16[4,4,16,512]{3,2,1,0:T(8,128)(2,1)}, u32[]{:S(2)}, u32[]{:S(2)}) collective-permute-start(bf16[4,4,16,512]{3,2,1,0:T(8,128)(2,1)} %collective-permute-done.16.refs_13_), channel_id=1, source_target_pairs={{0,32},{32,64},{64,96},{96,128},{128,160},{160,192},{192,224},{224... | collective-permute-start | bytes 786440 | tf_op jit(solution)/shard_map/ppermute | solution.py:35
  227.5 11.5 %collective-permute-start.21 = (bf16[8,4,16,512]{3,2,1,0:T(8,128)(2,1)}, bf16[8,4,16,512]{3,2,1,0:T(8,128)(2,1)}, u32[]{:S(2)}, u32[]{:S(2)}) collective-permute-start(bf16[8,4,16,512]{3,2,1,0:T(8,128)(2,1)} %all-to-all-done.3.refs_18_), channel_id=1, source_target_pairs={{0,8},{8,16},{16,24},{24,0},{1,9},{9,17},{17,25},{25,1},{2,10},{10... | collective-permute-start | bytes 1572872 | tf_op jit(solution)/shard_map/ppermute | solution.py:35
  229.0 22.3 %collective-permute-start.22 = (bf16[8,4,16,512]{3,2,1,0:T(8,128)(2,1)}, bf16[8,4,16,512]{3,2,1,0:T(8,128)(2,1)}, u32[]{:S(2)}, u32[]{:S(2)}) collective-permute-start(bf16[8,4,16,512]{3,2,1,0:T(8,128)(2,1)} %all-to-all-done.3.refs_18_), channel_id=1, source_target_pairs={{0,16},{8,24},{16,0},{24,8},{1,17},{9,25},{17,1},{25,9},{2,18},{10... | collective-permute-start | bytes 1572872 | tf_op jit(solution)/shard_map/ppermute | solution.py:35
  234.2 17.6 %collective-permute-start.23 = (bf16[8,4,16,512]{3,2,1,0:T(8,128)(2,1)}, bf16[8,4,16,512]{3,2,1,0:T(8,128)(2,1)}, u32[]{:S(2)}, u32[]{:S(2)}) collective-permute-start(bf16[8,4,16,512]{3,2,1,0:T(8,128)(2,1)} %all-to-all-done.3.refs_18_), channel_id=1, source_target_pairs={{0,24},{8,0},{16,8},{24,16},{1,25},{9,1},{17,9},{25,17},{2,26},{10... | collective-permute-start | bytes 1572872 | tf_op jit(solution)/shard_map/ppermute | solution.py:35
  236.2 53.2 %copy-start.19 = (f32[22]{0:T(128)S(1)}, f32[22]{0:T(128)}, u32[]{:S(2)}) copy-start(f32[22]{0:T(128)} %param.29) | copy-start | bytes 268
  236.2 53.2 %copy-start.20 = (f32[22]{0:T(128)S(1)}, f32[22]{0:T(128)}, u32[]{:S(2)}) copy-start(f32[22]{0:T(128)} %param.28) | copy-start | bytes 268
  251.9 1.1 copy-start.2
  253.0 1.1 copy-start.5
  254.2 0.9 copy-start.6
  255.1 0.9 copy-start.9
  256.1 0.9 copy-start.11
  275.6 23.1 %all-to-all-start.4 = ((f32[32,8,128]{2,1,0:T(8,128)}), f32[32,8,128]{2,1,0:T(8,128)S(1)}, u32[]{:S(2)}, u32[]{:S(2)}) async-start(f32[32,8,128]{2,1,0:T(8,128)} %logits.1), calls=%async_computation.4 | async-start | bytes 262144 | tf_op jit(solution)/shard_map/all_to_all | solution.py:428
  301.1 10.1 %all-to-all-start.5 = ((f32[8,8,128]{2,1,0:T(8,128)}), f32[8,8,128]{2,1,0:T(8,128)S(1)}, u32[]{:S(2)}, u32[]{:S(2)}) async-start(f32[8,8,128]{2,1,0:T(8,128)} %get-tuple-element.30), calls=%async_computation.5 | async-start | bytes 65536 | tf_op jit(solution)/shard_map/all_to_all | solution.py:433
  (2 other events, 1.3 us)

commit v2 on v1

--- a/solution.py
+++ b/solution.py
@@ -202,39 +202,55 @@
 WIDTH = 512
 
 
-FIRST = 192
+FRONT = 256
 
 
 def logits_kernel(at_ref, *refs):
-    own, f1, f2, f3, g1, g2, g3, w_other, first, second = refs[:10]
-    rows_a, rows_b = refs[10:18], refs[18:22]
-    goal_ref, out_ref, buffer, rows_ref, top_ref, sum_ref, pick_ref, sems = refs[22:]
-    late = 512 - FIRST
-    pieces = []
-    for f, g in ((own, own), (f1, g1), (f2, g2), (f3, g3)):
-        pieces += [(f, 0, FIRST), (g, FIRST if g is own else 0, late)]
-    pieces += [(w_other, 0, FIRST), (w_other, FIRST, late)]
-    for s in range(3):
-        pieces += [(first, s * FIRST, FIRST), (second, s * late, late)]
+    pieces, rows, goal_ref = refs[:14], refs[14:26], refs[26]
+    (out_ref, buffer, stage_ref, rows_ref, logit_ref, top_ref, sum_ref, pick_ref, goals_ref,
+     sems, row_sems) = refs[27:]
+    whole, starts, at = (0, 7), [], 0
+    for p in range(14):
+        starts.append(at)
+        at += 512 if p in whole else 256
 
     def copies(j):
-        found, at = [], 0
-        for p, (ref, lo, n) in enumerate(pieces):
-            found.append(
-                pltpu.make_async_copy(
-                    ref.at[pl.ds(lo, n), pl.ds(pl.multiple_of(j * WIDTH, WIDTH), WIDTH)],
-                    buffer.at[j, pl.ds(at, n)],
-                    sems.at[j, p],
-                )
+        column = pl.ds(pl.multiple_of(j * WIDTH, WIDTH), WIDTH)
+        return [
+            pltpu.make_async_copy(
+                ref.at[:, column],
+                buffer.at[j, pl.ds(starts[p], 512 if p in whole else 256)],
+                sems.at[j, p],
             )
-            at += n
-        return found
+            for p, ref in enumerate(pieces)
+        ]
+
+    row_copies = [
+        pltpu.make_async_copy(ref, stage_ref.at[pl.ds(k * 256, 256)], row_sems.at[k])
+        for k, ref in enumerate(rows[:8])
+    ] + [
+        pltpu.make_async_copy(ref, stage_ref.at[pl.ds(2048 + k * 512, 512)], row_sems.at[8 + k])
+        for k, ref in enumerate(rows[8:])
+    ]
+    for copy in row_copies:
+        copy.start()
 
     @pl.loop(0, BLOCKS)
     def _(j):
         for copy in copies(j):
             copy.start()
 
+    eye = lax.broadcasted_iota(i32, (128, 128), 0) == lax.broadcasted_iota(i32, (128, 128), 1)
+    for q in range(4):
+        goals_ref[q * 128 : q * 128 + 128] = jnp.sum(
+            jnp.where(eye, goal_ref[q : q + 1], 0.0), axis=1, keepdims=True
+        )
+    top_ref[...] = jnp.full((512, 1), -jnp.inf, f32)
+    sum_ref[...] = jnp.zeros((512, 1), f32)
+    pick_ref[...] = jnp.zeros((512, 1), f32)
+
+    for copy in row_copies:
+        copy.wait()
     z, y = at_ref[2], at_ref[3]
     for dz in range(8):
         for dy in range(4):
@@ -242,28 +258,35 @@
             a_rows = pl.ds(pl.multiple_of((lax.rem(z + (8 - dz), 8) * 4 + in_y) * 16, 16), 16)
             b_rows = pl.ds(pl.multiple_of((dz * 4 + in_y) * 16, 16), 16)
             for k in range(4):
-                rows_ref[a_rows, k * 512 : k * 512 + 512] = rows_a[dz][dy, k]
-                rows_ref[b_rows, 2048 + k * 512 : 2048 + k * 512 + 512] = rows_b[dy][dz, k]
-    top_ref[...] = jnp.full((512, 1), -jnp.inf, f32)
-    sum_ref[...] = jnp.zeros((512, 1), f32)
-    pick_ref[...] = jnp.zeros((512, 1), f32)
-
-    @pl.loop(0, BLOCKS)
-    def _(j):
+                lo = dz * 256 + (dy * 4 + k) * 16
+                rows_ref[a_rows, k * 512 : k * 512 + 512] = stage_ref[lo : lo + 16]
+                lo = 2048 + dy * 512 + (dz * 4 + k) * 16
+                rows_ref[b_rows, 2048 + k * 512 : 2560 + k * 512] = stage_ref[lo : lo + 16]
+
+    def multiply(j):
         for copy in copies(j):
             copy.wait()
-        logits = jnp.dot(rows_ref[...], buffer[j], preferred_element_type=f32)
-        column = lax.broadcasted_iota(i32, logits.shape, 1)
+        return jnp.dot(rows_ref[...], buffer[j], preferred_element_type=f32)
+
+    def reduce(j, logits):
+        column = lax.broadcasted_iota(i32, logits.shape, 1).astype(f32)
         top = top_ref[...]
         new = jnp.maximum(top, jnp.max(logits, axis=1, keepdims=True))
         sum_ref[...] = sum_ref[...] * jnp.exp(top - new) + jnp.sum(
             jnp.exp(logits - new), axis=1, keepdims=True
         )
-        hit = column == goal_ref[...] - j * WIDTH
+        hit = column == goals_ref[...] - lax.convert_element_type(j * WIDTH, f32)
         pick_ref[...] += jnp.sum(jnp.where(hit, logits, 0.0), axis=1, keepdims=True)
         top_ref[...] = new
 
-    eye = lax.broadcasted_iota(i32, (128, 128), 0) == lax.broadcasted_iota(i32, (128, 128), 1)
+    logit_ref[0] = multiply(0)
+
+    @pl.loop(1, BLOCKS)
+    def _(j):
+        reduce(j - 1, logit_ref[lax.rem(j - 1, 2)])
+        logit_ref[lax.rem(j, 2)] = multiply(j)
+
+    reduce(jnp.int32(BLOCKS - 1), logit_ref[(BLOCKS - 1) % 2])
     lines = []
     for values in (top_ref[...] + jnp.log(sum_ref[...]), pick_ref[...]):
         for q in range(4):
@@ -274,29 +297,35 @@
         out_ref[t] = lines
 
 
-def logits_call(at, weights, rest):
+def logits_call(at, weights, rows, goals):
     vmem = pl.BlockSpec(memory_space=pltpu.VMEM)
+    hbm = pl.BlockSpec(memory_space=pltpu.HBM)
+    rows = [r.reshape(-1, 512) for r in rows]
     return pl.pallas_call(
         logits_kernel,
         out_shape=sds((32, 8, 128), f32),
         in_specs=[pl.BlockSpec(memory_space=pltpu.SMEM)]
-        + [pl.BlockSpec(memory_space=pltpu.HBM)] * len(weights)
-        + [vmem] * len(rest),
+        + [hbm] * (len(weights) + len(rows))
+        + [vmem],
         out_specs=vmem,
         scratch_shapes=[
             pltpu.VMEM((BLOCKS, 4096, WIDTH), bf16),
+            pltpu.VMEM((4096, 512), bf16),
             pltpu.VMEM((512, 4096), bf16),
+            pltpu.VMEM((2, 512, WIDTH), f32),
             pltpu.VMEM((512, 1), f32),
             pltpu.VMEM((512, 1), f32),
             pltpu.VMEM((512, 1), f32),
-            pltpu.SemaphoreType.DMA((BLOCKS, 16)),
+            pltpu.VMEM((512, 1), f32),
+            pltpu.SemaphoreType.DMA((BLOCKS, 14)),
+            pltpu.SemaphoreType.DMA((12,)),
         ],
         name="logits",
         cost_estimate=pl.CostEstimate(
             flops=2 * 512 * 4096 * 2048, bytes_accessed=20 << 20, transcendentals=0
         ),
-        compiler_params=pltpu.CompilerParams(vmem_limit_bytes=44 << 20),
-    )(at, *weights, *rest)
+        compiler_params=pltpu.CompilerParams(vmem_limit_bytes=36 << 20),
+    )(at, *weights, *rows, goals)
 
 
 def merge_kernel(got_ref, label_ref, loss_ref, sums_ref):
@@ -342,8 +371,8 @@
     at = jnp.stack([x, c, z, y]).astype(i32)
 
     w_other = shift(w_vocab, "c", 1)
-    rows = w_vocab[:FIRST]
-    w_first = [shift(rows, "x", s) for s in (1, 2, 3)]
+    rows = w_vocab[:FRONT]
+    front_1, front_3 = shift(rows, "x", 1), shift(rows, "x", 3)
 
     packed = call(
         pack_kernel, sds((32, 5, 8, 128), bf16),
@@ -381,10 +410,13 @@
     pair = call(pair_kernel, sds((4, 8, 16, 512), bf16), (keep, got_part))
     sums = lax.all_to_all(pair, "x", 0, 0, tiled=True)
 
-    (_, first_w, own_w) = lax.optimization_barrier((pair, tuple(w_first), w_vocab))
-    rows = own_w[FIRST:]
-    w_second = [shift(rows, "x", s) for s in (1, 2, 3)]
-    w_first_other = shift(jnp.concatenate(first_w, axis=0), "c", 1)
+    rows = w_vocab[FRONT:]
+    late_1, late_3 = shift(rows, "x", 1), shift(rows, "x", 3)
+    front_2 = shift(front_1, "x", 1)
+    late_2 = shift(late_3, "x", 3)
+    core_front_1, core_front_3 = shift(front_1, "c", 1), shift(front_3, "c", 1)
+    core_late_1, core_late_3 = shift(late_1, "c", 1), shift(late_3, "c", 1)
+    core_front_2, core_late_2 = shift(front_2, "c", 1), shift(late_2, "c", 1)
 
     seq_ids = jnp.dot(
         chosen.astype(bf16), meta[:, :4].reshape(128, 128), preferred_element_type=f32
@@ -396,7 +428,7 @@
     ).reshape(512)
     kinds = lax.dynamic_slice(seq_labels.reshape(32, 2), (0, m // 4), (32, 1))
     kinds = jnp.broadcast_to(kinds, (32, 16)).reshape(4, 128)
-    goals = (mine - d * 2048).reshape(512, 1)
+    goals = (mine - d * 2048).astype(f32).reshape(4, 128)
     domain = jnp.arange(128, dtype=i32)
     tally = SEQ_LEN * jnp.sum(
         (live[:, None] & (label_of[:, None] == domain[None, :])).astype(f32), axis=0
@@ -419,12 +451,11 @@
     rows_b = [column] + [shift(column, "y", s) for s in (1, 2, 3)]
     up.append(shift(up[-1], "z", 1))
     rows_a = [*up, down[3], down[2], down[1]]
-    w_second_other = shift(jnp.concatenate(w_second, axis=0), "c", 1)
-
-    pieces = logits_call(
-        at, (w_vocab, *w_first, *w_second, w_other, w_first_other, w_second_other),
-        (*rows_a, *rows_b, goals),
-    )
+    weights = (
+        w_vocab, front_1, late_1, front_2, late_2, front_3, late_3,
+        w_other, core_front_1, core_late_1, core_front_2, core_late_2, core_front_3, core_late_3,
+    )
+    pieces = logits_call(at, weights, (*rows_a, *rows_b), goals)
     merged = lax.all_to_all(pieces, DP, 0, 0, tiled=True)
     losses, sums_here = call(
         merge_kernel, [sds((4, 128), f32), sds((8, 8, 128), f32)], (merged, kinds)

time: 314 us -> 260 us (0.83)
  waiting for transfers between devices: 153 us -> 109 us
  local copies, waits for them, and re-layouts: 20.9 us -> 9.54 us
  starting transfers between devices: 68.4 us -> 74.8 us
  other arithmetic: 9.03 us -> 3.05 us
  blocking collectives: 24.6 us -> 27.8 us
    ppermute x24 -> x28, waiting for transfers between devices: 125 us -> 76.3 us  [shift(): return lax.ppermute(array, axis, [(i, (i + by) % n) for i in range(n)])]
    all_gather x1, blocking collectives: 10.4 us -> 27.8 us  [program(): same = lax.all_gather(block, 'x', axis=0, tiled=False)]
    all_to_all x1 -> x0, blocking collectives: 14.2 us -> none  [program(): block = lax.all_to_all(picked.reshape(32, 16, 128), DP, 0, 0, tiled=True)]
    unnamed x42 -> x24, local copies, waits for them, and re-layouts: 10.8 us -> 2.86 us
    all_to_all x0 -> x1, waiting for transfers between devices: none -> 6.79 us  [program(): block = lax.all_to_all(picked.reshape(32, 16, 128), DP, 0, 0, tiled=True)]
    all_to_all x1, starting transfers between devices: 13.7 us -> 8.54 us  [program(): merged = lax.all_to_all(pieces, DP, 0, 0, tiled=True)]
    ppermute x24 -> x28, starting transfers between devices: 29 us -> 34.1 us  [shift(): return lax.ppermute(array, axis, [(i, (i + by) % n) for i in range(n)])]
    all_to_all x1, waiting for transfers between devices: 11.8 us -> 6.85 us  [program(): got = lax.all_to_all(packed, DP, 0, 0, tiled=True)]
  transfers between devices with their start and end apart: 29 -> 34, of which waited for: 21 -> 16; matrix products, arithmetic and copies ran while one was open for 5% -> 4% of each run, Pallas kernels for 3% -> 5%
where the time goes in v2:
time: 260 us; the launch traced here: 259 us
  waiting for transfers between devices  109 us (42%)
  starting transfers between devices  74.8 us (29%)
  Pallas kernels  33.5 us (13%)
  blocking collectives  27.8 us (11%)
  local copies, waits for them, and re-layouts  9.54 us (4%)
  other arithmetic  3.05 us (1%)
    ppermute x28, waiting for transfers between devices, shift(): return lax.ppermute(array, axis, [(i, (i + by) % n) for i in range(n)])  76.3 us
    ppermute x28, starting transfers between devices, shift(): return lax.ppermute(array, axis, [(i, (i + by) % n) for i in range(n)])  34.1 us
    all_gather x1, blocking collectives, program(): same = lax.all_gather(block, 'x', axis=0, tiled=False)  27.8 us
    pallas_call x7, Pallas kernels, call(): pl.pallas_call(kernel, out_shape=out_shape, in_specs=([pl.BlockSpec(memor...  17.2 us
    pallas_call x1, Pallas kernels, logits_call(): pl.pallas_call(logits_kernel, out_shape=sds((32, 8, 128), f32), in_specs=...  16.3 us
    all_to_all x1, starting transfers between devices, program(): got = lax.all_to_all(packed, DP, 0, 0, tiled=True)  12 us
    all_to_all x1, waiting for transfers between devices, program(): sums = lax.all_to_all(pair, 'x', 0, 0, tiled=True)  8.95 us
    all_to_all x1, starting transfers between devices, program(): merged = lax.all_to_all(pieces, DP, 0, 0, tiled=True)  8.54 us
  transfers between devices with their start and end apart: 34, of which 16 were waited for; matrix products, arithmetic and copies ran while one was open for 4% of the time, Pallas kernels for 5%

profile of v2, /device:TPU:1, one launch (start us, length us, event | category | flops | bytes accessed | tf_op | source)
XLA Modules:
  0.0 259.1 jit_solution(1229285150516644475)
XLA Ops:
  0.6 1.8 shard_map.175
  2.4 12.0 %all-to-all-start = ((bf16[32,5,8,128]{3,2,1,0:T(8,128)(2,1)}), bf16[32,5,8,128]{3,2,1,0:T(8,128)(2,1)S(1)}, u32[]{:S(2)}, u32[]{:S(2)}) async-start(bf16[32,5,8,128]{3,2,1,0:T(8,128)(2,1)} %shard_map.175), calls=%async_computation | async-start | bytes 655360 | tf_op jit(solution)/shard_map/all_to_all | solution.py:382
  14.5 3.1 %fusion.10 = (bf16[256,2048]{1,0:T(8,128)(2,1)}, bf16[256,2048]{1,0:T(8,128)(2,1)}) fusion(bf16[512,2048]{1,0:T(8,128)(2,1)} %refs_0_.1), kind=kLoop, calls=%fused_computation.32 | loop fusion | bytes 4194304 | tf_op jit(solution)/shard_map/slice | solution.py:413
  17.6 2.5 collective-permute-start.3
  20.3 6.9 %all-to-all-done = bf16[32,5,8,128]{3,2,1,0:T(8,128)(2,1)S(1)} async-done(((bf16[32,5,8,128]{3,2,1,0:T(8,128)(2,1)}), bf16[32,5,8,128]{3,2,1,0:T(8,128)(2,1)S(1)}, u32[]{:S(2)}, u32[]{:S(2)}) %all-to-all-start) | async-done | bytes 327712 | tf_op jit(solution)/shard_map/all_to_all | solution.py:382
  28.2 1.7 shard_map.176
  29.8 4.8 %all-to-all-start.1 = ((bf16[32,16,128]{2,1,0:T(8,128)(2,1)}), bf16[32,16,128]{2,1,0:T(8,128)(2,1)S(1)}, u32[]{:S(2)}, u32[]{:S(2)}) async-start(bf16[32,16,128]{2,1,0:T(8,128)(2,1)} %bitcast.52), calls=%async_computation.1 | async-start | bytes 262144 | tf_op jit(solution)/shard_map/all_to_all | solution.py:392
  34.7 2.6 collective-permute-start.5
  37.2 6.8 %all-to-all-done.1 = bf16[32,16,128]{2,1,0:T(8,128)(2,1)S(1)} async-done(((bf16[32,16,128]{2,1,0:T(8,128)(2,1)}), bf16[32,16,128]{2,1,0:T(8,128)(2,1)S(1)}, u32[]{:S(2)}, u32[]{:S(2)}) %all-to-all-start.1) | async-done | bytes 131104 | tf_op jit(solution)/shard_map/all_to_all | solution.py:392
  44.0 27.8 %all-gather = bf16[128,16,128]{2,1,0:T(8,128)(2,1)S(1)} all-gather(bf16[32,16,128]{2,1,0:T(8,128)(2,1)S(1)} %all-to-all-done.1), channel_id=2, replica_groups=mesh['z'=8,'y'=4,'x'=4,'c'=2] {'x'}, dimensions={0}, use_global_device_ids=true | all-gather | bytes 655360 | tf_op jit(solution)/shard_map/all_gather | solution.py:394
  71.8 3.3 %collective-permute-start.13 = (bf16[4,32,16,128]{3,2,1,0:T(8,128)(2,1)S(1)}, bf16[4,32,16,128]{3,2,1,0:T(8,128)(2,1)S(1)}, u32[]{:S(2)}, u32[]{:S(2)}) collective-permute-start(bf16[4,32,16,128]{3,2,1,0:T(8,128)(2,1)S(1)} %bitcast.49), channel_id=1, source_target_pairs={{0,1},{1,0},{2,3},{3,2},{4,5},{5,4},{6,7},{7,6},{8,9},{9,8},{10,11... | collective-permute-start | bytes 1572872 | tf_op jit(solution)/shard_map/ppermute | solution.py:35
  75.1 2.0 collective-permute-start.1
  77.7 1.2 collective-permute-start.4
  80.0 6.3 %shard_map.177 = (bf16[4,8,16,512]{3,2,1,0:T(8,128)(2,1)}, bf16[4,8,16,512]{3,2,1,0:T(8,128)(2,1)}, bf16[8,16,512]{2,1,0:T(8,128)(2,1)}) custom-call(s32[4]{0:T(128)} %pad_add_fusion.at_ref, bf16[4,32,16,128]{3,2,1,0:T(8,128)(2,1)} %bitcast.50, bf16[4,32,16,128]{3,2,1,0:T(8,128)(2,1)} %copy-done.5, f32[8,1,512]{2,1,0:T(1,128)} %bitcast.58, ...), custom_call_target="tpu_custom_call" | custom-call | flops 1073741824 | tf_op jit(solution)/shard_map/pallas_call | solution.py:42
  86.4 0.8 collective-permute-start.14
  87.3 14.9 %collective-permute-done.1.refs_2_ = bf16[256,2048]{1,0:T(8,128)(2,1)} collective-permute-done((bf16[256,2048]{1,0:T(8,128)(2,1)}, bf16[256,2048]{1,0:T(8,128)(2,1)}, u32[]{:S(2)}, u32[]{:S(2)}) %collective-permute-start.1) | collective-permute-done | bytes 1048608 | tf_op jit(solution)/shard_map/ppermute | solution.py:35
  103.5 21.2 %collective-permute-done.2.refs_3_ = bf16[256,2048]{1,0:T(8,128)(2,1)} collective-permute-done((bf16[256,2048]{1,0:T(8,128)(2,1)S(1)}, bf16[256,2048]{1,0:T(8,128)(2,1)}, u32[]{:S(2)}, u32[]{:S(2)}) %collective-permute-start.2) | collective-permute-done | bytes 1048608 | tf_op jit(solution)/shard_map/ppermute | solution.py:35
  125.2 2.1 shard_map.178
  127.4 3.6 %all-to-all-start.2 = ((bf16[4,8,16,512]{3,2,1,0:T(8,128)(2,1)}), bf16[4,8,16,512]{3,2,1,0:T(8,128)(2,1)S(1)}, u32[]{:S(2)}, u32[]{:S(2)}) async-start(bf16[4,8,16,512]{3,2,1,0:T(8,128)(2,1)} %shard_map.178), calls=%async_computation.2 | async-start | bytes 1048576 | tf_op jit(solution)/shard_map/all_to_all | solution.py:411
  131.6 9.0 %all-to-all-done.2.sums = bf16[4,8,16,512]{3,2,1,0:T(8,128)(2,1)S(1)} async-done(((bf16[4,8,16,512]{3,2,1,0:T(8,128)(2,1)}), bf16[4,8,16,512]{3,2,1,0:T(8,128)(2,1)S(1)}, u32[]{:S(2)}, u32[]{:S(2)}) %all-to-all-start.2) | async-done | bytes 524320 | tf_op jit(solution)/shard_map/all_to_all | solution.py:411
  141.3 2.1 shard_map.179
  143.4 1.2 collective-permute-start.15
  144.7 3.3 %collective-permute-done.15 = bf16[4,16,512]{2,1,0:T(8,128)(2,1)S(1)} collective-permute-done((bf16[4,16,512]{2,1,0:T(8,128)(2,1)}, bf16[4,16,512]{2,1,0:T(8,128)(2,1)S(1)}, u32[]{:S(2)}, u32[]{:S(2)}) %collective-permute-start.15) | collective-permute-done | bytes 65568 | tf_op jit(solution)/shard_map/ppermute | solution.py:35
  148.0 1.5 collective-permute-start.16
  149.5 6.4 %all-to-all-start.3 = ((bf16[8,4,16,512]{3,2,1,0:T(8,128)(2,1)}), bf16[8,4,16,512]{3,2,1,0:T(8,128)(2,1)S(1)}, u32[]{:S(2)}, u32[]{:S(2)}) async-start(bf16[8,4,16,512]{3,2,1,0:T(8,128)(2,1)} %get-tuple-element.19), calls=%async_computation.3 | async-start | bytes 1048576 | tf_op jit(solution)/shard_map/all_to_all | solution.py:445
  155.9 1.0 collective-permute-start.17
  156.8 2.4 collective-permute-done.17
  159.3 3.7 %collective-permute-start.9 = (bf16[256,2048]{1,0:T(8,128)(2,1)}, bf16[256,2048]{1,0:T(8,128)(2,1)}, u32[]{:S(2)}, u32[]{:S(2)}) collective-permute-start(bf16[256,2048]{1,0:T(8,128)(2,1)} %collective-permute-done.2.refs_3_), channel_id=1, source_target_pairs={{0,1},{1,0},{2,3},{3,2},{4,5},{5,4},{6,7},{7,6},{8,9},{9,8},{10,11... | collective-permute-start | bytes 3145736 | tf_op jit(solution)/shard_map/ppermute | solution.py:35
  163.0 0.9 pad_maximum_fusion
  163.9 1.7 collective-permute-start.18
  165.6 1.3 collective-permute-start.22
  166.9 9.3 %collective-permute-done.18 = bf16[4,4,16,512]{3,2,1,0:T(8,128)(2,1)S(1)} collective-permute-done((bf16[4,4,16,512]{3,2,1,0:T(8,128)(2,1)S(1)}, bf16[4,4,16,512]{3,2,1,0:T(8,128)(2,1)S(1)}, u32[]{:S(2)}, u32[]{:S(2)}) %collective-permute-start.18) | collective-permute-done | bytes 262176 | tf_op jit(solution)/shard_map/ppermute | solution.py:35
  176.2 2.7 %collective-permute-start.23 = (bf16[4,4,16,512]{3,2,1,0:T(8,128)(2,1)S(1)}, bf16[4,4,16,512]{3,2,1,0:T(8,128)(2,1)}, u32[]{:S(2)}, u32[]{:S(2)}) collective-permute-start(bf16[4,4,16,512]{3,2,1,0:T(8,128)(2,1)S(1)} %collective-permute-done.22), channel_id=1, source_target_pairs={{0,224},{32,0},{64,32},{96,64},{128,96},{160,128},{192,160},{224,1... | collective-permute-start | bytes 786440 | tf_op jit(solution)/shard_map/ppermute | solution.py:35
  178.9 5.5 %collective-permute-done.19 = bf16[4,4,16,512]{3,2,1,0:T(8,128)(2,1)} collective-permute-done((bf16[4,4,16,512]{3,2,1,0:T(8,128)(2,1)S(1)}, bf16[4,4,16,512]{3,2,1,0:T(8,128)(2,1)}, u32[]{:S(2)}, u32[]{:S(2)}) %collective-permute-start.19) | collective-permute-done | bytes 262176 | tf_op jit(solution)/shard_map/ppermute | solution.py:35
  184.8 2.9 %collective-permute-start.26 = (bf16[8,4,16,512]{3,2,1,0:T(8,128)(2,1)S(1)}, bf16[8,4,16,512]{3,2,1,0:T(8,128)(2,1)S(1)}, u32[]{:S(2)}, u32[]{:S(2)}) collective-permute-start(bf16[8,4,16,512]{3,2,1,0:T(8,128)(2,1)S(1)} %all-to-all-done.3), channel_id=1, source_target_pairs={{0,16},{8,24},{16,0},{24,8},{1,17},{9,25},{17,1},{25,9},{2,18},{10... | collective-permute-start | bytes 1572872 | tf_op jit(solution)/shard_map/ppermute | solution.py:35
  188.1 2.6 %collective-permute-start.24 = (bf16[4,4,16,512]{3,2,1,0:T(8,128)(2,1)}, bf16[4,4,16,512]{3,2,1,0:T(8,128)(2,1)S(1)}, u32[]{:S(2)}, u32[]{:S(2)}) collective-permute-start(bf16[4,4,16,512]{3,2,1,0:T(8,128)(2,1)} %collective-permute-done.23), channel_id=1, source_target_pairs={{0,224},{32,0},{64,32},{96,64},{128,96},{160,128},{192,160},{224,1... | collective-permute-start | bytes 786440 | tf_op jit(solution)/shard_map/ppermute | solution.py:35
  190.7 1.3 collective-permute-done.20
  192.0 2.4 collective-permute-done.24
  194.3 4.6 %collective-permute-done.21 = bf16[4,4,16,512]{3,2,1,0:T(8,128)(2,1)S(1)} collective-permute-done((bf16[4,4,16,512]{3,2,1,0:T(8,128)(2,1)}, bf16[4,4,16,512]{3,2,1,0:T(8,128)(2,1)S(1)}, u32[]{:S(2)}, u32[]{:S(2)}) %collective-permute-start.21) | collective-permute-done | bytes 262176 | tf_op jit(solution)/shard_map/ppermute | solution.py:35
  198.9 10.7 %collective-permute-done.26 = bf16[8,4,16,512]{3,2,1,0:T(8,128)(2,1)S(1)} collective-permute-done((bf16[8,4,16,512]{3,2,1,0:T(8,128)(2,1)S(1)}, bf16[8,4,16,512]{3,2,1,0:T(8,128)(2,1)S(1)}, u32[]{:S(2)}, u32[]{:S(2)}) %collective-permute-start.26) | collective-permute-done | bytes 524320 | tf_op jit(solution)/shard_map/ppermute | solution.py:35
  210.4 16.3 %logits.1 = f32[32,8,128]{2,1,0:T(8,128)} custom-call(s32[4]{0:T(128)S(1)} %copy-done, bf16[512,2048]{1,0:T(8,128)(2,1)} %refs_0_.1, bf16[256,2048]{1,0:T(8,128)(2,1)S(1)} %collective-permute-done.refs_1_, bf16[256,2048]{1,0:T(8,128)(2,1)} %collective-permute-done.1.refs_2_, bf16[256,2048]{1,0:T(8,128)(2,1)} %collective-permute-done.2.refs_3_, ...), custom_call_target="tpu_custom_call" | custom-call | flops 8589934592 | bytes 20971520 | tf_op jit(solution)/shard_map/logits/pallas_call | solution.py:304
  226.7 8.5 %all-to-all-start.4 = ((f32[32,8,128]{2,1,0:T(8,128)}), f32[32,8,128]{2,1,0:T(8,128)S(1)}, u32[]{:S(2)}, u32[]{:S(2)}) async-start(f32[32,8,128]{2,1,0:T(8,128)} %logits.1), calls=%async_computation.4 | async-start | bytes 262144 | tf_op jit(solution)/shard_map/all_to_all | solution.py:459
  237.1 7.5 %all-to-all-done.4.got_ref = f32[32,8,128]{2,1,0:T(8,128)S(1)} async-done(((f32[32,8,128]{2,1,0:T(8,128)}), f32[32,8,128]{2,1,0:T(8,128)S(1)}, u32[]{:S(2)}, u32[]{:S(2)}) %all-to-all-start.4) | async-done | bytes 131104 | tf_op jit(solution)/shard_map/all_to_all | solution.py:459
  245.2 1.7 shard_map.180
  246.9 5.3 %all-to-all-start.5 = ((f32[8,8,128]{2,1,0:T(8,128)}), f32[8,8,128]{2,1,0:T(8,128)S(1)}, u32[]{:S(2)}, u32[]{:S(2)}) async-start(f32[8,8,128]{2,1,0:T(8,128)} %get-tuple-element.22), calls=%async_computation.5 | async-start | bytes 65536 | tf_op jit(solution)/shard_map/all_to_all | solution.py:464
  252.8 1.3 dynamic_slice.11
  254.0 3.0 %all-to-all-done.5.sums_ref = f32[8,8,128]{2,1,0:T(8,128)S(1)} async-done(((f32[8,8,128]{2,1,0:T(8,128)}), f32[8,8,128]{2,1,0:T(8,128)S(1)}, u32[]{:S(2)}, u32[]{:S(2)}) %all-to-all-start.5) | async-done | bytes 32800 | tf_op jit(solution)/shard_map/all_to_all | solution.py:464
  257.6 1.5 shard_map.181
  (81 shorter events, 11.3 us)
Async XLA Ops:
  2.4 24.7 %all-to-all-start = ((bf16[32,5,8,128]{3,2,1,0:T(8,128)(2,1)}), bf16[32,5,8,128]{3,2,1,0:T(8,128)(2,1)S(1)}, u32[]{:S(2)}, u32[]{:S(2)}) async-start(bf16[32,5,8,128]{3,2,1,0:T(8,128)(2,1)} %shard_map.175), calls=%async_computation | async-start | bytes 655360 | tf_op jit(solution)/shard_map/all_to_all | solution.py:382
  14.5 5.6 %copy-start.9 = (s32[32]{0:T(128)S(1)}, s32[32]{0:T(128)}, u32[]{:S(2)}) copy-start(s32[32]{0:T(128)} %param.19) | copy-start | bytes 388
  17.6 60.1 %collective-permute-start.3 = (bf16[256,2048]{1,0:T(8,128)(2,1)}, bf16[256,2048]{1,0:T(8,128)(2,1)S(1)}, u32[]{:S(2)}, u32[]{:S(2)}) collective-permute-start(bf16[256,2048]{1,0:T(8,128)(2,1)} %get-tuple-element.29), channel_id=1, source_target_pairs={{0,6},{2,0},{4,2},{6,4},{1,7},{3,1},{5,3},{7,5},{8,14},{10,8},{12,... | collective-permute-start | bytes 3145736 | tf_op jit(solution)/shard_map/ppermute | solution.py:35
  20.1 58.9 %collective-permute-start = (bf16[256,2048]{1,0:T(8,128)(2,1)}, bf16[256,2048]{1,0:T(8,128)(2,1)S(1)}, u32[]{:S(2)}, u32[]{:S(2)}) collective-permute-start(bf16[256,2048]{1,0:T(8,128)(2,1)} %get-tuple-element.30), channel_id=1, source_target_pairs={{0,2},{2,4},{4,6},{6,0},{1,3},{3,5},{5,7},{7,1},{8,10},{10,12},{12... | collective-permute-start | bytes 3145736 | tf_op jit(solution)/shard_map/ppermute | solution.py:35
  27.2 1.0 copy-start.3
  27.2 98.1 %copy-start.7 = (bf16[32,8,128]{2,1,0:T(8,128)(2,1)}, bf16[32,8,128]{2,1,0:T(8,128)(2,1)S(1)}, u32[]{:S(2)}) copy-start(bf16[32,8,128]{2,1,0:T(8,128)(2,1)S(1)} %slice_bitcast_fusion) | copy-start | bytes 196612
  29.8 14.2 %all-to-all-start.1 = ((bf16[32,16,128]{2,1,0:T(8,128)(2,1)}), bf16[32,16,128]{2,1,0:T(8,128)(2,1)S(1)}, u32[]{:S(2)}, u32[]{:S(2)}) async-start(bf16[32,16,128]{2,1,0:T(8,128)(2,1)} %bitcast.52), calls=%async_computation.1 | async-start | bytes 262144 | tf_op jit(solution)/shard_map/all_to_all | solution.py:392
  34.7 52.5 %collective-permute-start.5 = (bf16[256,2048]{1,0:T(8,128)(2,1)}, bf16[256,2048]{1,0:T(8,128)(2,1)}, u32[]{:S(2)}, u32[]{:S(2)}) collective-permute-start(bf16[256,2048]{1,0:T(8,128)(2,1)} %get-tuple-element.30), channel_id=1, source_target_pairs={{0,6},{2,0},{4,2},{6,4},{1,7},{3,1},{5,3},{7,5},{8,14},{10,8},{12,... | collective-permute-start | bytes 3145736 | tf_op jit(solution)/shard_map/ppermute | solution.py:35
  71.8 7.4 %copy-start.1 = (bf16[128,16,128]{2,1,0:T(8,128)(2,1)}, bf16[128,16,128]{2,1,0:T(8,128)(2,1)S(1)}, u32[]{:S(2)}) copy-start(bf16[128,16,128]{2,1,0:T(8,128)(2,1)S(1)} %all-gather) | copy-start | bytes 1572868
  71.8 7.4 %collective-permute-start.13 = (bf16[4,32,16,128]{3,2,1,0:T(8,128)(2,1)S(1)}, bf16[4,32,16,128]{3,2,1,0:T(8,128)(2,1)S(1)}, u32[]{:S(2)}, u32[]{:S(2)}) collective-permute-start(bf16[4,32,16,128]{3,2,1,0:T(8,128)(2,1)S(1)} %bitcast.49), channel_id=1, source_target_pairs={{0,1},{1,0},{2,3},{3,2},{4,5},{5,4},{6,7},{7,6},{8,9},{9,8},{10,11... | collective-permute-start | bytes 1572872 | tf_op jit(solution)/shard_map/ppermute | solution.py:35
  75.1 27.1 %collective-permute-start.1 = (bf16[256,2048]{1,0:T(8,128)(2,1)}, bf16[256,2048]{1,0:T(8,128)(2,1)}, u32[]{:S(2)}, u32[]{:S(2)}) collective-permute-start(bf16[256,2048]{1,0:T(8,128)(2,1)} %get-tuple-element.29), channel_id=1, source_target_pairs={{0,2},{2,4},{4,6},{6,0},{1,3},{3,5},{5,7},{7,1},{8,10},{10,12},{12... | collective-permute-start | bytes 3145736 | tf_op jit(solution)/shard_map/ppermute | solution.py:35
  77.7 25.3 %collective-permute-start.4 = (bf16[256,2048]{1,0:T(8,128)(2,1)S(1)}, bf16[256,2048]{1,0:T(8,128)(2,1)}, u32[]{:S(2)}, u32[]{:S(2)}) collective-permute-start(bf16[256,2048]{1,0:T(8,128)(2,1)S(1)} %collective-permute-done.3.refs_6_), channel_id=1, source_target_pairs={{0,6},{2,0},{4,2},{6,4},{1,7},{3,1},{5,3},{7,5},{8,14},{10,8},{12,... | collective-permute-start | bytes 3145736 | tf_op jit(solution)/shard_map/ppermute | solution.py:35
  79.0 45.7 %collective-permute-start.2 = (bf16[256,2048]{1,0:T(8,128)(2,1)S(1)}, bf16[256,2048]{1,0:T(8,128)(2,1)}, u32[]{:S(2)}, u32[]{:S(2)}) collective-permute-start(bf16[256,2048]{1,0:T(8,128)(2,1)S(1)} %collective-permute-done.refs_1_), channel_id=1, source_target_pairs={{0,2},{2,4},{4,6},{6,0},{1,3},{3,5},{5,7},{7,1},{8,10},{10,12},{12... | collective-permute-start | bytes 3145736 | tf_op jit(solution)/shard_map/ppermute | solution.py:35
  79.2 0.8 copy-start.5
  86.4 16.6 %collective-permute-start.14 = (bf16[4,8,16,512]{3,2,1,0:T(8,128)(2,1)}, bf16[4,8,16,512]{3,2,1,0:T(8,128)(2,1)S(1)}, u32[]{:S(2)}, u32[]{:S(2)}) collective-permute-start(bf16[4,8,16,512]{3,2,1,0:T(8,128)(2,1)} %get-tuple-element.16), channel_id=1, source_target_pairs={{0,1},{1,0},{2,3},{3,2},{4,5},{5,4},{6,7},{7,6},{8,9},{9,8},{10,11... | collective-permute-start | bytes 1572872 | tf_op jit(solution)/shard_map/ppermute | solution.py:35
  87.2 43.9 %collective-permute-start.12 = (bf16[256,2048]{1,0:T(8,128)(2,1)S(1)}, bf16[256,2048]{1,0:T(8,128)(2,1)}, u32[]{:S(2)}, u32[]{:S(2)}) collective-permute-start(bf16[256,2048]{1,0:T(8,128)(2,1)S(1)} %collective-permute-done.3.refs_6_), channel_id=1, source_target_pairs={{0,1},{1,0},{2,3},{3,2},{4,5},{5,4},{6,7},{7,6},{8,9},{9,8},{10,11... | collective-permute-start | bytes 3145736 | tf_op jit(solution)/shard_map/ppermute | solution.py:35
  102.2 82.2 %collective-permute-start.6 = (bf16[512,2048]{1,0:T(8,128)(2,1)}, bf16[512,2048]{1,0:T(8,128)(2,1)}, u32[]{:S(2)}, u32[]{:S(2)}) collective-permute-start(bf16[512,2048]{1,0:T(8,128)(2,1)} %refs_0_.1), channel_id=1, source_target_pairs={{0,1},{1,0},{2,3},{3,2},{4,5},{5,4},{6,7},{7,6},{8,9},{9,8},{10,11... | collective-permute-start | bytes 6291464 | tf_op jit(solution)/shard_map/ppermute | solution.py:35
  102.9 22.3 %copy-start.4 = (bf16[4,8,16,512]{3,2,1,0:T(8,128)(2,1)}, bf16[4,8,16,512]{3,2,1,0:T(8,128)(2,1)S(1)}, u32[]{:S(2)}) copy-start(bf16[4,8,16,512]{3,2,1,0:T(8,128)(2,1)S(1)} %collective-permute-done.14.got_ref) | copy-start | bytes 1572868
  102.9 40.5 %collective-permute-start.7 = (bf16[256,2048]{1,0:T(8,128)(2,1)S(1)}, bf16[256,2048]{1,0:T(8,128)(2,1)}, u32[]{:S(2)}, u32[]{:S(2)}) collective-permute-start(bf16[256,2048]{1,0:T(8,128)(2,1)S(1)} %collective-permute-done.refs_1_), channel_id=1, source_target_pairs={{0,1},{1,0},{2,3},{3,2},{4,5},{5,4},{6,7},{7,6},{8,9},{9,8},{10,11... | collective-permute-start | bytes 3145736 | tf_op jit(solution)/shard_map/ppermute | solution.py:35
  103.0 60.8 %collective-permute-start.11 = (bf16[256,2048]{1,0:T(8,128)(2,1)}, bf16[256,2048]{1,0:T(8,128)(2,1)}, u32[]{:S(2)}, u32[]{:S(2)}) collective-permute-start(bf16[256,2048]{1,0:T(8,128)(2,1)} %collective-permute-done.5.refs_5_), channel_id=1, source_target_pairs={{0,1},{1,0},{2,3},{3,2},{4,5},{5,4},{6,7},{7,6},{8,9},{9,8},{10,11... | collective-permute-start | bytes 3145736 | tf_op jit(solution)/shard_map/ppermute | solution.py:35
  124.7 41.0 %collective-permute-start.8 = (bf16[256,2048]{1,0:T(8,128)(2,1)}, bf16[256,2048]{1,0:T(8,128)(2,1)}, u32[]{:S(2)}, u32[]{:S(2)}) collective-permute-start(bf16[256,2048]{1,0:T(8,128)(2,1)} %collective-permute-done.1.refs_2_), channel_id=1, source_target_pairs={{0,1},{1,0},{2,3},{3,2},{4,5},{5,4},{6,7},{7,6},{8,9},{9,8},{10,11... | collective-permute-start | bytes 3145736 | tf_op jit(solution)/shard_map/ppermute | solution.py:35
  125.2 5.7 %slice-start = ((bf16[32,8,128]{2,1,0:T(8,128)(2,1)}), bf16[32,4,128]{2,1,0:T(4,128)(2,1)S(1)}, s32[]{:S(2)}) async-start(bf16[32,8,128]{2,1,0:T(8,128)(2,1)} %copy-done.7), calls=%async_computation.6 | async-start | bytes 65536 | tf_op jit(solution)/shard_map/slice | solution.py:422
  127.4 83.0 %copy-start = (s32[4]{0:T(128)S(1)}, s32[4]{0:T(128)}, u32[]{:S(2)}) copy-start(s32[4]{0:T(128)} %pad_add_fusion.at_ref) | copy-start | bytes 52
  127.4 13.1 %all-to-all-start.2 = ((bf16[4,8,16,512]{3,2,1,0:T(8,128)(2,1)}), bf16[4,8,16,512]{3,2,1,0:T(8,128)(2,1)S(1)}, u32[]{:S(2)}, u32[]{:S(2)}) async-start(bf16[4,8,16,512]{3,2,1,0:T(8,128)(2,1)} %shard_map.178), calls=%async_computation.2 | async-start | bytes 1048576 | tf_op jit(solution)/shard_map/all_to_all | solution.py:411
  131.1 56.6 %collective-permute-start.10 = (bf16[256,2048]{1,0:T(8,128)(2,1)}, bf16[256,2048]{1,0:T(8,128)(2,1)}, u32[]{:S(2)}, u32[]{:S(2)}) collective-permute-start(bf16[256,2048]{1,0:T(8,128)(2,1)} %collective-permute-done.4.refs_4_), channel_id=1, source_target_pairs={{0,1},{1,0},{2,3},{3,2},{4,5},{5,4},{6,7},{7,6},{8,9},{9,8},{10,11... | collective-permute-start | bytes 3145736 | tf_op jit(solution)/shard_map/ppermute | solution.py:35
  140.5 0.8 copy-start.2
  143.4 4.5 %collective-permute-start.15 = (bf16[4,16,512]{2,1,0:T(8,128)(2,1)}, bf16[4,16,512]{2,1,0:T(8,128)(2,1)S(1)}, u32[]{:S(2)}, u32[]{:S(2)}) collective-permute-start(bf16[4,16,512]{2,1,0:T(8,128)(2,1)} %get-tuple-element.18), channel_id=1, source_target_pairs={{0,8},{8,16},{16,24},{24,0},{1,9},{9,17},{17,25},{25,1},{2,10},{10... | collective-permute-start | bytes 196616 | tf_op jit(solution)/shard_map/ppermute | solution.py:35
  148.0 7.9 %collective-permute-start.16 = (bf16[4,16,512]{2,1,0:T(8,128)(2,1)}, bf16[4,16,512]{2,1,0:T(8,128)(2,1)S(1)}, u32[]{:S(2)}, u32[]{:S(2)}) collective-permute-start(bf16[4,16,512]{2,1,0:T(8,128)(2,1)} %get-tuple-element.18), channel_id=1, source_target_pairs={{0,16},{8,24},{16,0},{24,8},{1,17},{9,25},{17,1},{25,9},{2,18},{10... | collective-permute-start | bytes 196616 | tf_op jit(solution)/shard_map/ppermute | solution.py:35
  149.5 34.9 %all-to-all-start.3 = ((bf16[8,4,16,512]{3,2,1,0:T(8,128)(2,1)}), bf16[8,4,16,512]{3,2,1,0:T(8,128)(2,1)S(1)}, u32[]{:S(2)}, u32[]{:S(2)}) async-start(bf16[8,4,16,512]{3,2,1,0:T(8,128)(2,1)} %get-tuple-element.19), calls=%async_computation.3 | async-start | bytes 1048576 | tf_op jit(solution)/shard_map/all_to_all | solution.py:445
  155.9 3.4 %collective-permute-start.17 = (bf16[4,16,512]{2,1,0:T(8,128)(2,1)}, bf16[4,16,512]{2,1,0:T(8,128)(2,1)S(1)}, u32[]{:S(2)}, u32[]{:S(2)}) collective-permute-start(bf16[4,16,512]{2,1,0:T(8,128)(2,1)} %get-tuple-element.18), channel_id=1, source_target_pairs={{0,24},{8,0},{16,8},{24,16},{1,25},{9,1},{17,9},{25,17},{2,26},{10... | collective-permute-start | bytes 196616 | tf_op jit(solution)/shard_map/ppermute | solution.py:35
  159.3 28.8 %collective-permute-start.9 = (bf16[256,2048]{1,0:T(8,128)(2,1)}, bf16[256,2048]{1,0:T(8,128)(2,1)}, u32[]{:S(2)}, u32[]{:S(2)}) collective-permute-start(bf16[256,2048]{1,0:T(8,128)(2,1)} %collective-permute-done.2.refs_3_), channel_id=1, source_target_pairs={{0,1},{1,0},{2,3},{3,2},{4,5},{5,4},{6,7},{7,6},{8,9},{9,8},{10,11... | collective-permute-start | bytes 3145736 | tf_op jit(solution)/shard_map/ppermute | solution.py:35
  163.9 12.4 %collective-permute-start.18 = (bf16[4,4,16,512]{3,2,1,0:T(8,128)(2,1)S(1)}, bf16[4,4,16,512]{3,2,1,0:T(8,128)(2,1)S(1)}, u32[]{:S(2)}, u32[]{:S(2)}) collective-permute-start(bf16[4,4,16,512]{3,2,1,0:T(8,128)(2,1)S(1)} %pad_maximum_fusion), channel_id=1, source_target_pairs={{0,32},{32,64},{64,96},{96,128},{128,160},{160,192},{192,224},{224... | collective-permute-start | bytes 786440 | tf_op jit(solution)/shard_map/ppermute | solution.py:35
  165.6 10.6 %collective-permute-start.22 = (bf16[4,4,16,512]{3,2,1,0:T(8,128)(2,1)S(1)}, bf16[4,4,16,512]{3,2,1,0:T(8,128)(2,1)S(1)}, u32[]{:S(2)}, u32[]{:S(2)}) collective-permute-start(bf16[4,4,16,512]{3,2,1,0:T(8,128)(2,1)S(1)} %pad_maximum_fusion), channel_id=1, source_target_pairs={{0,224},{32,0},{64,32},{96,64},{128,96},{160,128},{192,160},{224,1... | collective-permute-start | bytes 786440 | tf_op jit(solution)/shard_map/ppermute | solution.py:35
  176.2 8.2 %collective-permute-start.19 = (bf16[4,4,16,512]{3,2,1,0:T(8,128)(2,1)S(1)}, bf16[4,4,16,512]{3,2,1,0:T(8,128)(2,1)}, u32[]{:S(2)}, u32[]{:S(2)}) collective-permute-start(bf16[4,4,16,512]{3,2,1,0:T(8,128)(2,1)S(1)} %collective-permute-done.18), channel_id=1, source_target_pairs={{0,32},{32,64},{64,96},{96,128},{128,160},{160,192},{192,224},{224... | collective-permute-start | bytes 786440 | tf_op jit(solution)/shard_map/ppermute | solution.py:35
  176.2 8.6 %collective-permute-start.23 = (bf16[4,4,16,512]{3,2,1,0:T(8,128)(2,1)S(1)}, bf16[4,4,16,512]{3,2,1,0:T(8,128)(2,1)}, u32[]{:S(2)}, u32[]{:S(2)}) collective-permute-start(bf16[4,4,16,512]{3,2,1,0:T(8,128)(2,1)S(1)} %collective-permute-done.22), channel_id=1, source_target_pairs={{0,224},{32,0},{64,32},{96,64},{128,96},{160,128},{192,160},{224,1... | collective-permute-start | bytes 786440 | tf_op jit(solution)/shard_map/ppermute | solution.py:35
  184.4 7.5 %collective-permute-start.20 = (bf16[4,4,16,512]{3,2,1,0:T(8,128)(2,1)}, bf16[4,4,16,512]{3,2,1,0:T(8,128)(2,1)}, u32[]{:S(2)}, u32[]{:S(2)}) collective-permute-start(bf16[4,4,16,512]{3,2,1,0:T(8,128)(2,1)} %collective-permute-done.19), channel_id=1, source_target_pairs={{0,32},{32,64},{64,96},{96,128},{128,160},{160,192},{192,224},{224... | collective-permute-start | bytes 786440 | tf_op jit(solution)/shard_map/ppermute | solution.py:35
  184.4 14.5 %collective-permute-start.25 = (bf16[8,4,16,512]{3,2,1,0:T(8,128)(2,1)S(1)}, bf16[8,4,16,512]{3,2,1,0:T(8,128)(2,1)S(1)}, u32[]{:S(2)}, u32[]{:S(2)}) collective-permute-start(bf16[8,4,16,512]{3,2,1,0:T(8,128)(2,1)S(1)} %all-to-all-done.3), channel_id=1, source_target_pairs={{0,8},{8,16},{16,24},{24,0},{1,9},{9,17},{17,25},{25,1},{2,10},{10... | collective-permute-start | bytes 1572872 | tf_op jit(solution)/shard_map/ppermute | solution.py:35
  184.8 24.8 %collective-permute-start.26 = (bf16[8,4,16,512]{3,2,1,0:T(8,128)(2,1)S(1)}, bf16[8,4,16,512]{3,2,1,0:T(8,128)(2,1)S(1)}, u32[]{:S(2)}, u32[]{:S(2)}) collective-permute-start(bf16[8,4,16,512]{3,2,1,0:T(8,128)(2,1)S(1)} %all-to-all-done.3), channel_id=1, source_target_pairs={{0,16},{8,24},{16,0},{24,8},{1,17},{9,25},{17,1},{25,9},{2,18},{10... | collective-permute-start | bytes 1572872 | tf_op jit(solution)/shard_map/ppermute | solution.py:35
  187.7 22.7 %collective-permute-start.27 = (bf16[8,4,16,512]{3,2,1,0:T(8,128)(2,1)S(1)}, bf16[8,4,16,512]{3,2,1,0:T(8,128)(2,1)S(1)}, u32[]{:S(2)}, u32[]{:S(2)}) collective-permute-start(bf16[8,4,16,512]{3,2,1,0:T(8,128)(2,1)S(1)} %all-to-all-done.3), channel_id=1, source_target_pairs={{0,24},{8,0},{16,8},{24,16},{1,25},{9,1},{17,9},{25,17},{2,26},{10... | collective-permute-start | bytes 1572872 | tf_op jit(solution)/shard_map/ppermute | solution.py:35
  188.1 6.2 %collective-permute-start.24 = (bf16[4,4,16,512]{3,2,1,0:T(8,128)(2,1)}, bf16[4,4,16,512]{3,2,1,0:T(8,128)(2,1)S(1)}, u32[]{:S(2)}, u32[]{:S(2)}) collective-permute-start(bf16[4,4,16,512]{3,2,1,0:T(8,128)(2,1)} %collective-permute-done.23), channel_id=1, source_target_pairs={{0,224},{32,0},{64,32},{96,64},{128,96},{160,128},{192,160},{224,1... | collective-permute-start | bytes 786440 | tf_op jit(solution)/shard_map/ppermute | solution.py:35
  192.0 6.9 %collective-permute-start.21 = (bf16[4,4,16,512]{3,2,1,0:T(8,128)(2,1)}, bf16[4,4,16,512]{3,2,1,0:T(8,128)(2,1)S(1)}, u32[]{:S(2)}, u32[]{:S(2)}) collective-permute-start(bf16[4,4,16,512]{3,2,1,0:T(8,128)(2,1)} %collective-permute-done.20), channel_id=1, source_target_pairs={{0,32},{32,64},{64,96},{96,128},{128,160},{160,192},{192,224},{224... | collective-permute-start | bytes 786440 | tf_op jit(solution)/shard_map/ppermute | solution.py:35
  210.4 24.9 %copy-start.10 = (f32[22]{0:T(128)S(1)}, f32[22]{0:T(128)}, u32[]{:S(2)}) copy-start(f32[22]{0:T(128)} %param.29) | copy-start | bytes 268
  210.4 24.9 %copy-start.11 = (f32[22]{0:T(128)S(1)}, f32[22]{0:T(128)}, u32[]{:S(2)}) copy-start(f32[22]{0:T(128)} %param.28) | copy-start | bytes 268
  226.7 17.9 %all-to-all-start.4 = ((f32[32,8,128]{2,1,0:T(8,128)}), f32[32,8,128]{2,1,0:T(8,128)S(1)}, u32[]{:S(2)}, u32[]{:S(2)}) async-start(f32[32,8,128]{2,1,0:T(8,128)} %logits.1), calls=%async_computation.4 | async-start | bytes 262144 | tf_op jit(solution)/shard_map/all_to_all | solution.py:459
  244.6 0.6 copy-start.6
  246.9 10.1 %all-to-all-start.5 = ((f32[8,8,128]{2,1,0:T(8,128)}), f32[8,8,128]{2,1,0:T(8,128)S(1)}, u32[]{:S(2)}, u32[]{:S(2)}) async-start(f32[8,8,128]{2,1,0:T(8,128)} %get-tuple-element.22), calls=%async_computation.5 | async-start | bytes 65536 | tf_op jit(solution)/shard_map/all_to_all | solution.py:464
  257.0 0.6 copy-start.8

commit v3 on v2

--- a/solution.py
+++ b/solution.py
@@ -35,10 +35,9 @@
     return lax.ppermute(array, axis, [(i, (i + by) % n) for i in range(n)])
 
 
-def call(kernel, out_shape, args, scalars=None, scratch=(), flops=0, vmem=None):
+def call(kernel, out_shape, args, scalars=None, scratch=(), flops=0, vmem=4):
     spec = pl.BlockSpec(memory_space=pltpu.VMEM)
     many = isinstance(out_shape, (list, tuple))
-    params = {} if vmem is None else {"vmem_limit_bytes": vmem}
     return pl.pallas_call(
         kernel,
         out_shape=out_shape,
@@ -46,7 +45,7 @@
         + [spec] * len(args),
         out_specs=[spec] * len(out_shape) if many else spec,
         scratch_shapes=scratch,
-        compiler_params=pltpu.CompilerParams(**params),
+        compiler_params=pltpu.CompilerParams(vmem_limit_bytes=vmem << 20),
         cost_estimate=pl.CostEstimate(flops=flops, bytes_accessed=0, transcendentals=0)
         if flops
         else None,
@@ -283,8 +282,9 @@
 
     @pl.loop(1, BLOCKS)
     def _(j):
+        logits = multiply(j)
         reduce(j - 1, logit_ref[lax.rem(j - 1, 2)])
-        logit_ref[lax.rem(j, 2)] = multiply(j)
+        logit_ref[lax.rem(j, 2)] = logits
 
     reduce(jnp.int32(BLOCKS - 1), logit_ref[(BLOCKS - 1) % 2])
     lines = []
@@ -377,7 +377,7 @@
     packed = call(
         pack_kernel, sds((32, 5, 8, 128), bf16),
         (embedded, targets, labels.reshape(1, 4), destinations.reshape(1, 4)),
-        scratch=[pltpu.VMEM((8, 128), f32)],
+        scratch=[pltpu.VMEM((8, 128), f32)], vmem=60,
     )
     got = lax.all_to_all(packed, DP, 0, 0, tiled=True)
 
@@ -405,6 +405,7 @@
         at,
         scratch=[pltpu.VMEM((8, 16, 256), bf16)],
         flops=1 << 30,
+        vmem=60,
     )
     got_part = shift(send, "c", 1)
     pair = call(pair_kernel, sds((4, 8, 16, 512), bf16), (keep, got_part))

time: 260 us -> 253 us (0.973)
  Pallas kernels: 33.5 us -> 28.3 us
  waiting for transfers between devices: 109 us -> 112 us
  local copies, waits for them, and re-layouts: 9.54 us -> 6.7 us
    pallas_call x7, Pallas kernels: 17.2 us -> 13.5 us  [call(): pl.pallas_call(kernel, out_shape=out_shape, in_specs=([pl.BlockSpec(memor...]
  transfers between devices with their start and end apart: 34 -> 34, of which waited for: 16 -> 16; matrix products, arithmetic and copies ran while one was open for 4% -> 2% of each run, Pallas kernels for 5% -> 4%
where the time goes in v3:
time: 253 us
  waiting for transfers between devices  112 us (44%)
  starting transfers between devices  75.1 us (30%)
  blocking collectives  28.8 us (11%)
  Pallas kernels  28.3 us (11%)
  local copies, waits for them, and re-layouts  6.7 us (3%)
    ppermute x28, waiting for transfers between devices, shift(): return lax.ppermute(array, axis, [(i, (i + by) % n) for i in range(n)])  76.2 us
    ppermute x28, starting transfers between devices, shift(): return lax.ppermute(array, axis, [(i, (i + by) % n) for i in range(n)])  34.2 us
    all_gather x1, blocking collectives, program(): same = lax.all_gather(block, 'x', axis=0, tiled=False)  28.8 us
    pallas_call x1, Pallas kernels, logits_call(): pl.pallas_call(logits_kernel, out_shape=sds((32, 8, 128), f32), in_specs=...  14.8 us
    pallas_call x7, Pallas kernels, call(): pl.pallas_call(kernel, out_shape=out_shape, in_specs=([pl.BlockSpec(memor...  13.5 us
    all_to_all x1, starting transfers between devices, program(): got = lax.all_to_all(packed, DP, 0, 0, tiled=True)  12 us
    all_to_all x1, waiting for transfers between devices, program(): sums = lax.all_to_all(pair, 'x', 0, 0, tiled=True)  8.95 us
    all_to_all x1, starting transfers between devices, program(): merged = lax.all_to_all(pieces, DP, 0, 0, tiled=True)  8.85 us
  transfers between devices with their start and end apart: 34, of which 16 were waited for; matrix products, arithmetic and copies ran while one was open for 2% of the time, Pallas kernels for 4%

profile of v3, /device:TPU:1, one launch (start us, length us, event | category | flops | bytes accessed | tf_op | source)
XLA Modules:
  0.0 252.6 jit_solution(13109124539870735616)
XLA Ops:
  0.6 1.8 shard_map.175
  2.4 12.0 %all-to-all-start = ((bf16[32,5,8,128]{3,2,1,0:T(8,128)(2,1)}), bf16[32,5,8,128]{3,2,1,0:T(8,128)(2,1)S(1)}, u32[]{:S(2)}, u32[]{:S(2)}) async-start(bf16[32,5,8,128]{3,2,1,0:T(8,128)(2,1)} %shard_map.175), calls=%async_computation | async-start | bytes 655360 | tf_op jit(solution)/shard_map/all_to_all | solution.py:382
  14.5 3.2 %fusion.10 = (bf16[256,2048]{1,0:T(8,128)(2,1)}, bf16[256,2048]{1,0:T(8,128)(2,1)}) fusion(bf16[512,2048]{1,0:T(8,128)(2,1)} %refs_0_.1), kind=kLoop, calls=%fused_computation.32 | loop fusion | bytes 4194304 | tf_op jit(solution)/shard_map/slice | solution.py:414
  17.6 2.5 collective-permute-start.3
  20.3 6.8 %all-to-all-done = bf16[32,5,8,128]{3,2,1,0:T(8,128)(2,1)S(1)} async-done(((bf16[32,5,8,128]{3,2,1,0:T(8,128)(2,1)}), bf16[32,5,8,128]{3,2,1,0:T(8,128)(2,1)S(1)}, u32[]{:S(2)}, u32[]{:S(2)}) %all-to-all-start) | async-done | bytes 327712 | tf_op jit(solution)/shard_map/all_to_all | solution.py:382
  27.6 1.2 shard_map.176
  28.9 4.8 %all-to-all-start.1 = ((bf16[32,16,128]{2,1,0:T(8,128)(2,1)}), bf16[32,16,128]{2,1,0:T(8,128)(2,1)S(1)}, u32[]{:S(2)}, u32[]{:S(2)}) async-start(bf16[32,16,128]{2,1,0:T(8,128)(2,1)} %bitcast.8), calls=%async_computation.1 | async-start | bytes 262144 | tf_op jit(solution)/shard_map/all_to_all | solution.py:392
  33.7 2.6 %collective-permute-start.5 = (bf16[256,2048]{1,0:T(8,128)(2,1)}, bf16[256,2048]{1,0:T(8,128)(2,1)}, u32[]{:S(2)}, u32[]{:S(2)}) collective-permute-start(bf16[256,2048]{1,0:T(8,128)(2,1)} %get-tuple-element.30), channel_id=1, source_target_pairs={{0,6},{2,0},{4,2},{6,4},{1,7},{3,1},{5,3},{7,5},{8,14},{10,8},{12,... | collective-permute-start | bytes 3145736 | tf_op jit(solution)/shard_map/ppermute | solution.py:35
  36.3 6.8 %all-to-all-done.1 = bf16[32,16,128]{2,1,0:T(8,128)(2,1)S(1)} async-done(((bf16[32,16,128]{2,1,0:T(8,128)(2,1)}), bf16[32,16,128]{2,1,0:T(8,128)(2,1)S(1)}, u32[]{:S(2)}, u32[]{:S(2)}) %all-to-all-start.1) | async-done | bytes 131104 | tf_op jit(solution)/shard_map/all_to_all | solution.py:392
  43.1 28.8 %all-gather = bf16[128,16,128]{2,1,0:T(8,128)(2,1)S(1)} all-gather(bf16[32,16,128]{2,1,0:T(8,128)(2,1)S(1)} %all-to-all-done.1), channel_id=2, replica_groups=mesh['z'=8,'y'=4,'x'=4,'c'=2] {'x'}, dimensions={0}, use_global_device_ids=true | all-gather | bytes 655360 | tf_op jit(solution)/shard_map/all_gather | solution.py:394
  71.8 3.3 %collective-permute-start.13 = (bf16[4,32,16,128]{3,2,1,0:T(8,128)(2,1)S(1)}, bf16[4,32,16,128]{3,2,1,0:T(8,128)(2,1)S(1)}, u32[]{:S(2)}, u32[]{:S(2)}) collective-permute-start(bf16[4,32,16,128]{3,2,1,0:T(8,128)(2,1)S(1)} %bitcast.53), channel_id=1, source_target_pairs={{0,1},{1,0},{2,3},{3,2},{4,5},{5,4},{6,7},{7,6},{8,9},{9,8},{10,11... | collective-permute-start | bytes 1572872 | tf_op jit(solution)/shard_map/ppermute | solution.py:35
  75.1 2.0 collective-permute-start.1
  77.8 1.2 collective-permute-start.4
  79.3 0.8 copy-done.5
  80.1 6.4 %shard_map.177 = (bf16[4,8,16,512]{3,2,1,0:T(8,128)(2,1)}, bf16[4,8,16,512]{3,2,1,0:T(8,128)(2,1)}, bf16[8,16,512]{2,1,0:T(8,128)(2,1)}) custom-call(s32[4]{0:T(128)} %pad_add_fusion.at_ref, bf16[4,32,16,128]{3,2,1,0:T(8,128)(2,1)} %bitcast.54, bf16[4,32,16,128]{3,2,1,0:T(8,128)(2,1)} %copy-done.5, f32[8,1,512]{2,1,0:T(1,128)} %bitcast.59, ...), custom_call_target="tpu_custom_call" | custom-call | flops 1073741824 | tf_op jit(solution)/shard_map/pallas_call | solution.py:41
  86.5 0.9 collective-permute-start.14
  87.5 14.7 %collective-permute-done.1.refs_2_ = bf16[256,2048]{1,0:T(8,128)(2,1)} collective-permute-done((bf16[256,2048]{1,0:T(8,128)(2,1)}, bf16[256,2048]{1,0:T(8,128)(2,1)}, u32[]{:S(2)}, u32[]{:S(2)}) %collective-permute-start.1) | collective-permute-done | bytes 1048608 | tf_op jit(solution)/shard_map/ppermute | solution.py:35
  103.5 21.2 %collective-permute-done.2.refs_3_ = bf16[256,2048]{1,0:T(8,128)(2,1)} collective-permute-done((bf16[256,2048]{1,0:T(8,128)(2,1)S(1)}, bf16[256,2048]{1,0:T(8,128)(2,1)}, u32[]{:S(2)}, u32[]{:S(2)}) %collective-permute-start.2) | collective-permute-done | bytes 1048608 | tf_op jit(solution)/shard_map/ppermute | solution.py:35
  125.3 1.0 copy-done
  126.3 0.9 shard_map.178
  127.2 3.5 %all-to-all-start.2 = ((bf16[4,8,16,512]{3,2,1,0:T(8,128)(2,1)}), bf16[4,8,16,512]{3,2,1,0:T(8,128)(2,1)S(1)}, u32[]{:S(2)}, u32[]{:S(2)}) async-start(bf16[4,8,16,512]{3,2,1,0:T(8,128)(2,1)} %shard_map.178), calls=%async_computation.2 | async-start | bytes 1048576 | tf_op jit(solution)/shard_map/all_to_all | solution.py:412
  131.3 9.0 %all-to-all-done.2.sums = bf16[4,8,16,512]{3,2,1,0:T(8,128)(2,1)S(1)} async-done(((bf16[4,8,16,512]{3,2,1,0:T(8,128)(2,1)}), bf16[4,8,16,512]{3,2,1,0:T(8,128)(2,1)S(1)}, u32[]{:S(2)}, u32[]{:S(2)}) %all-to-all-start.2) | async-done | bytes 524320 | tf_op jit(solution)/shard_map/all_to_all | solution.py:412
  140.3 1.6 shard_map.179
  141.8 1.2 collective-permute-start.15
  143.1 3.1 %collective-permute-done.15 = bf16[4,16,512]{2,1,0:T(8,128)(2,1)S(1)} collective-permute-done((bf16[4,16,512]{2,1,0:T(8,128)(2,1)S(1)}, bf16[4,16,512]{2,1,0:T(8,128)(2,1)S(1)}, u32[]{:S(2)}, u32[]{:S(2)}) %collective-permute-start.15) | collective-permute-done | bytes 65568 | tf_op jit(solution)/shard_map/ppermute | solution.py:35
  146.2 1.5 collective-permute-start.16
  147.7 6.4 %all-to-all-start.3 = ((bf16[8,4,16,512]{3,2,1,0:T(8,128)(2,1)}), bf16[8,4,16,512]{3,2,1,0:T(8,128)(2,1)S(1)}, u32[]{:S(2)}, u32[]{:S(2)}) async-start(bf16[8,4,16,512]{3,2,1,0:T(8,128)(2,1)} %get-tuple-element.19), calls=%async_computation.3 | async-start | bytes 1048576 | tf_op jit(solution)/shard_map/all_to_all | solution.py:446
  154.1 1.0 collective-permute-start.17
  155.0 2.2 collective-permute-done.17
  157.3 3.7 %collective-permute-start.9 = (bf16[256,2048]{1,0:T(8,128)(2,1)}, bf16[256,2048]{1,0:T(8,128)(2,1)}, u32[]{:S(2)}, u32[]{:S(2)}) collective-permute-start(bf16[256,2048]{1,0:T(8,128)(2,1)} %collective-permute-done.2.refs_3_), channel_id=1, source_target_pairs={{0,1},{1,0},{2,3},{3,2},{4,5},{5,4},{6,7},{7,6},{8,9},{9,8},{10,11... | collective-permute-start | bytes 3145736 | tf_op jit(solution)/shard_map/ppermute | solution.py:35
  161.0 1.7 collective-permute-start.18
  162.8 1.3 collective-permute-start.22
  164.1 10.1 %collective-permute-done.18 = bf16[4,4,16,512]{3,2,1,0:T(8,128)(2,1)S(1)} collective-permute-done((bf16[4,4,16,512]{3,2,1,0:T(8,128)(2,1)S(1)}, bf16[4,4,16,512]{3,2,1,0:T(8,128)(2,1)S(1)}, u32[]{:S(2)}, u32[]{:S(2)}) %collective-permute-start.18) | collective-permute-done | bytes 262176 | tf_op jit(solution)/shard_map/ppermute | solution.py:35
  174.2 2.7 %collective-permute-start.23 = (bf16[4,4,16,512]{3,2,1,0:T(8,128)(2,1)S(1)}, bf16[4,4,16,512]{3,2,1,0:T(8,128)(2,1)}, u32[]{:S(2)}, u32[]{:S(2)}) collective-permute-start(bf16[4,4,16,512]{3,2,1,0:T(8,128)(2,1)S(1)} %collective-permute-done.22), channel_id=1, source_target_pairs={{0,224},{32,0},{64,32},{96,64},{128,96},{160,128},{192,160},{224,1... | collective-permute-start | bytes 786440 | tf_op jit(solution)/shard_map/ppermute | solution.py:35
  176.9 5.2 %collective-permute-done.19 = bf16[4,4,16,512]{3,2,1,0:T(8,128)(2,1)} collective-permute-done((bf16[4,4,16,512]{3,2,1,0:T(8,128)(2,1)S(1)}, bf16[4,4,16,512]{3,2,1,0:T(8,128)(2,1)}, u32[]{:S(2)}, u32[]{:S(2)}) %collective-permute-start.19) | collective-permute-done | bytes 262176 | tf_op jit(solution)/shard_map/ppermute | solution.py:35
  182.5 2.6 %collective-permute-start.26 = (bf16[8,4,16,512]{3,2,1,0:T(8,128)(2,1)S(1)}, bf16[8,4,16,512]{3,2,1,0:T(8,128)(2,1)S(1)}, u32[]{:S(2)}, u32[]{:S(2)}) collective-permute-start(bf16[8,4,16,512]{3,2,1,0:T(8,128)(2,1)S(1)} %all-to-all-done.3), channel_id=1, source_target_pairs={{0,16},{8,24},{16,0},{24,8},{1,17},{9,25},{17,1},{25,9},{2,18},{10... | collective-permute-start | bytes 1572872 | tf_op jit(solution)/shard_map/ppermute | solution.py:35
  185.8 2.6 %collective-permute-start.24 = (bf16[4,4,16,512]{3,2,1,0:T(8,128)(2,1)}, bf16[4,4,16,512]{3,2,1,0:T(8,128)(2,1)S(1)}, u32[]{:S(2)}, u32[]{:S(2)}) collective-permute-start(bf16[4,4,16,512]{3,2,1,0:T(8,128)(2,1)} %collective-permute-done.23), channel_id=1, source_target_pairs={{0,224},{32,0},{64,32},{96,64},{128,96},{160,128},{192,160},{224,1... | collective-permute-start | bytes 786440 | tf_op jit(solution)/shard_map/ppermute | solution.py:35
  188.4 1.0 collective-permute-done.20
  189.4 2.6 %collective-permute-done.24 = bf16[4,4,16,512]{3,2,1,0:T(8,128)(2,1)S(1)} collective-permute-done((bf16[4,4,16,512]{3,2,1,0:T(8,128)(2,1)}, bf16[4,4,16,512]{3,2,1,0:T(8,128)(2,1)S(1)}, u32[]{:S(2)}, u32[]{:S(2)}) %collective-permute-start.24) | collective-permute-done | bytes 262176 | tf_op jit(solution)/shard_map/ppermute | solution.py:35
  192.0 4.3 %collective-permute-done.21 = bf16[4,4,16,512]{3,2,1,0:T(8,128)(2,1)S(1)} collective-permute-done((bf16[4,4,16,512]{3,2,1,0:T(8,128)(2,1)}, bf16[4,4,16,512]{3,2,1,0:T(8,128)(2,1)S(1)}, u32[]{:S(2)}, u32[]{:S(2)}) %collective-permute-start.21) | collective-permute-done | bytes 262176 | tf_op jit(solution)/shard_map/ppermute | solution.py:35
  196.3 10.2 %collective-permute-done.26 = bf16[8,4,16,512]{3,2,1,0:T(8,128)(2,1)S(1)} collective-permute-done((bf16[8,4,16,512]{3,2,1,0:T(8,128)(2,1)S(1)}, bf16[8,4,16,512]{3,2,1,0:T(8,128)(2,1)S(1)}, u32[]{:S(2)}, u32[]{:S(2)}) %collective-permute-start.26) | collective-permute-done | bytes 524320 | tf_op jit(solution)/shard_map/ppermute | solution.py:35
  206.5 1.5 collective-permute-done.27
  208.0 14.8 %logits.1 = f32[32,8,128]{2,1,0:T(8,128)} custom-call(s32[4]{0:T(128)S(1)} %copy-done.3, bf16[512,2048]{1,0:T(8,128)(2,1)} %refs_0_.1, bf16[256,2048]{1,0:T(8,128)(2,1)S(1)} %collective-permute-done.refs_1_, bf16[256,2048]{1,0:T(8,128)(2,1)} %collective-permute-done.1.refs_2_, bf16[256,2048]{1,0:T(8,128)(2,1)} %collective-permute-done.2.refs_3_, ...), custom_call_target="tpu_custom_call" | custom-call | flops 8589934592 | bytes 20971520 | tf_op jit(solution)/shard_map/logits/pallas_call | solution.py:304
  222.9 8.8 %all-to-all-start.4 = ((f32[32,8,128]{2,1,0:T(8,128)}), f32[32,8,128]{2,1,0:T(8,128)S(1)}, u32[]{:S(2)}, u32[]{:S(2)}) async-start(f32[32,8,128]{2,1,0:T(8,128)} %logits.1), calls=%async_computation.4 | async-start | bytes 262144 | tf_op jit(solution)/shard_map/all_to_all | solution.py:460
  232.4 8.7 %all-to-all-done.4.got_ref = f32[32,8,128]{2,1,0:T(8,128)S(1)} async-done(((f32[32,8,128]{2,1,0:T(8,128)}), f32[32,8,128]{2,1,0:T(8,128)S(1)}, u32[]{:S(2)}, u32[]{:S(2)}) %all-to-all-start.4) | async-done | bytes 131104 | tf_op jit(solution)/shard_map/all_to_all | solution.py:460
  241.1 0.8 shard_map.180
  241.9 5.3 %all-to-all-start.5 = ((f32[8,8,128]{2,1,0:T(8,128)}), f32[8,8,128]{2,1,0:T(8,128)S(1)}, u32[]{:S(2)}, u32[]{:S(2)}) async-start(f32[8,8,128]{2,1,0:T(8,128)} %get-tuple-element.22), calls=%async_computation.5 | async-start | bytes 65536 | tf_op jit(solution)/shard_map/all_to_all | solution.py:465
  247.8 4.2 %all-to-all-done.5.sums_ref = f32[8,8,128]{2,1,0:T(8,128)S(1)} async-done(((f32[8,8,128]{2,1,0:T(8,128)}), f32[8,8,128]{2,1,0:T(8,128)S(1)}, u32[]{:S(2)}, u32[]{:S(2)}) %all-to-all-start.5) | async-done | bytes 32800 | tf_op jit(solution)/shard_map/all_to_all | solution.py:465
  (77 shorter events, 7.2 us)
Async XLA Ops:
  2.4 24.7 %all-to-all-start = ((bf16[32,5,8,128]{3,2,1,0:T(8,128)(2,1)}), bf16[32,5,8,128]{3,2,1,0:T(8,128)(2,1)S(1)}, u32[]{:S(2)}, u32[]{:S(2)}) async-start(bf16[32,5,8,128]{3,2,1,0:T(8,128)(2,1)} %shard_map.175), calls=%async_computation | async-start | bytes 655360 | tf_op jit(solution)/shard_map/all_to_all | solution.py:382
  14.5 5.7 %copy-start.7 = (s32[32]{0:T(128)S(1)}, s32[32]{0:T(128)}, u32[]{:S(2)}) copy-start(s32[32]{0:T(128)} %param.19) | copy-start | bytes 388
  17.6 60.2 %collective-permute-start.3 = (bf16[256,2048]{1,0:T(8,128)(2,1)}, bf16[256,2048]{1,0:T(8,128)(2,1)S(1)}, u32[]{:S(2)}, u32[]{:S(2)}) collective-permute-start(bf16[256,2048]{1,0:T(8,128)(2,1)} %get-tuple-element.29), channel_id=1, source_target_pairs={{0,6},{2,0},{4,2},{6,4},{1,7},{3,1},{5,3},{7,5},{8,14},{10,8},{12,... | collective-permute-start | bytes 3145736 | tf_op jit(solution)/shard_map/ppermute | solution.py:35
  20.1 58.9 %collective-permute-start = (bf16[256,2048]{1,0:T(8,128)(2,1)}, bf16[256,2048]{1,0:T(8,128)(2,1)S(1)}, u32[]{:S(2)}, u32[]{:S(2)}) collective-permute-start(bf16[256,2048]{1,0:T(8,128)(2,1)} %get-tuple-element.30), channel_id=1, source_target_pairs={{0,2},{2,4},{4,6},{6,0},{1,3},{3,5},{5,7},{7,1},{8,10},{10,12},{12... | collective-permute-start | bytes 3145736 | tf_op jit(solution)/shard_map/ppermute | solution.py:35
  27.2 98.1 %copy-start.6 = (bf16[32,8,128]{2,1,0:T(8,128)(2,1)}, bf16[32,8,128]{2,1,0:T(8,128)(2,1)S(1)}, u32[]{:S(2)}) copy-start(bf16[32,8,128]{2,1,0:T(8,128)(2,1)S(1)} %slice_bitcast_fusion) | copy-start | bytes 196612
  28.9 14.2 %all-to-all-start.1 = ((bf16[32,16,128]{2,1,0:T(8,128)(2,1)}), bf16[32,16,128]{2,1,0:T(8,128)(2,1)S(1)}, u32[]{:S(2)}, u32[]{:S(2)}) async-start(bf16[32,16,128]{2,1,0:T(8,128)(2,1)} %bitcast.8), calls=%async_computation.1 | async-start | bytes 262144 | tf_op jit(solution)/shard_map/all_to_all | solution.py:392
  33.7 53.7 %collective-permute-start.5 = (bf16[256,2048]{1,0:T(8,128)(2,1)}, bf16[256,2048]{1,0:T(8,128)(2,1)}, u32[]{:S(2)}, u32[]{:S(2)}) collective-permute-start(bf16[256,2048]{1,0:T(8,128)(2,1)} %get-tuple-element.30), channel_id=1, source_target_pairs={{0,6},{2,0},{4,2},{6,4},{1,7},{3,1},{5,3},{7,5},{8,14},{10,8},{12,... | collective-permute-start | bytes 3145736 | tf_op jit(solution)/shard_map/ppermute | solution.py:35
  71.8 7.5 %copy-start.4 = (bf16[128,16,128]{2,1,0:T(8,128)(2,1)}, bf16[128,16,128]{2,1,0:T(8,128)(2,1)S(1)}, u32[]{:S(2)}) copy-start(bf16[128,16,128]{2,1,0:T(8,128)(2,1)S(1)} %all-gather) | copy-start | bytes 1572868
  71.8 7.5 %collective-permute-start.13 = (bf16[4,32,16,128]{3,2,1,0:T(8,128)(2,1)S(1)}, bf16[4,32,16,128]{3,2,1,0:T(8,128)(2,1)S(1)}, u32[]{:S(2)}, u32[]{:S(2)}) collective-permute-start(bf16[4,32,16,128]{3,2,1,0:T(8,128)(2,1)S(1)} %bitcast.53), channel_id=1, source_target_pairs={{0,1},{1,0},{2,3},{3,2},{4,5},{5,4},{6,7},{7,6},{8,9},{9,8},{10,11... | collective-permute-start | bytes 1572872 | tf_op jit(solution)/shard_map/ppermute | solution.py:35
  75.1 27.1 %collective-permute-start.1 = (bf16[256,2048]{1,0:T(8,128)(2,1)}, bf16[256,2048]{1,0:T(8,128)(2,1)}, u32[]{:S(2)}, u32[]{:S(2)}) collective-permute-start(bf16[256,2048]{1,0:T(8,128)(2,1)} %get-tuple-element.29), channel_id=1, source_target_pairs={{0,2},{2,4},{4,6},{6,0},{1,3},{3,5},{5,7},{7,1},{8,10},{10,12},{12... | collective-permute-start | bytes 3145736 | tf_op jit(solution)/shard_map/ppermute | solution.py:35
  77.8 25.2 %collective-permute-start.4 = (bf16[256,2048]{1,0:T(8,128)(2,1)S(1)}, bf16[256,2048]{1,0:T(8,128)(2,1)}, u32[]{:S(2)}, u32[]{:S(2)}) collective-permute-start(bf16[256,2048]{1,0:T(8,128)(2,1)S(1)} %collective-permute-done.3.refs_6_), channel_id=1, source_target_pairs={{0,6},{2,0},{4,2},{6,4},{1,7},{3,1},{5,3},{7,5},{8,14},{10,8},{12,... | collective-permute-start | bytes 3145736 | tf_op jit(solution)/shard_map/ppermute | solution.py:35
  79.0 45.6 %collective-permute-start.2 = (bf16[256,2048]{1,0:T(8,128)(2,1)S(1)}, bf16[256,2048]{1,0:T(8,128)(2,1)}, u32[]{:S(2)}, u32[]{:S(2)}) collective-permute-start(bf16[256,2048]{1,0:T(8,128)(2,1)S(1)} %collective-permute-done.refs_1_), channel_id=1, source_target_pairs={{0,2},{2,4},{4,6},{6,0},{1,3},{3,5},{5,7},{7,1},{8,10},{10,12},{12... | collective-permute-start | bytes 3145736 | tf_op jit(solution)/shard_map/ppermute | solution.py:35
  79.3 0.8 copy-start.5
  86.5 53.8 %copy-start.2 = (f32[4096]{0:T(1024)S(1)}, f32[4096]{0:T(1024)}, u32[]{:S(2)}) copy-start(f32[4096]{0:T(1024)} %param.26) | copy-start | bytes 49156
  86.5 53.8 %copy-start.3 = (s32[4]{0:T(128)S(1)}, s32[4]{0:T(128)}, u32[]{:S(2)}) copy-start(s32[4]{0:T(128)} %pad_add_fusion.at_ref) | copy-start | bytes 52
  86.5 16.5 %collective-permute-start.14 = (bf16[4,8,16,512]{3,2,1,0:T(8,128)(2,1)}, bf16[4,8,16,512]{3,2,1,0:T(8,128)(2,1)S(1)}, u32[]{:S(2)}, u32[]{:S(2)}) collective-permute-start(bf16[4,8,16,512]{3,2,1,0:T(8,128)(2,1)} %get-tuple-element.16), channel_id=1, source_target_pairs={{0,1},{1,0},{2,3},{3,2},{4,5},{5,4},{6,7},{7,6},{8,9},{9,8},{10,11... | collective-permute-start | bytes 1572872 | tf_op jit(solution)/shard_map/ppermute | solution.py:35
  87.4 43.4 %collective-permute-start.12 = (bf16[256,2048]{1,0:T(8,128)(2,1)S(1)}, bf16[256,2048]{1,0:T(8,128)(2,1)}, u32[]{:S(2)}, u32[]{:S(2)}) collective-permute-start(bf16[256,2048]{1,0:T(8,128)(2,1)S(1)} %collective-permute-done.3.refs_6_), channel_id=1, source_target_pairs={{0,1},{1,0},{2,3},{3,2},{4,5},{5,4},{6,7},{7,6},{8,9},{9,8},{10,11... | collective-permute-start | bytes 3145736 | tf_op jit(solution)/shard_map/ppermute | solution.py:35
  102.2 79.9 %collective-permute-start.6 = (bf16[512,2048]{1,0:T(8,128)(2,1)}, bf16[512,2048]{1,0:T(8,128)(2,1)}, u32[]{:S(2)}, u32[]{:S(2)}) collective-permute-start(bf16[512,2048]{1,0:T(8,128)(2,1)} %refs_0_.1), channel_id=1, source_target_pairs={{0,1},{1,0},{2,3},{3,2},{4,5},{5,4},{6,7},{7,6},{8,9},{9,8},{10,11... | collective-permute-start | bytes 6291464 | tf_op jit(solution)/shard_map/ppermute | solution.py:35
  103.0 38.9 %collective-permute-start.7 = (bf16[256,2048]{1,0:T(8,128)(2,1)S(1)}, bf16[256,2048]{1,0:T(8,128)(2,1)}, u32[]{:S(2)}, u32[]{:S(2)}) collective-permute-start(bf16[256,2048]{1,0:T(8,128)(2,1)S(1)} %collective-permute-done.refs_1_), channel_id=1, source_target_pairs={{0,1},{1,0},{2,3},{3,2},{4,5},{5,4},{6,7},{7,6},{8,9},{9,8},{10,11... | collective-permute-start | bytes 3145736 | tf_op jit(solution)/shard_map/ppermute | solution.py:35
  103.0 58.1 %collective-permute-start.11 = (bf16[256,2048]{1,0:T(8,128)(2,1)}, bf16[256,2048]{1,0:T(8,128)(2,1)}, u32[]{:S(2)}, u32[]{:S(2)}) collective-permute-start(bf16[256,2048]{1,0:T(8,128)(2,1)} %collective-permute-done.5.refs_5_), channel_id=1, source_target_pairs={{0,1},{1,0},{2,3},{3,2},{4,5},{5,4},{6,7},{7,6},{8,9},{9,8},{10,11... | collective-permute-start | bytes 3145736 | tf_op jit(solution)/shard_map/ppermute | solution.py:35
  124.7 38.1 %collective-permute-start.8 = (bf16[256,2048]{1,0:T(8,128)(2,1)}, bf16[256,2048]{1,0:T(8,128)(2,1)}, u32[]{:S(2)}, u32[]{:S(2)}) collective-permute-start(bf16[256,2048]{1,0:T(8,128)(2,1)} %collective-permute-done.1.refs_2_), channel_id=1, source_target_pairs={{0,1},{1,0},{2,3},{3,2},{4,5},{5,4},{6,7},{7,6},{8,9},{9,8},{10,11... | collective-permute-start | bytes 3145736 | tf_op jit(solution)/shard_map/ppermute | solution.py:35
  125.3 1.0 copy-start
  126.3 4.4 %slice-start = ((bf16[32,8,128]{2,1,0:T(8,128)(2,1)}), bf16[32,4,128]{2,1,0:T(4,128)(2,1)S(1)}, s32[]{:S(2)}) async-start(bf16[32,8,128]{2,1,0:T(8,128)(2,1)} %copy-done.6), calls=%async_computation.6 | async-start | bytes 65536 | tf_op jit(solution)/shard_map/slice | solution.py:423
  126.3 14.0 %copy-start.1 = (bf16[8,16,512]{2,1,0:T(8,128)(2,1)S(1)}, bf16[8,16,512]{2,1,0:T(8,128)(2,1)}, u32[]{:S(2)}) copy-start(bf16[8,16,512]{2,1,0:T(8,128)(2,1)} %get-tuple-element.14.resid) | copy-start | bytes 393220
  127.2 13.0 %all-to-all-start.2 = ((bf16[4,8,16,512]{3,2,1,0:T(8,128)(2,1)}), bf16[4,8,16,512]{3,2,1,0:T(8,128)(2,1)S(1)}, u32[]{:S(2)}, u32[]{:S(2)}) async-start(bf16[4,8,16,512]{3,2,1,0:T(8,128)(2,1)} %shard_map.178), calls=%async_computation.2 | async-start | bytes 1048576 | tf_op jit(solution)/shard_map/all_to_all | solution.py:412
  130.9 54.2 %collective-permute-start.10 = (bf16[256,2048]{1,0:T(8,128)(2,1)}, bf16[256,2048]{1,0:T(8,128)(2,1)}, u32[]{:S(2)}, u32[]{:S(2)}) collective-permute-start(bf16[256,2048]{1,0:T(8,128)(2,1)} %collective-permute-done.4.refs_4_), channel_id=1, source_target_pairs={{0,1},{1,0},{2,3},{3,2},{4,5},{5,4},{6,7},{7,6},{8,9},{9,8},{10,11... | collective-permute-start | bytes 3145736 | tf_op jit(solution)/shard_map/ppermute | solution.py:35
  141.8 4.3 %collective-permute-start.15 = (bf16[4,16,512]{2,1,0:T(8,128)(2,1)S(1)}, bf16[4,16,512]{2,1,0:T(8,128)(2,1)S(1)}, u32[]{:S(2)}, u32[]{:S(2)}) collective-permute-start(bf16[4,16,512]{2,1,0:T(8,128)(2,1)S(1)} %get-tuple-element.18), channel_id=1, source_target_pairs={{0,8},{8,16},{16,24},{24,0},{1,9},{9,17},{17,25},{25,1},{2,10},{10... | collective-permute-start | bytes 196616 | tf_op jit(solution)/shard_map/ppermute | solution.py:35
  146.2 7.9 %collective-permute-start.16 = (bf16[4,16,512]{2,1,0:T(8,128)(2,1)S(1)}, bf16[4,16,512]{2,1,0:T(8,128)(2,1)S(1)}, u32[]{:S(2)}, u32[]{:S(2)}) collective-permute-start(bf16[4,16,512]{2,1,0:T(8,128)(2,1)S(1)} %get-tuple-element.18), channel_id=1, source_target_pairs={{0,16},{8,24},{16,0},{24,8},{1,17},{9,25},{17,1},{25,9},{2,18},{10... | collective-permute-start | bytes 196616 | tf_op jit(solution)/shard_map/ppermute | solution.py:35
  147.7 34.4 %all-to-all-start.3 = ((bf16[8,4,16,512]{3,2,1,0:T(8,128)(2,1)}), bf16[8,4,16,512]{3,2,1,0:T(8,128)(2,1)S(1)}, u32[]{:S(2)}, u32[]{:S(2)}) async-start(bf16[8,4,16,512]{3,2,1,0:T(8,128)(2,1)} %get-tuple-element.19), calls=%async_computation.3 | async-start | bytes 1048576 | tf_op jit(solution)/shard_map/all_to_all | solution.py:446
  154.1 3.2 %collective-permute-start.17 = (bf16[4,16,512]{2,1,0:T(8,128)(2,1)S(1)}, bf16[4,16,512]{2,1,0:T(8,128)(2,1)S(1)}, u32[]{:S(2)}, u32[]{:S(2)}) collective-permute-start(bf16[4,16,512]{2,1,0:T(8,128)(2,1)S(1)} %get-tuple-element.18), channel_id=1, source_target_pairs={{0,24},{8,0},{16,8},{24,16},{1,25},{9,1},{17,9},{25,17},{2,26},{10... | collective-permute-start | bytes 196616 | tf_op jit(solution)/shard_map/ppermute | solution.py:35
  157.3 28.5 %collective-permute-start.9 = (bf16[256,2048]{1,0:T(8,128)(2,1)}, bf16[256,2048]{1,0:T(8,128)(2,1)}, u32[]{:S(2)}, u32[]{:S(2)}) collective-permute-start(bf16[256,2048]{1,0:T(8,128)(2,1)} %collective-permute-done.2.refs_3_), channel_id=1, source_target_pairs={{0,1},{1,0},{2,3},{3,2},{4,5},{5,4},{6,7},{7,6},{8,9},{9,8},{10,11... | collective-permute-start | bytes 3145736 | tf_op jit(solution)/shard_map/ppermute | solution.py:35
  161.0 13.1 %collective-permute-start.18 = (bf16[4,4,16,512]{3,2,1,0:T(8,128)(2,1)S(1)}, bf16[4,4,16,512]{3,2,1,0:T(8,128)(2,1)S(1)}, u32[]{:S(2)}, u32[]{:S(2)}) collective-permute-start(bf16[4,4,16,512]{3,2,1,0:T(8,128)(2,1)S(1)} %pad_maximum_fusion), channel_id=1, source_target_pairs={{0,32},{32,64},{64,96},{96,128},{128,160},{160,192},{192,224},{224... | collective-permute-start | bytes 786440 | tf_op jit(solution)/shard_map/ppermute | solution.py:35
  162.8 11.4 %collective-permute-start.22 = (bf16[4,4,16,512]{3,2,1,0:T(8,128)(2,1)S(1)}, bf16[4,4,16,512]{3,2,1,0:T(8,128)(2,1)S(1)}, u32[]{:S(2)}, u32[]{:S(2)}) collective-permute-start(bf16[4,4,16,512]{3,2,1,0:T(8,128)(2,1)S(1)} %pad_maximum_fusion), channel_id=1, source_target_pairs={{0,224},{32,0},{64,32},{96,64},{128,96},{160,128},{192,160},{224,1... | collective-permute-start | bytes 786440 | tf_op jit(solution)/shard_map/ppermute | solution.py:35
  174.2 7.9 %collective-permute-start.19 = (bf16[4,4,16,512]{3,2,1,0:T(8,128)(2,1)S(1)}, bf16[4,4,16,512]{3,2,1,0:T(8,128)(2,1)}, u32[]{:S(2)}, u32[]{:S(2)}) collective-permute-start(bf16[4,4,16,512]{3,2,1,0:T(8,128)(2,1)S(1)} %collective-permute-done.18), channel_id=1, source_target_pairs={{0,32},{32,64},{64,96},{96,128},{128,160},{160,192},{192,224},{224... | collective-permute-start | bytes 786440 | tf_op jit(solution)/shard_map/ppermute | solution.py:35
  174.2 8.3 %collective-permute-start.23 = (bf16[4,4,16,512]{3,2,1,0:T(8,128)(2,1)S(1)}, bf16[4,4,16,512]{3,2,1,0:T(8,128)(2,1)}, u32[]{:S(2)}, u32[]{:S(2)}) collective-permute-start(bf16[4,4,16,512]{3,2,1,0:T(8,128)(2,1)S(1)} %collective-permute-done.22), channel_id=1, source_target_pairs={{0,224},{32,0},{64,32},{96,64},{128,96},{160,128},{192,160},{224,1... | collective-permute-start | bytes 786440 | tf_op jit(solution)/shard_map/ppermute | solution.py:35
  182.1 7.3 %collective-permute-start.20 = (bf16[4,4,16,512]{3,2,1,0:T(8,128)(2,1)}, bf16[4,4,16,512]{3,2,1,0:T(8,128)(2,1)}, u32[]{:S(2)}, u32[]{:S(2)}) collective-permute-start(bf16[4,4,16,512]{3,2,1,0:T(8,128)(2,1)} %collective-permute-done.19), channel_id=1, source_target_pairs={{0,32},{32,64},{64,96},{96,128},{128,160},{160,192},{192,224},{224... | collective-permute-start | bytes 786440 | tf_op jit(solution)/shard_map/ppermute | solution.py:35
  182.1 14.2 %collective-permute-start.25 = (bf16[8,4,16,512]{3,2,1,0:T(8,128)(2,1)S(1)}, bf16[8,4,16,512]{3,2,1,0:T(8,128)(2,1)S(1)}, u32[]{:S(2)}, u32[]{:S(2)}) collective-permute-start(bf16[8,4,16,512]{3,2,1,0:T(8,128)(2,1)S(1)} %all-to-all-done.3), channel_id=1, source_target_pairs={{0,8},{8,16},{16,24},{24,0},{1,9},{9,17},{17,25},{25,1},{2,10},{10... | collective-permute-start | bytes 1572872 | tf_op jit(solution)/shard_map/ppermute | solution.py:35
  182.5 24.1 %collective-permute-start.26 = (bf16[8,4,16,512]{3,2,1,0:T(8,128)(2,1)S(1)}, bf16[8,4,16,512]{3,2,1,0:T(8,128)(2,1)S(1)}, u32[]{:S(2)}, u32[]{:S(2)}) collective-permute-start(bf16[8,4,16,512]{3,2,1,0:T(8,128)(2,1)S(1)} %all-to-all-done.3), channel_id=1, source_target_pairs={{0,16},{8,24},{16,0},{24,8},{1,17},{9,25},{17,1},{25,9},{2,18},{10... | collective-permute-start | bytes 1572872 | tf_op jit(solution)/shard_map/ppermute | solution.py:35
  185.0 23.0 %collective-permute-start.27 = (bf16[8,4,16,512]{3,2,1,0:T(8,128)(2,1)S(1)}, bf16[8,4,16,512]{3,2,1,0:T(8,128)(2,1)S(1)}, u32[]{:S(2)}, u32[]{:S(2)}) collective-permute-start(bf16[8,4,16,512]{3,2,1,0:T(8,128)(2,1)S(1)} %all-to-all-done.3), channel_id=1, source_target_pairs={{0,24},{8,0},{16,8},{24,16},{1,25},{9,1},{17,9},{25,17},{2,26},{10... | collective-permute-start | bytes 1572872 | tf_op jit(solution)/shard_map/ppermute | solution.py:35
  185.8 6.2 %collective-permute-start.24 = (bf16[4,4,16,512]{3,2,1,0:T(8,128)(2,1)}, bf16[4,4,16,512]{3,2,1,0:T(8,128)(2,1)S(1)}, u32[]{:S(2)}, u32[]{:S(2)}) collective-permute-start(bf16[4,4,16,512]{3,2,1,0:T(8,128)(2,1)} %collective-permute-done.23), channel_id=1, source_target_pairs={{0,224},{32,0},{64,32},{96,64},{128,96},{160,128},{192,160},{224,1... | collective-permute-start | bytes 786440 | tf_op jit(solution)/shard_map/ppermute | solution.py:35
  189.4 6.9 %collective-permute-start.21 = (bf16[4,4,16,512]{3,2,1,0:T(8,128)(2,1)}, bf16[4,4,16,512]{3,2,1,0:T(8,128)(2,1)S(1)}, u32[]{:S(2)}, u32[]{:S(2)}) collective-permute-start(bf16[4,4,16,512]{3,2,1,0:T(8,128)(2,1)} %collective-permute-done.20), channel_id=1, source_target_pairs={{0,32},{32,64},{64,96},{96,128},{128,160},{160,192},{192,224},{224... | collective-permute-start | bytes 786440 | tf_op jit(solution)/shard_map/ppermute | solution.py:35
  208.0 23.7 %copy-start.8 = (f32[22]{0:T(128)S(1)}, f32[22]{0:T(128)}, u32[]{:S(2)}) copy-start(f32[22]{0:T(128)} %param.29) | copy-start | bytes 268
  208.0 23.7 %copy-start.9 = (f32[22]{0:T(128)S(1)}, f32[22]{0:T(128)}, u32[]{:S(2)}) copy-start(f32[22]{0:T(128)} %param.28) | copy-start | bytes 268
  222.9 18.2 %all-to-all-start.4 = ((f32[32,8,128]{2,1,0:T(8,128)}), f32[32,8,128]{2,1,0:T(8,128)S(1)}, u32[]{:S(2)}, u32[]{:S(2)}) async-start(f32[32,8,128]{2,1,0:T(8,128)} %logits.1), calls=%async_computation.4 | async-start | bytes 262144 | tf_op jit(solution)/shard_map/all_to_all | solution.py:460
  241.9 10.0 %all-to-all-start.5 = ((f32[8,8,128]{2,1,0:T(8,128)}), f32[8,8,128]{2,1,0:T(8,128)S(1)}, u32[]{:S(2)}, u32[]{:S(2)}) async-start(f32[8,8,128]{2,1,0:T(8,128)} %get-tuple-element.22), calls=%async_computation.5 | async-start | bytes 65536 | tf_op jit(solution)/shard_map/all_to_all | solution.py:465

commit v4 on v3

--- a/solution.py
+++ b/solution.py
@@ -171,10 +171,6 @@
                 cols.append(jnp.where(first, v[:8], v[8:]))
             rows.append(jnp.concatenate(cols, axis=1))
         resid_ref[fb] = jnp.concatenate(rows, axis=0).astype(bf16)
-
-
-def pair_kernel(keep_ref, got_ref, out_ref):
-    out_ref[...] = (keep_ref[...].astype(f32) + got_ref[...].astype(f32)).astype(bf16)
 
 
 def final_kernel(at_ref, resid, sums, gain, fa_ref, fb_ref, hidden_ref):
@@ -205,9 +201,9 @@
 
 
 def logits_kernel(at_ref, *refs):
-    pieces, rows, goal_ref = refs[:14], refs[14:26], refs[26]
-    (out_ref, buffer, stage_ref, rows_ref, logit_ref, top_ref, sum_ref, pick_ref, goals_ref,
-     sems, row_sems) = refs[27:]
+    pieces, rows_a, rows_b, goal_ref = refs[:14], refs[14:22], refs[22:26], refs[26]
+    (out_ref, buffer, rows_ref, logit_ref, top_ref, sum_ref, pick_ref, goals_ref,
+     sems) = refs[27:]
     whole, starts, at = (0, 7), [], 0
     for p in range(14):
         starts.append(at)
@@ -224,16 +220,6 @@
             for p, ref in enumerate(pieces)
         ]
 
-    row_copies = [
-        pltpu.make_async_copy(ref, stage_ref.at[pl.ds(k * 256, 256)], row_sems.at[k])
-        for k, ref in enumerate(rows[:8])
-    ] + [
-        pltpu.make_async_copy(ref, stage_ref.at[pl.ds(2048 + k * 512, 512)], row_sems.at[8 + k])
-        for k, ref in enumerate(rows[8:])
-    ]
-    for copy in row_copies:
-        copy.start()
-
     @pl.loop(0, BLOCKS)
     def _(j):
         for copy in copies(j):
@@ -248,8 +234,6 @@
     sum_ref[...] = jnp.zeros((512, 1), f32)
     pick_ref[...] = jnp.zeros((512, 1), f32)
 
-    for copy in row_copies:
-        copy.wait()
     z, y = at_ref[2], at_ref[3]
     for dz in range(8):
         for dy in range(4):
@@ -257,10 +241,8 @@
             a_rows = pl.ds(pl.multiple_of((lax.rem(z + (8 - dz), 8) * 4 + in_y) * 16, 16), 16)
             b_rows = pl.ds(pl.multiple_of((dz * 4 + in_y) * 16, 16), 16)
             for k in range(4):
-                lo = dz * 256 + (dy * 4 + k) * 16
-                rows_ref[a_rows, k * 512 : k * 512 + 512] = stage_ref[lo : lo + 16]
-                lo = 2048 + dy * 512 + (dz * 4 + k) * 16
-                rows_ref[b_rows, 2048 + k * 512 : 2560 + k * 512] = stage_ref[lo : lo + 16]
+                rows_ref[a_rows, k * 512 : k * 512 + 512] = rows_a[dz][dy, k]
+                rows_ref[b_rows, 2048 + k * 512 : 2560 + k * 512] = rows_b[dy][dz, k]
 
     def multiply(j):
         for copy in copies(j):
@@ -300,17 +282,15 @@
 def logits_call(at, weights, rows, goals):
     vmem = pl.BlockSpec(memory_space=pltpu.VMEM)
     hbm = pl.BlockSpec(memory_space=pltpu.HBM)
-    rows = [r.reshape(-1, 512) for r in rows]
     return pl.pallas_call(
         logits_kernel,
         out_shape=sds((32, 8, 128), f32),
         in_specs=[pl.BlockSpec(memory_space=pltpu.SMEM)]
-        + [hbm] * (len(weights) + len(rows))
-        + [vmem],
+        + [hbm] * len(weights)
+        + [vmem] * (len(rows) + 1),
         out_specs=vmem,
         scratch_shapes=[
             pltpu.VMEM((BLOCKS, 4096, WIDTH), bf16),
-            pltpu.VMEM((4096, 512), bf16),
             pltpu.VMEM((512, 4096), bf16),
             pltpu.VMEM((2, 512, WIDTH), f32),
             pltpu.VMEM((512, 1), f32),
@@ -318,7 +298,6 @@
             pltpu.VMEM((512, 1), f32),
             pltpu.VMEM((512, 1), f32),
             pltpu.SemaphoreType.DMA((BLOCKS, 14)),
-            pltpu.SemaphoreType.DMA((12,)),
         ],
         name="logits",
         cost_estimate=pl.CostEstimate(
@@ -408,7 +387,7 @@
         vmem=60,
     )
     got_part = shift(send, "c", 1)
-    pair = call(pair_kernel, sds((4, 8, 16, 512), bf16), (keep, got_part))
+    pair = (keep.astype(f32) + got_part.astype(f32)).astype(bf16)
     sums = lax.all_to_all(pair, "x", 0, 0, tiled=True)
 
     rows = w_vocab[FRONT:]

time: 253 us -> 253 us (level)
    pallas_call x7 -> x6, Pallas kernels: 13.5 us -> 12.5 us  [call(): pl.pallas_call(kernel, out_shape=out_shape, in_specs=([pl.BlockSpec(memor...]
  transfers between devices with their start and end apart: 34 -> 34, of which waited for: 16 -> 16; matrix products, arithmetic and copies ran while one was open for 2% -> 3% of each run, Pallas kernels for 4% -> 4%
where the time goes in v4:
time: 253 us
  waiting for transfers between devices  112 us (44%)
  starting transfers between devices  75.2 us (30%)
  blocking collectives  28.8 us (11%)
  Pallas kernels  27.2 us (11%)
  local copies, waits for them, and re-layouts  5.67 us (2%)
  other arithmetic  3.21 us (1%)
    ppermute x28, waiting for transfers between devices, shift(): return lax.ppermute(array, axis, [(i, (i + by) % n) for i in range(n)])  76.2 us
    ppermute x28, starting transfers between devices, shift(): return lax.ppermute(array, axis, [(i, (i + by) % n) for i in range(n)])  34.3 us
    all_gather x1, blocking collectives, program(): same = lax.all_gather(block, 'x', axis=0, tiled=False)  28.8 us
    pallas_call x1, Pallas kernels, logits_call(): pl.pallas_call(logits_kernel, out_shape=sds((32, 8, 128), f32), in_specs=...  14.7 us
    pallas_call x6, Pallas kernels, call(): pl.pallas_call(kernel, out_shape=out_shape, in_specs=([pl.BlockSpec(memor...  12.5 us
    all_to_all x1, starting transfers between devices, program(): got = lax.all_to_all(packed, DP, 0, 0, tiled=True)  12 us
    all_to_all x1, waiting for transfers between devices, program(): sums = lax.all_to_all(pair, 'x', 0, 0, tiled=True)  8.95 us
    all_to_all x1, starting transfers between devices, program(): merged = lax.all_to_all(pieces, DP, 0, 0, tiled=True)  8.91 us
  transfers between devices with their start and end apart: 34, of which 16 were waited for; matrix products, arithmetic and copies ran while one was open for 3% of the time, Pallas kernels for 4%

profile of v4, /device:TPU:1, one launch (start us, length us, event | category | flops | bytes accessed | tf_op | source)
XLA Modules:
  0.0 252.7 jit_solution(9632338039016403811)
XLA Ops:
  0.6 1.8 shard_map.175
  2.4 12.0 %all-to-all-start = ((bf16[32,5,8,128]{3,2,1,0:T(8,128)(2,1)}), bf16[32,5,8,128]{3,2,1,0:T(8,128)(2,1)S(1)}, u32[]{:S(2)}, u32[]{:S(2)}) async-start(bf16[32,5,8,128]{3,2,1,0:T(8,128)(2,1)} %shard_map.175), calls=%async_computation | async-start | bytes 655360 | tf_op jit(solution)/shard_map/all_to_all | solution.py:361
  14.5 3.2 %fusion.10 = (bf16[256,2048]{1,0:T(8,128)(2,1)}, bf16[256,2048]{1,0:T(8,128)(2,1)}) fusion(bf16[512,2048]{1,0:T(8,128)(2,1)} %refs_0_.1), kind=kLoop, calls=%fused_computation.33 | loop fusion | bytes 4194304 | tf_op jit(solution)/shard_map/slice | solution.py:393
  17.6 2.5 collective-permute-start.3
  20.3 6.8 %all-to-all-done = bf16[32,5,8,128]{3,2,1,0:T(8,128)(2,1)S(1)} async-done(((bf16[32,5,8,128]{3,2,1,0:T(8,128)(2,1)}), bf16[32,5,8,128]{3,2,1,0:T(8,128)(2,1)S(1)}, u32[]{:S(2)}, u32[]{:S(2)}) %all-to-all-start) | async-done | bytes 327712 | tf_op jit(solution)/shard_map/all_to_all | solution.py:361
  27.6 1.3 shard_map.176
  28.9 4.8 %all-to-all-start.1 = ((bf16[32,16,128]{2,1,0:T(8,128)(2,1)}), bf16[32,16,128]{2,1,0:T(8,128)(2,1)S(1)}, u32[]{:S(2)}, u32[]{:S(2)}) async-start(bf16[32,16,128]{2,1,0:T(8,128)(2,1)} %bitcast.8), calls=%async_computation.1 | async-start | bytes 262144 | tf_op jit(solution)/shard_map/all_to_all | solution.py:371
  33.7 2.6 %collective-permute-start.5 = (bf16[256,2048]{1,0:T(8,128)(2,1)}, bf16[256,2048]{1,0:T(8,128)(2,1)}, u32[]{:S(2)}, u32[]{:S(2)}) collective-permute-start(bf16[256,2048]{1,0:T(8,128)(2,1)} %get-tuple-element.30), channel_id=1, source_target_pairs={{0,6},{2,0},{4,2},{6,4},{1,7},{3,1},{5,3},{7,5},{8,14},{10,8},{12,... | collective-permute-start | bytes 3145736 | tf_op jit(solution)/shard_map/ppermute | solution.py:35
  36.3 6.8 %all-to-all-done.1 = bf16[32,16,128]{2,1,0:T(8,128)(2,1)S(1)} async-done(((bf16[32,16,128]{2,1,0:T(8,128)(2,1)}), bf16[32,16,128]{2,1,0:T(8,128)(2,1)S(1)}, u32[]{:S(2)}, u32[]{:S(2)}) %all-to-all-start.1) | async-done | bytes 131104 | tf_op jit(solution)/shard_map/all_to_all | solution.py:371
  43.0 28.8 %all-gather = bf16[128,16,128]{2,1,0:T(8,128)(2,1)S(1)} all-gather(bf16[32,16,128]{2,1,0:T(8,128)(2,1)S(1)} %all-to-all-done.1), channel_id=2, replica_groups=mesh['z'=8,'y'=4,'x'=4,'c'=2] {'x'}, dimensions={0}, use_global_device_ids=true | all-gather | bytes 655360 | tf_op jit(solution)/shard_map/all_gather | solution.py:373
  71.8 3.3 %collective-permute-start.13 = (bf16[4,32,16,128]{3,2,1,0:T(8,128)(2,1)S(1)}, bf16[4,32,16,128]{3,2,1,0:T(8,128)(2,1)S(1)}, u32[]{:S(2)}, u32[]{:S(2)}) collective-permute-start(bf16[4,32,16,128]{3,2,1,0:T(8,128)(2,1)S(1)} %bitcast.32), channel_id=1, source_target_pairs={{0,1},{1,0},{2,3},{3,2},{4,5},{5,4},{6,7},{7,6},{8,9},{9,8},{10,11... | collective-permute-start | bytes 1572872 | tf_op jit(solution)/shard_map/ppermute | solution.py:35
  75.1 2.0 collective-permute-start.1
  77.1 1.2 collective-permute-start.4
  79.2 0.8 copy-done.4
  80.0 6.4 %shard_map.177 = (bf16[4,8,16,512]{3,2,1,0:T(8,128)(2,1)}, bf16[4,8,16,512]{3,2,1,0:T(8,128)(2,1)}, bf16[8,16,512]{2,1,0:T(8,128)(2,1)}) custom-call(s32[4]{0:T(128)} %pad_add_fusion.at_ref, bf16[4,32,16,128]{3,2,1,0:T(8,128)(2,1)} %bitcast.33, bf16[4,32,16,128]{3,2,1,0:T(8,128)(2,1)} %copy-done.4, f32[8,1,512]{2,1,0:T(1,128)} %bitcast.38, ...), custom_call_target="tpu_custom_call" | custom-call | flops 1073741824 | tf_op jit(solution)/shard_map/pallas_call | solution.py:41
  86.4 0.9 collective-permute-start.14
  87.4 14.7 %collective-permute-done.1.refs_2_ = bf16[256,2048]{1,0:T(8,128)(2,1)} collective-permute-done((bf16[256,2048]{1,0:T(8,128)(2,1)}, bf16[256,2048]{1,0:T(8,128)(2,1)}, u32[]{:S(2)}, u32[]{:S(2)}) %collective-permute-start.1) | collective-permute-done | bytes 1048608 | tf_op jit(solution)/shard_map/ppermute | solution.py:35
  102.2 0.8 collective-permute-start.6
  103.6 21.1 %collective-permute-done.2.refs_3_ = bf16[256,2048]{1,0:T(8,128)(2,1)} collective-permute-done((bf16[256,2048]{1,0:T(8,128)(2,1)S(1)}, bf16[256,2048]{1,0:T(8,128)(2,1)}, u32[]{:S(2)}, u32[]{:S(2)}) %collective-permute-start.2) | collective-permute-done | bytes 1048608 | tf_op jit(solution)/shard_map/ppermute | solution.py:35
  125.2 2.0 add_convert_fusion
  127.3 3.5 %all-to-all-start.2 = ((bf16[4,8,16,512]{3,2,1,0:T(8,128)(2,1)}), bf16[4,8,16,512]{3,2,1,0:T(8,128)(2,1)S(1)}, u32[]{:S(2)}, u32[]{:S(2)}) async-start(bf16[4,8,16,512]{3,2,1,0:T(8,128)(2,1)} %add_convert_fusion), calls=%async_computation.2 | async-start | bytes 1048576 | tf_op jit(solution)/shard_map/all_to_all | solution.py:391
  131.3 9.0 %all-to-all-done.2.sums = bf16[4,8,16,512]{3,2,1,0:T(8,128)(2,1)S(1)} async-done(((bf16[4,8,16,512]{3,2,1,0:T(8,128)(2,1)}), bf16[4,8,16,512]{3,2,1,0:T(8,128)(2,1)S(1)}, u32[]{:S(2)}, u32[]{:S(2)}) %all-to-all-start.2) | async-done | bytes 524320 | tf_op jit(solution)/shard_map/all_to_all | solution.py:391
  140.3 1.6 shard_map.178
  141.9 1.2 collective-permute-start.15
  143.1 3.1 %collective-permute-done.15 = bf16[4,16,512]{2,1,0:T(8,128)(2,1)S(1)} collective-permute-done((bf16[4,16,512]{2,1,0:T(8,128)(2,1)S(1)}, bf16[4,16,512]{2,1,0:T(8,128)(2,1)S(1)}, u32[]{:S(2)}, u32[]{:S(2)}) %collective-permute-start.15) | collective-permute-done | bytes 65568 | tf_op jit(solution)/shard_map/ppermute | solution.py:35
  146.2 1.5 collective-permute-start.16
  147.7 6.4 %all-to-all-start.3 = ((bf16[8,4,16,512]{3,2,1,0:T(8,128)(2,1)}), bf16[8,4,16,512]{3,2,1,0:T(8,128)(2,1)S(1)}, u32[]{:S(2)}, u32[]{:S(2)}) async-start(bf16[8,4,16,512]{3,2,1,0:T(8,128)(2,1)} %get-tuple-element.19), calls=%async_computation.3 | async-start | bytes 1048576 | tf_op jit(solution)/shard_map/all_to_all | solution.py:425
  154.1 1.0 collective-permute-start.17
  155.1 2.2 collective-permute-done.17
  157.3 3.7 %collective-permute-start.9 = (bf16[256,2048]{1,0:T(8,128)(2,1)}, bf16[256,2048]{1,0:T(8,128)(2,1)}, u32[]{:S(2)}, u32[]{:S(2)}) collective-permute-start(bf16[256,2048]{1,0:T(8,128)(2,1)} %collective-permute-done.2.refs_3_), channel_id=1, source_target_pairs={{0,1},{1,0},{2,3},{3,2},{4,5},{5,4},{6,7},{7,6},{8,9},{9,8},{10,11... | collective-permute-start | bytes 3145736 | tf_op jit(solution)/shard_map/ppermute | solution.py:35
  161.1 1.7 collective-permute-start.18
  162.8 1.3 collective-permute-start.22
  164.1 10.1 %collective-permute-done.18.refs_15_ = bf16[4,4,16,512]{3,2,1,0:T(8,128)(2,1)S(1)} collective-permute-done((bf16[4,4,16,512]{3,2,1,0:T(8,128)(2,1)S(1)}, bf16[4,4,16,512]{3,2,1,0:T(8,128)(2,1)S(1)}, u32[]{:S(2)}, u32[]{:S(2)}) %collective-permute-start.18) | collective-permute-done | bytes 262176 | tf_op jit(solution)/shard_map/ppermute | solution.py:35
  174.2 2.7 %collective-permute-start.23 = (bf16[4,4,16,512]{3,2,1,0:T(8,128)(2,1)S(1)}, bf16[4,4,16,512]{3,2,1,0:T(8,128)(2,1)}, u32[]{:S(2)}, u32[]{:S(2)}) collective-permute-start(bf16[4,4,16,512]{3,2,1,0:T(8,128)(2,1)S(1)} %collective-permute-done.22.refs_21_), channel_id=1, source_target_pairs={{0,224},{32,0},{64,32},{96,64},{128,96},{160,128},{192,160},{224,1... | collective-permute-start | bytes 786440 | tf_op jit(solution)/shard_map/ppermute | solution.py:35
  176.9 5.2 %collective-permute-done.19.refs_16_ = bf16[4,4,16,512]{3,2,1,0:T(8,128)(2,1)} collective-permute-done((bf16[4,4,16,512]{3,2,1,0:T(8,128)(2,1)S(1)}, bf16[4,4,16,512]{3,2,1,0:T(8,128)(2,1)}, u32[]{:S(2)}, u32[]{:S(2)}) %collective-permute-start.19) | collective-permute-done | bytes 262176 | tf_op jit(solution)/shard_map/ppermute | solution.py:35
  182.5 2.6 %collective-permute-start.26 = (bf16[8,4,16,512]{3,2,1,0:T(8,128)(2,1)S(1)}, bf16[8,4,16,512]{3,2,1,0:T(8,128)(2,1)S(1)}, u32[]{:S(2)}, u32[]{:S(2)}) collective-permute-start(bf16[8,4,16,512]{3,2,1,0:T(8,128)(2,1)S(1)} %all-to-all-done.3.refs_22_), channel_id=1, source_target_pairs={{0,16},{8,24},{16,0},{24,8},{1,17},{9,25},{17,1},{25,9},{2,18},{10... | collective-permute-start | bytes 1572872 | tf_op jit(solution)/shard_map/ppermute | solution.py:35
  185.8 2.6 %collective-permute-start.24 = (bf16[4,4,16,512]{3,2,1,0:T(8,128)(2,1)}, bf16[4,4,16,512]{3,2,1,0:T(8,128)(2,1)S(1)}, u32[]{:S(2)}, u32[]{:S(2)}) collective-permute-start(bf16[4,4,16,512]{3,2,1,0:T(8,128)(2,1)} %collective-permute-done.23.refs_20_), channel_id=1, source_target_pairs={{0,224},{32,0},{64,32},{96,64},{128,96},{160,128},{192,160},{224,1... | collective-permute-start | bytes 786440 | tf_op jit(solution)/shard_map/ppermute | solution.py:35
  188.4 1.0 collective-permute-done.20.refs_17_
  189.4 2.6 %collective-permute-done.24.refs_19_ = bf16[4,4,16,512]{3,2,1,0:T(8,128)(2,1)S(1)} collective-permute-done((bf16[4,4,16,512]{3,2,1,0:T(8,128)(2,1)}, bf16[4,4,16,512]{3,2,1,0:T(8,128)(2,1)S(1)}, u32[]{:S(2)}, u32[]{:S(2)}) %collective-permute-start.24) | collective-permute-done | bytes 262176 | tf_op jit(solution)/shard_map/ppermute | solution.py:35
  192.0 4.3 %collective-permute-done.21.refs_18_ = bf16[4,4,16,512]{3,2,1,0:T(8,128)(2,1)S(1)} collective-permute-done((bf16[4,4,16,512]{3,2,1,0:T(8,128)(2,1)}, bf16[4,4,16,512]{3,2,1,0:T(8,128)(2,1)S(1)}, u32[]{:S(2)}, u32[]{:S(2)}) %collective-permute-start.21) | collective-permute-done | bytes 262176 | tf_op jit(solution)/shard_map/ppermute | solution.py:35
  196.4 10.3 %collective-permute-done.26.refs_24_ = bf16[8,4,16,512]{3,2,1,0:T(8,128)(2,1)S(1)} collective-permute-done((bf16[8,4,16,512]{3,2,1,0:T(8,128)(2,1)S(1)}, bf16[8,4,16,512]{3,2,1,0:T(8,128)(2,1)S(1)}, u32[]{:S(2)}, u32[]{:S(2)}) %collective-permute-start.26) | collective-permute-done | bytes 524320 | tf_op jit(solution)/shard_map/ppermute | solution.py:35
  206.7 1.4 collective-permute-done.27.refs_25_
  208.1 14.7 %logits.1 = f32[32,8,128]{2,1,0:T(8,128)} custom-call(s32[4]{0:T(128)S(1)} %copy-done.2, bf16[512,2048]{1,0:T(8,128)(2,1)} %refs_0_.1, bf16[256,2048]{1,0:T(8,128)(2,1)S(1)} %collective-permute-done.refs_1_, bf16[256,2048]{1,0:T(8,128)(2,1)} %collective-permute-done.1.refs_2_, bf16[256,2048]{1,0:T(8,128)(2,1)} %collective-permute-done.2.refs_3_, ...), custom_call_target="tpu_custom_call" | custom-call | flops 8589934592 | bytes 20971520 | tf_op jit(solution)/shard_map/logits/pallas_call | solution.py:285
  222.8 8.9 %all-to-all-start.4 = ((f32[32,8,128]{2,1,0:T(8,128)}), f32[32,8,128]{2,1,0:T(8,128)S(1)}, u32[]{:S(2)}, u32[]{:S(2)}) async-start(f32[32,8,128]{2,1,0:T(8,128)} %logits.1), calls=%async_computation.4 | async-start | bytes 262144 | tf_op jit(solution)/shard_map/all_to_all | solution.py:439
  232.4 8.7 %all-to-all-done.4.got_ref = f32[32,8,128]{2,1,0:T(8,128)S(1)} async-done(((f32[32,8,128]{2,1,0:T(8,128)}), f32[32,8,128]{2,1,0:T(8,128)S(1)}, u32[]{:S(2)}, u32[]{:S(2)}) %all-to-all-start.4) | async-done | bytes 131104 | tf_op jit(solution)/shard_map/all_to_all | solution.py:439
  241.1 0.8 shard_map.179
  241.9 5.3 %all-to-all-start.5 = ((f32[8,8,128]{2,1,0:T(8,128)}), f32[8,8,128]{2,1,0:T(8,128)S(1)}, u32[]{:S(2)}, u32[]{:S(2)}) async-start(f32[8,8,128]{2,1,0:T(8,128)} %get-tuple-element.22), calls=%async_computation.5 | async-start | bytes 65536 | tf_op jit(solution)/shard_map/all_to_all | solution.py:444
  247.8 4.2 %all-to-all-done.5.sums_ref = f32[8,8,128]{2,1,0:T(8,128)S(1)} async-done(((f32[8,8,128]{2,1,0:T(8,128)}), f32[8,8,128]{2,1,0:T(8,128)S(1)}, u32[]{:S(2)}, u32[]{:S(2)}) %all-to-all-start.5) | async-done | bytes 32800 | tf_op jit(solution)/shard_map/all_to_all | solution.py:444
  (75 shorter events, 6.4 us)
Async XLA Ops:
  2.4 24.7 %all-to-all-start = ((bf16[32,5,8,128]{3,2,1,0:T(8,128)(2,1)}), bf16[32,5,8,128]{3,2,1,0:T(8,128)(2,1)S(1)}, u32[]{:S(2)}, u32[]{:S(2)}) async-start(bf16[32,5,8,128]{3,2,1,0:T(8,128)(2,1)} %shard_map.175), calls=%async_computation | async-start | bytes 655360 | tf_op jit(solution)/shard_map/all_to_all | solution.py:361
  14.5 5.7 %copy-start.6 = (s32[32]{0:T(128)S(1)}, s32[32]{0:T(128)}, u32[]{:S(2)}) copy-start(s32[32]{0:T(128)} %param.19) | copy-start | bytes 388
  17.6 59.5 %collective-permute-start.3 = (bf16[256,2048]{1,0:T(8,128)(2,1)}, bf16[256,2048]{1,0:T(8,128)(2,1)S(1)}, u32[]{:S(2)}, u32[]{:S(2)}) collective-permute-start(bf16[256,2048]{1,0:T(8,128)(2,1)} %get-tuple-element.29), channel_id=1, source_target_pairs={{0,6},{2,0},{4,2},{6,4},{1,7},{3,1},{5,3},{7,5},{8,14},{10,8},{12,... | collective-permute-start | bytes 3145736 | tf_op jit(solution)/shard_map/ppermute | solution.py:35
  20.1 58.2 %collective-permute-start = (bf16[256,2048]{1,0:T(8,128)(2,1)}, bf16[256,2048]{1,0:T(8,128)(2,1)S(1)}, u32[]{:S(2)}, u32[]{:S(2)}) collective-permute-start(bf16[256,2048]{1,0:T(8,128)(2,1)} %get-tuple-element.30), channel_id=1, source_target_pairs={{0,2},{2,4},{4,6},{6,0},{1,3},{3,5},{5,7},{7,1},{8,10},{10,12},{12... | collective-permute-start | bytes 3145736 | tf_op jit(solution)/shard_map/ppermute | solution.py:35
  27.2 75.8 %copy-start.5 = (bf16[32,8,128]{2,1,0:T(8,128)(2,1)}, bf16[32,8,128]{2,1,0:T(8,128)(2,1)S(1)}, u32[]{:S(2)}) copy-start(bf16[32,8,128]{2,1,0:T(8,128)(2,1)S(1)} %slice_bitcast_fusion) | copy-start | bytes 196612
  28.9 14.2 %all-to-all-start.1 = ((bf16[32,16,128]{2,1,0:T(8,128)(2,1)}), bf16[32,16,128]{2,1,0:T(8,128)(2,1)S(1)}, u32[]{:S(2)}, u32[]{:S(2)}) async-start(bf16[32,16,128]{2,1,0:T(8,128)(2,1)} %bitcast.8), calls=%async_computation.1 | async-start | bytes 262144 | tf_op jit(solution)/shard_map/all_to_all | solution.py:371
  33.7 53.6 %collective-permute-start.5 = (bf16[256,2048]{1,0:T(8,128)(2,1)}, bf16[256,2048]{1,0:T(8,128)(2,1)}, u32[]{:S(2)}, u32[]{:S(2)}) collective-permute-start(bf16[256,2048]{1,0:T(8,128)(2,1)} %get-tuple-element.30), channel_id=1, source_target_pairs={{0,6},{2,0},{4,2},{6,4},{1,7},{3,1},{5,3},{7,5},{8,14},{10,8},{12,... | collective-permute-start | bytes 3145736 | tf_op jit(solution)/shard_map/ppermute | solution.py:35
  71.8 7.4 %copy-start.3 = (bf16[128,16,128]{2,1,0:T(8,128)(2,1)}, bf16[128,16,128]{2,1,0:T(8,128)(2,1)S(1)}, u32[]{:S(2)}) copy-start(bf16[128,16,128]{2,1,0:T(8,128)(2,1)S(1)} %all-gather) | copy-start | bytes 1572868
  71.8 7.4 %collective-permute-start.13 = (bf16[4,32,16,128]{3,2,1,0:T(8,128)(2,1)S(1)}, bf16[4,32,16,128]{3,2,1,0:T(8,128)(2,1)S(1)}, u32[]{:S(2)}, u32[]{:S(2)}) collective-permute-start(bf16[4,32,16,128]{3,2,1,0:T(8,128)(2,1)S(1)} %bitcast.32), channel_id=1, source_target_pairs={{0,1},{1,0},{2,3},{3,2},{4,5},{5,4},{6,7},{7,6},{8,9},{9,8},{10,11... | collective-permute-start | bytes 1572872 | tf_op jit(solution)/shard_map/ppermute | solution.py:35
  75.1 27.1 %collective-permute-start.1 = (bf16[256,2048]{1,0:T(8,128)(2,1)}, bf16[256,2048]{1,0:T(8,128)(2,1)}, u32[]{:S(2)}, u32[]{:S(2)}) collective-permute-start(bf16[256,2048]{1,0:T(8,128)(2,1)} %get-tuple-element.29), channel_id=1, source_target_pairs={{0,2},{2,4},{4,6},{6,0},{1,3},{3,5},{5,7},{7,1},{8,10},{10,12},{12... | collective-permute-start | bytes 3145736 | tf_op jit(solution)/shard_map/ppermute | solution.py:35
  77.1 25.8 %collective-permute-start.4 = (bf16[256,2048]{1,0:T(8,128)(2,1)S(1)}, bf16[256,2048]{1,0:T(8,128)(2,1)}, u32[]{:S(2)}, u32[]{:S(2)}) collective-permute-start(bf16[256,2048]{1,0:T(8,128)(2,1)S(1)} %collective-permute-done.3.refs_6_), channel_id=1, source_target_pairs={{0,6},{2,0},{4,2},{6,4},{1,7},{3,1},{5,3},{7,5},{8,14},{10,8},{12,... | collective-permute-start | bytes 3145736 | tf_op jit(solution)/shard_map/ppermute | solution.py:35
  78.4 46.3 %collective-permute-start.2 = (bf16[256,2048]{1,0:T(8,128)(2,1)S(1)}, bf16[256,2048]{1,0:T(8,128)(2,1)}, u32[]{:S(2)}, u32[]{:S(2)}) collective-permute-start(bf16[256,2048]{1,0:T(8,128)(2,1)S(1)} %collective-permute-done.refs_1_), channel_id=1, source_target_pairs={{0,2},{2,4},{4,6},{6,0},{1,3},{3,5},{5,7},{7,1},{8,10},{10,12},{12... | collective-permute-start | bytes 3145736 | tf_op jit(solution)/shard_map/ppermute | solution.py:35
  79.2 0.8 copy-start.4
  86.4 53.9 %copy-start = (bf16[8,16,512]{2,1,0:T(8,128)(2,1)S(1)}, bf16[8,16,512]{2,1,0:T(8,128)(2,1)}, u32[]{:S(2)}) copy-start(bf16[8,16,512]{2,1,0:T(8,128)(2,1)} %get-tuple-element.14.resid) | copy-start | bytes 393220
  86.4 53.9 %copy-start.1 = (f32[4096]{0:T(1024)S(1)}, f32[4096]{0:T(1024)}, u32[]{:S(2)}) copy-start(f32[4096]{0:T(1024)} %param.26) | copy-start | bytes 49156
  86.4 53.9 %copy-start.2 = (s32[4]{0:T(128)S(1)}, s32[4]{0:T(128)}, u32[]{:S(2)}) copy-start(s32[4]{0:T(128)} %pad_add_fusion.at_ref) | copy-start | bytes 52
  86.4 16.6 %collective-permute-start.14 = (bf16[4,8,16,512]{3,2,1,0:T(8,128)(2,1)}, bf16[4,8,16,512]{3,2,1,0:T(8,128)(2,1)S(1)}, u32[]{:S(2)}, u32[]{:S(2)}) collective-permute-start(bf16[4,8,16,512]{3,2,1,0:T(8,128)(2,1)} %get-tuple-element.16), channel_id=1, source_target_pairs={{0,1},{1,0},{2,3},{3,2},{4,5},{5,4},{6,7},{7,6},{8,9},{9,8},{10,11... | collective-permute-start | bytes 1572872 | tf_op jit(solution)/shard_map/ppermute | solution.py:35
  87.3 43.6 %collective-permute-start.12 = (bf16[256,2048]{1,0:T(8,128)(2,1)S(1)}, bf16[256,2048]{1,0:T(8,128)(2,1)}, u32[]{:S(2)}, u32[]{:S(2)}) collective-permute-start(bf16[256,2048]{1,0:T(8,128)(2,1)S(1)} %collective-permute-done.3.refs_6_), channel_id=1, source_target_pairs={{0,1},{1,0},{2,3},{3,2},{4,5},{5,4},{6,7},{7,6},{8,9},{9,8},{10,11... | collective-permute-start | bytes 3145736 | tf_op jit(solution)/shard_map/ppermute | solution.py:35
  102.2 80.0 %collective-permute-start.6 = (bf16[512,2048]{1,0:T(8,128)(2,1)}, bf16[512,2048]{1,0:T(8,128)(2,1)}, u32[]{:S(2)}, u32[]{:S(2)}) collective-permute-start(bf16[512,2048]{1,0:T(8,128)(2,1)} %refs_0_.1), channel_id=1, source_target_pairs={{0,1},{1,0},{2,3},{3,2},{4,5},{5,4},{6,7},{7,6},{8,9},{9,8},{10,11... | collective-permute-start | bytes 6291464 | tf_op jit(solution)/shard_map/ppermute | solution.py:35
  103.0 38.9 %collective-permute-start.7 = (bf16[256,2048]{1,0:T(8,128)(2,1)S(1)}, bf16[256,2048]{1,0:T(8,128)(2,1)}, u32[]{:S(2)}, u32[]{:S(2)}) collective-permute-start(bf16[256,2048]{1,0:T(8,128)(2,1)S(1)} %collective-permute-done.refs_1_), channel_id=1, source_target_pairs={{0,1},{1,0},{2,3},{3,2},{4,5},{5,4},{6,7},{7,6},{8,9},{9,8},{10,11... | collective-permute-start | bytes 3145736 | tf_op jit(solution)/shard_map/ppermute | solution.py:35
  103.0 27.8 %slice-start = ((bf16[32,8,128]{2,1,0:T(8,128)(2,1)}), bf16[32,4,128]{2,1,0:T(4,128)(2,1)S(1)}, s32[]{:S(2)}) async-start(bf16[32,8,128]{2,1,0:T(8,128)(2,1)} %copy-done.5), calls=%async_computation.6 | async-start | bytes 65536 | tf_op jit(solution)/shard_map/slice | solution.py:402
  103.0 58.1 %collective-permute-start.11 = (bf16[256,2048]{1,0:T(8,128)(2,1)}, bf16[256,2048]{1,0:T(8,128)(2,1)}, u32[]{:S(2)}, u32[]{:S(2)}) collective-permute-start(bf16[256,2048]{1,0:T(8,128)(2,1)} %collective-permute-done.5.refs_5_), channel_id=1, source_target_pairs={{0,1},{1,0},{2,3},{3,2},{4,5},{5,4},{6,7},{7,6},{8,9},{9,8},{10,11... | collective-permute-start | bytes 3145736 | tf_op jit(solution)/shard_map/ppermute | solution.py:35
  124.7 38.2 %collective-permute-start.8 = (bf16[256,2048]{1,0:T(8,128)(2,1)}, bf16[256,2048]{1,0:T(8,128)(2,1)}, u32[]{:S(2)}, u32[]{:S(2)}) collective-permute-start(bf16[256,2048]{1,0:T(8,128)(2,1)} %collective-permute-done.1.refs_2_), channel_id=1, source_target_pairs={{0,1},{1,0},{2,3},{3,2},{4,5},{5,4},{6,7},{7,6},{8,9},{9,8},{10,11... | collective-permute-start | bytes 3145736 | tf_op jit(solution)/shard_map/ppermute | solution.py:35
  127.3 13.0 %all-to-all-start.2 = ((bf16[4,8,16,512]{3,2,1,0:T(8,128)(2,1)}), bf16[4,8,16,512]{3,2,1,0:T(8,128)(2,1)S(1)}, u32[]{:S(2)}, u32[]{:S(2)}) async-start(bf16[4,8,16,512]{3,2,1,0:T(8,128)(2,1)} %add_convert_fusion), calls=%async_computation.2 | async-start | bytes 1048576 | tf_op jit(solution)/shard_map/all_to_all | solution.py:391
  130.9 54.2 %collective-permute-start.10 = (bf16[256,2048]{1,0:T(8,128)(2,1)}, bf16[256,2048]{1,0:T(8,128)(2,1)}, u32[]{:S(2)}, u32[]{:S(2)}) collective-permute-start(bf16[256,2048]{1,0:T(8,128)(2,1)} %collective-permute-done.4.refs_4_), channel_id=1, source_target_pairs={{0,1},{1,0},{2,3},{3,2},{4,5},{5,4},{6,7},{7,6},{8,9},{9,8},{10,11... | collective-permute-start | bytes 3145736 | tf_op jit(solution)/shard_map/ppermute | solution.py:35
  141.9 4.3 %collective-permute-start.15 = (bf16[4,16,512]{2,1,0:T(8,128)(2,1)S(1)}, bf16[4,16,512]{2,1,0:T(8,128)(2,1)S(1)}, u32[]{:S(2)}, u32[]{:S(2)}) collective-permute-start(bf16[4,16,512]{2,1,0:T(8,128)(2,1)S(1)} %get-tuple-element.18), channel_id=1, source_target_pairs={{0,8},{8,16},{16,24},{24,0},{1,9},{9,17},{17,25},{25,1},{2,10},{10... | collective-permute-start | bytes 196616 | tf_op jit(solution)/shard_map/ppermute | solution.py:35
  146.2 7.9 %collective-permute-start.16 = (bf16[4,16,512]{2,1,0:T(8,128)(2,1)S(1)}, bf16[4,16,512]{2,1,0:T(8,128)(2,1)S(1)}, u32[]{:S(2)}, u32[]{:S(2)}) collective-permute-start(bf16[4,16,512]{2,1,0:T(8,128)(2,1)S(1)} %get-tuple-element.18), channel_id=1, source_target_pairs={{0,16},{8,24},{16,0},{24,8},{1,17},{9,25},{17,1},{25,9},{2,18},{10... | collective-permute-start | bytes 196616 | tf_op jit(solution)/shard_map/ppermute | solution.py:35
  147.7 34.4 %all-to-all-start.3 = ((bf16[8,4,16,512]{3,2,1,0:T(8,128)(2,1)}), bf16[8,4,16,512]{3,2,1,0:T(8,128)(2,1)S(1)}, u32[]{:S(2)}, u32[]{:S(2)}) async-start(bf16[8,4,16,512]{3,2,1,0:T(8,128)(2,1)} %get-tuple-element.19), calls=%async_computation.3 | async-start | bytes 1048576 | tf_op jit(solution)/shard_map/all_to_all | solution.py:425
  154.1 3.2 %collective-permute-start.17 = (bf16[4,16,512]{2,1,0:T(8,128)(2,1)S(1)}, bf16[4,16,512]{2,1,0:T(8,128)(2,1)S(1)}, u32[]{:S(2)}, u32[]{:S(2)}) collective-permute-start(bf16[4,16,512]{2,1,0:T(8,128)(2,1)S(1)} %get-tuple-element.18), channel_id=1, source_target_pairs={{0,24},{8,0},{16,8},{24,16},{1,25},{9,1},{17,9},{25,17},{2,26},{10... | collective-permute-start | bytes 196616 | tf_op jit(solution)/shard_map/ppermute | solution.py:35
  157.3 28.5 %collective-permute-start.9 = (bf16[256,2048]{1,0:T(8,128)(2,1)}, bf16[256,2048]{1,0:T(8,128)(2,1)}, u32[]{:S(2)}, u32[]{:S(2)}) collective-permute-start(bf16[256,2048]{1,0:T(8,128)(2,1)} %collective-permute-done.2.refs_3_), channel_id=1, source_target_pairs={{0,1},{1,0},{2,3},{3,2},{4,5},{5,4},{6,7},{7,6},{8,9},{9,8},{10,11... | collective-permute-start | bytes 3145736 | tf_op jit(solution)/shard_map/ppermute | solution.py:35
  161.1 70.7 %copy-start.7 = (f32[22]{0:T(128)S(1)}, f32[22]{0:T(128)}, u32[]{:S(2)}) copy-start(f32[22]{0:T(128)} %param.29) | copy-start | bytes 268
  161.1 70.7 %copy-start.8 = (f32[22]{0:T(128)S(1)}, f32[22]{0:T(128)}, u32[]{:S(2)}) copy-start(f32[22]{0:T(128)} %param.28) | copy-start | bytes 268
  161.1 13.1 %collective-permute-start.18 = (bf16[4,4,16,512]{3,2,1,0:T(8,128)(2,1)S(1)}, bf16[4,4,16,512]{3,2,1,0:T(8,128)(2,1)S(1)}, u32[]{:S(2)}, u32[]{:S(2)}) collective-permute-start(bf16[4,4,16,512]{3,2,1,0:T(8,128)(2,1)S(1)} %pad_maximum_fusion.refs_14_), channel_id=1, source_target_pairs={{0,32},{32,64},{64,96},{96,128},{128,160},{160,192},{192,224},{224... | collective-permute-start | bytes 786440 | tf_op jit(solution)/shard_map/ppermute | solution.py:35
  162.8 11.4 %collective-permute-start.22 = (bf16[4,4,16,512]{3,2,1,0:T(8,128)(2,1)S(1)}, bf16[4,4,16,512]{3,2,1,0:T(8,128)(2,1)S(1)}, u32[]{:S(2)}, u32[]{:S(2)}) collective-permute-start(bf16[4,4,16,512]{3,2,1,0:T(8,128)(2,1)S(1)} %pad_maximum_fusion.refs_14_), channel_id=1, source_target_pairs={{0,224},{32,0},{64,32},{96,64},{128,96},{160,128},{192,160},{224,1... | collective-permute-start | bytes 786440 | tf_op jit(solution)/shard_map/ppermute | solution.py:35
  174.2 7.9 %collective-permute-start.19 = (bf16[4,4,16,512]{3,2,1,0:T(8,128)(2,1)S(1)}, bf16[4,4,16,512]{3,2,1,0:T(8,128)(2,1)}, u32[]{:S(2)}, u32[]{:S(2)}) collective-permute-start(bf16[4,4,16,512]{3,2,1,0:T(8,128)(2,1)S(1)} %collective-permute-done.18.refs_15_), channel_id=1, source_target_pairs={{0,32},{32,64},{64,96},{96,128},{128,160},{160,192},{192,224},{224... | collective-permute-start | bytes 786440 | tf_op jit(solution)/shard_map/ppermute | solution.py:35
  174.2 8.3 %collective-permute-start.23 = (bf16[4,4,16,512]{3,2,1,0:T(8,128)(2,1)S(1)}, bf16[4,4,16,512]{3,2,1,0:T(8,128)(2,1)}, u32[]{:S(2)}, u32[]{:S(2)}) collective-permute-start(bf16[4,4,16,512]{3,2,1,0:T(8,128)(2,1)S(1)} %collective-permute-done.22.refs_21_), channel_id=1, source_target_pairs={{0,224},{32,0},{64,32},{96,64},{128,96},{160,128},{192,160},{224,1... | collective-permute-start | bytes 786440 | tf_op jit(solution)/shard_map/ppermute | solution.py:35
  182.1 7.3 %collective-permute-start.20 = (bf16[4,4,16,512]{3,2,1,0:T(8,128)(2,1)}, bf16[4,4,16,512]{3,2,1,0:T(8,128)(2,1)}, u32[]{:S(2)}, u32[]{:S(2)}) collective-permute-start(bf16[4,4,16,512]{3,2,1,0:T(8,128)(2,1)} %collective-permute-done.19.refs_16_), channel_id=1, source_target_pairs={{0,32},{32,64},{64,96},{96,128},{128,160},{160,192},{192,224},{224... | collective-permute-start | bytes 786440 | tf_op jit(solution)/shard_map/ppermute | solution.py:35
  182.2 14.2 %collective-permute-start.25 = (bf16[8,4,16,512]{3,2,1,0:T(8,128)(2,1)S(1)}, bf16[8,4,16,512]{3,2,1,0:T(8,128)(2,1)S(1)}, u32[]{:S(2)}, u32[]{:S(2)}) collective-permute-start(bf16[8,4,16,512]{3,2,1,0:T(8,128)(2,1)S(1)} %all-to-all-done.3.refs_22_), channel_id=1, source_target_pairs={{0,8},{8,16},{16,24},{24,0},{1,9},{9,17},{17,25},{25,1},{2,10},{10... | collective-permute-start | bytes 1572872 | tf_op jit(solution)/shard_map/ppermute | solution.py:35
  182.5 24.1 %collective-permute-start.26 = (bf16[8,4,16,512]{3,2,1,0:T(8,128)(2,1)S(1)}, bf16[8,4,16,512]{3,2,1,0:T(8,128)(2,1)S(1)}, u32[]{:S(2)}, u32[]{:S(2)}) collective-permute-start(bf16[8,4,16,512]{3,2,1,0:T(8,128)(2,1)S(1)} %all-to-all-done.3.refs_22_), channel_id=1, source_target_pairs={{0,16},{8,24},{16,0},{24,8},{1,17},{9,25},{17,1},{25,9},{2,18},{10... | collective-permute-start | bytes 1572872 | tf_op jit(solution)/shard_map/ppermute | solution.py:35
  185.1 23.0 %collective-permute-start.27 = (bf16[8,4,16,512]{3,2,1,0:T(8,128)(2,1)S(1)}, bf16[8,4,16,512]{3,2,1,0:T(8,128)(2,1)S(1)}, u32[]{:S(2)}, u32[]{:S(2)}) collective-permute-start(bf16[8,4,16,512]{3,2,1,0:T(8,128)(2,1)S(1)} %all-to-all-done.3.refs_22_), channel_id=1, source_target_pairs={{0,24},{8,0},{16,8},{24,16},{1,25},{9,1},{17,9},{25,17},{2,26},{10... | collective-permute-start | bytes 1572872 | tf_op jit(solution)/shard_map/ppermute | solution.py:35
  185.8 6.2 %collective-permute-start.24 = (bf16[4,4,16,512]{3,2,1,0:T(8,128)(2,1)}, bf16[4,4,16,512]{3,2,1,0:T(8,128)(2,1)S(1)}, u32[]{:S(2)}, u32[]{:S(2)}) collective-permute-start(bf16[4,4,16,512]{3,2,1,0:T(8,128)(2,1)} %collective-permute-done.23.refs_20_), channel_id=1, source_target_pairs={{0,224},{32,0},{64,32},{96,64},{128,96},{160,128},{192,160},{224,1... | collective-permute-start | bytes 786440 | tf_op jit(solution)/shard_map/ppermute | solution.py:35
  189.4 6.9 %collective-permute-start.21 = (bf16[4,4,16,512]{3,2,1,0:T(8,128)(2,1)}, bf16[4,4,16,512]{3,2,1,0:T(8,128)(2,1)S(1)}, u32[]{:S(2)}, u32[]{:S(2)}) collective-permute-start(bf16[4,4,16,512]{3,2,1,0:T(8,128)(2,1)} %collective-permute-done.20.refs_17_), channel_id=1, source_target_pairs={{0,32},{32,64},{64,96},{96,128},{128,160},{160,192},{192,224},{224... | collective-permute-start | bytes 786440 | tf_op jit(solution)/shard_map/ppermute | solution.py:35
  222.8 18.3 %all-to-all-start.4 = ((f32[32,8,128]{2,1,0:T(8,128)}), f32[32,8,128]{2,1,0:T(8,128)S(1)}, u32[]{:S(2)}, u32[]{:S(2)}) async-start(f32[32,8,128]{2,1,0:T(8,128)} %logits.1), calls=%async_computation.4 | async-start | bytes 262144 | tf_op jit(solution)/shard_map/all_to_all | solution.py:439
  241.9 10.1 %all-to-all-start.5 = ((f32[8,8,128]{2,1,0:T(8,128)}), f32[8,8,128]{2,1,0:T(8,128)S(1)}, u32[]{:S(2)}, u32[]{:S(2)}) async-start(f32[8,8,128]{2,1,0:T(8,128)} %get-tuple-element.22), calls=%async_computation.5 | async-start | bytes 65536 | tf_op jit(solution)/shard_map/all_to_all | solution.py:444

commit v5 on v4

--- a/solution.py
+++ b/solution.py
@@ -35,14 +35,15 @@
     return lax.ppermute(array, axis, [(i, (i + by) % n) for i in range(n)])
 
 
-def call(kernel, out_shape, args, scalars=None, scratch=(), flops=0, vmem=4):
+def call(kernel, out_shape, args, scalars=None, scratch=(), flops=0, vmem=4, far=0):
     spec = pl.BlockSpec(memory_space=pltpu.VMEM)
     many = isinstance(out_shape, (list, tuple))
     return pl.pallas_call(
         kernel,
         out_shape=out_shape,
         in_specs=([pl.BlockSpec(memory_space=pltpu.SMEM)] if scalars is not None else [])
-        + [spec] * len(args),
+        + [spec] * (len(args) - far)
+        + [pl.BlockSpec(memory_space=pltpu.HBM)] * far,
         out_specs=[spec] * len(out_shape) if many else spec,
         scratch_shapes=scratch,
         compiler_params=pltpu.CompilerParams(vmem_limit_bytes=vmem << 20),
@@ -89,8 +90,16 @@
 
 
 def attention_kernel(
-    at_ref, same, other, gain, wq, wk, wv, wo, cos, sin, keep_ref, send_ref, resid_ref, mixed_ref
+    at_ref, same, other, gain, cos, sin, *refs
 ):
+    weights, (keep_ref, send_ref, resid_ref) = refs[:4], refs[4:7]
+    mixed_ref, (wq, wk, wv, wo), sems = refs[7], refs[8:12], refs[12]
+    copies = [
+        pltpu.make_async_copy(ref, to, sems.at[k])
+        for k, (ref, to) in enumerate(zip(weights, (wq, wk, wv, wo)))
+    ]
+    for copy in copies:
+        copy.start()
     x, c = at_ref[0], at_ref[1]
     m = x * 2 + c
     blocks = [same.at[t] for t in range(4)] + [other.at[t] for t in range(4)]
@@ -108,6 +117,8 @@
             squares = squares + v * v
     inv_rms = lax.rsqrt(jnp.sum(squares, axis=1, keepdims=True) * (1.0 / 4096.0) + norm_eps)
 
+    for copy in copies[:3]:
+        copy.wait()
     query = jnp.zeros((128, 256), f32)
     key = jnp.zeros((128, 128), f32)
     value = jnp.zeros((128, 128), f32)
@@ -153,6 +164,7 @@
         [mixed_ref[t * 2 + c] for t in range(4)] + [mixed_ref[t * 2 + 1 - c] for t in range(4)],
         axis=0,
     )
+    copies[3].wait()
     for fb in range(8):
         part = jnp.dot(left, wo[:, fb * 512 : fb * 512 + 512], preferred_element_type=f32)
         part = part.astype(bf16).reshape(8, 16, 512)
@@ -378,13 +390,16 @@
         attention_kernel,
         [sds((4, 8, 16, 512), bf16), sds((4, 8, 16, 512), bf16), sds((8, 16, 512), bf16)],
         (
-            same, other, gain_in.reshape(8, 1, 512), w_query, w_key, w_value, w_out,
-            jnp.asarray(cosine), jnp.asarray(sine),
+            same, other, gain_in.reshape(8, 1, 512), jnp.asarray(cosine), jnp.asarray(sine),
+            w_query, w_key, w_value, w_out,
         ),
         at,
-        scratch=[pltpu.VMEM((8, 16, 256), bf16)],
+        scratch=[pltpu.VMEM((8, 16, 256), bf16)]
+        + [pltpu.VMEM(w.shape, bf16) for w in (w_query, w_key, w_value, w_out)]
+        + [pltpu.SemaphoreType.DMA((4,))],
         flops=1 << 30,
-        vmem=60,
+        vmem=48,
+        far=4,
     )
     got_part = shift(send, "c", 1)
     pair = (keep.astype(f32) + got_part.astype(f32)).astype(bf16)

time: 253 us -> 252 us (level)
  transfers between devices with their start and end apart: 34 -> 34, of which waited for: 16 -> 16; matrix products, arithmetic and copies ran while one was open for 3% -> 3% of each run, Pallas kernels for 4% -> 3%
where the time goes in v5:
time: 252 us
  waiting for transfers between devices  113 us (45%)
  starting transfers between devices  75.2 us (30%)
  blocking collectives  28.9 us (11%)
  Pallas kernels  25 us (10%)
  local copies, waits for them, and re-layouts  6.91 us (3%)
    ppermute x28, waiting for transfers between devices, shift(): return lax.ppermute(array, axis, [(i, (i + by) % n) for i in range(n)])  77.9 us
    ppermute x28, starting transfers between devices, shift(): return lax.ppermute(array, axis, [(i, (i + by) % n) for i in range(n)])  34.3 us
    all_gather x1, blocking collectives, program(): same = lax.all_gather(block, 'x', axis=0, tiled=False)  28.9 us
    pallas_call x1, Pallas kernels, logits_call(): pl.pallas_call(logits_kernel, out_shape=sds((32, 8, 128), f32), in_specs=...  14.8 us
    all_to_all x1, starting transfers between devices, program(): got = lax.all_to_all(packed, DP, 0, 0, tiled=True)  12 us
    pallas_call x6, Pallas kernels, call(): pl.pallas_call(kernel, out_shape=out_shape, in_specs=([pl.BlockSpec(memor...  10.3 us
    all_to_all x1, waiting for transfers between devices, program(): sums = lax.all_to_all(pair, 'x', 0, 0, tiled=True)  8.96 us
    all_to_all x1, starting transfers between devices, program(): merged = lax.all_to_all(pieces, DP, 0, 0, tiled=True)  8.92 us
  transfers between devices with their start and end apart: 34, of which 16 were waited for; matrix products, arithmetic and copies ran while one was open for 3% of the time, Pallas kernels for 3%

profile of v5, /device:TPU:1, one launch (start us, length us, event | category | flops | bytes accessed | tf_op | source)
XLA Modules:
  0.0 251.9 jit_solution(10195950933951947621)
XLA Ops:
  0.6 1.8 shard_map.175
  2.4 12.0 %all-to-all-start = ((bf16[32,5,8,128]{3,2,1,0:T(8,128)(2,1)}), bf16[32,5,8,128]{3,2,1,0:T(8,128)(2,1)S(1)}, u32[]{:S(2)}, u32[]{:S(2)}) async-start(bf16[32,5,8,128]{3,2,1,0:T(8,128)(2,1)} %shard_map.175), calls=%async_computation | async-start | bytes 655360 | tf_op jit(solution)/shard_map/all_to_all | solution.py:373
  14.5 3.3 %fusion.10 = (bf16[256,2048]{1,0:T(8,128)(2,1)}, bf16[256,2048]{1,0:T(8,128)(2,1)}) fusion(bf16[512,2048]{1,0:T(8,128)(2,1)} %refs_0_.3), kind=kLoop, calls=%fused_computation.33 | loop fusion | bytes 4194304 | tf_op jit(solution)/shard_map/slice | solution.py:408
  17.8 2.5 collective-permute-start.3
  20.5 6.6 %all-to-all-done = bf16[32,5,8,128]{3,2,1,0:T(8,128)(2,1)S(1)} async-done(((bf16[32,5,8,128]{3,2,1,0:T(8,128)(2,1)}), bf16[32,5,8,128]{3,2,1,0:T(8,128)(2,1)S(1)}, u32[]{:S(2)}, u32[]{:S(2)}) %all-to-all-start) | async-done | bytes 327712 | tf_op jit(solution)/shard_map/all_to_all | solution.py:373
  27.6 1.3 shard_map.176
  28.9 4.8 %all-to-all-start.1 = ((bf16[32,16,128]{2,1,0:T(8,128)(2,1)}), bf16[32,16,128]{2,1,0:T(8,128)(2,1)S(1)}, u32[]{:S(2)}, u32[]{:S(2)}) async-start(bf16[32,16,128]{2,1,0:T(8,128)(2,1)} %bitcast.8), calls=%async_computation.1 | async-start | bytes 262144 | tf_op jit(solution)/shard_map/all_to_all | solution.py:383
  33.7 2.6 %collective-permute-start.5 = (bf16[256,2048]{1,0:T(8,128)(2,1)}, bf16[256,2048]{1,0:T(8,128)(2,1)}, u32[]{:S(2)}, u32[]{:S(2)}) collective-permute-start(bf16[256,2048]{1,0:T(8,128)(2,1)} %get-tuple-element.30), channel_id=1, source_target_pairs={{0,6},{2,0},{4,2},{6,4},{1,7},{3,1},{5,3},{7,5},{8,14},{10,8},{12,... | collective-permute-start | bytes 3145736 | tf_op jit(solution)/shard_map/ppermute | solution.py:35
  36.3 6.8 %all-to-all-done.1 = bf16[32,16,128]{2,1,0:T(8,128)(2,1)S(1)} async-done(((bf16[32,16,128]{2,1,0:T(8,128)(2,1)}), bf16[32,16,128]{2,1,0:T(8,128)(2,1)S(1)}, u32[]{:S(2)}, u32[]{:S(2)}) %all-to-all-start.1) | async-done | bytes 131104 | tf_op jit(solution)/shard_map/all_to_all | solution.py:383
  43.1 28.9 %all-gather = bf16[128,16,128]{2,1,0:T(8,128)(2,1)S(1)} all-gather(bf16[32,16,128]{2,1,0:T(8,128)(2,1)S(1)} %all-to-all-done.1), channel_id=2, replica_groups=mesh['z'=8,'y'=4,'x'=4,'c'=2] {'x'}, dimensions={0}, use_global_device_ids=true | all-gather | bytes 655360 | tf_op jit(solution)/shard_map/all_gather | solution.py:385
  72.0 3.3 %collective-permute-start.13 = (bf16[4,32,16,128]{3,2,1,0:T(8,128)(2,1)S(1)}, bf16[4,32,16,128]{3,2,1,0:T(8,128)(2,1)S(1)}, u32[]{:S(2)}, u32[]{:S(2)}) collective-permute-start(bf16[4,32,16,128]{3,2,1,0:T(8,128)(2,1)S(1)} %bitcast.28), channel_id=1, source_target_pairs={{0,1},{1,0},{2,3},{3,2},{4,5},{5,4},{6,7},{7,6},{8,9},{9,8},{10,11... | collective-permute-start | bytes 1572872 | tf_op jit(solution)/shard_map/ppermute | solution.py:35
  75.3 2.0 collective-permute-start.1
  77.3 1.2 collective-permute-start.4
  78.9 0.8 copy-done.2
  79.8 1.0 copy-done.3
  80.8 4.1 %shard_map.177 = (bf16[4,8,16,512]{3,2,1,0:T(8,128)(2,1)S(1)}, bf16[4,8,16,512]{3,2,1,0:T(8,128)(2,1)S(1)}, bf16[8,16,512]{2,1,0:T(8,128)(2,1)S(1)}) custom-call(s32[4]{0:T(128)S(1)} %pad_add_fusion.at_ref, bf16[4,32,16,128]{3,2,1,0:T(8,128)(2,1)S(1)} %bitcast.29, bf16[4,32,16,128]{3,2,1,0:T(8,128)(2,1)S(1)} %copy-done.3, f32[8,1,512]{2,1,0:T(1,128)S(1)} %bitcast.32, ...), custom_call_target="tpu_custom_call" | custom-call | flops 1073741824 | tf_op jit(solution)/shard_map/pallas_call | solution.py:41
  84.9 0.9 collective-permute-start.14
  86.0 16.4 %collective-permute-done.1.refs_2_ = bf16[256,2048]{1,0:T(8,128)(2,1)} collective-permute-done((bf16[256,2048]{1,0:T(8,128)(2,1)}, bf16[256,2048]{1,0:T(8,128)(2,1)}, u32[]{:S(2)}, u32[]{:S(2)}) %collective-permute-start.1) | collective-permute-done | bytes 1048608 | tf_op jit(solution)/shard_map/ppermute | solution.py:35
  103.8 21.1 %collective-permute-done.2.refs_3_ = bf16[256,2048]{1,0:T(8,128)(2,1)} collective-permute-done((bf16[256,2048]{1,0:T(8,128)(2,1)}, bf16[256,2048]{1,0:T(8,128)(2,1)}, u32[]{:S(2)}, u32[]{:S(2)}) %collective-permute-start.2) | collective-permute-done | bytes 1048608 | tf_op jit(solution)/shard_map/ppermute | solution.py:35
  125.4 1.0 add_convert_fusion
  126.4 3.5 %all-to-all-start.2 = ((bf16[4,8,16,512]{3,2,1,0:T(8,128)(2,1)}), bf16[4,8,16,512]{3,2,1,0:T(8,128)(2,1)S(1)}, u32[]{:S(2)}, u32[]{:S(2)}) async-start(bf16[4,8,16,512]{3,2,1,0:T(8,128)(2,1)} %add_convert_fusion), calls=%async_computation.2 | async-start | bytes 1048576 | tf_op jit(solution)/shard_map/all_to_all | solution.py:406
  130.5 9.0 %all-to-all-done.2.sums = bf16[4,8,16,512]{3,2,1,0:T(8,128)(2,1)S(1)} async-done(((bf16[4,8,16,512]{3,2,1,0:T(8,128)(2,1)}), bf16[4,8,16,512]{3,2,1,0:T(8,128)(2,1)S(1)}, u32[]{:S(2)}, u32[]{:S(2)}) %all-to-all-start.2) | async-done | bytes 524320 | tf_op jit(solution)/shard_map/all_to_all | solution.py:406
  139.5 1.6 shard_map.178
  141.0 1.2 collective-permute-start.15
  142.3 3.1 %collective-permute-done.15 = bf16[4,16,512]{2,1,0:T(8,128)(2,1)S(1)} collective-permute-done((bf16[4,16,512]{2,1,0:T(8,128)(2,1)S(1)}, bf16[4,16,512]{2,1,0:T(8,128)(2,1)S(1)}, u32[]{:S(2)}, u32[]{:S(2)}) %collective-permute-start.15) | collective-permute-done | bytes 65568 | tf_op jit(solution)/shard_map/ppermute | solution.py:35
  145.4 1.5 collective-permute-start.16
  146.9 6.4 %all-to-all-start.3 = ((bf16[8,4,16,512]{3,2,1,0:T(8,128)(2,1)}), bf16[8,4,16,512]{3,2,1,0:T(8,128)(2,1)S(1)}, u32[]{:S(2)}, u32[]{:S(2)}) async-start(bf16[8,4,16,512]{3,2,1,0:T(8,128)(2,1)} %get-tuple-element.19), calls=%async_computation.3 | async-start | bytes 1048576 | tf_op jit(solution)/shard_map/all_to_all | solution.py:440
  153.3 1.0 collective-permute-start.17
  154.2 2.2 collective-permute-done.17
  156.5 3.7 %collective-permute-start.9 = (bf16[256,2048]{1,0:T(8,128)(2,1)}, bf16[256,2048]{1,0:T(8,128)(2,1)}, u32[]{:S(2)}, u32[]{:S(2)}) collective-permute-start(bf16[256,2048]{1,0:T(8,128)(2,1)} %collective-permute-done.2.refs_3_), channel_id=1, source_target_pairs={{0,1},{1,0},{2,3},{3,2},{4,5},{5,4},{6,7},{7,6},{8,9},{9,8},{10,11... | collective-permute-start | bytes 3145736 | tf_op jit(solution)/shard_map/ppermute | solution.py:35
  160.3 1.7 collective-permute-start.18
  162.0 1.3 collective-permute-start.22
  163.3 10.1 %collective-permute-done.18.refs_15_ = bf16[4,4,16,512]{3,2,1,0:T(8,128)(2,1)S(1)} collective-permute-done((bf16[4,4,16,512]{3,2,1,0:T(8,128)(2,1)S(1)}, bf16[4,4,16,512]{3,2,1,0:T(8,128)(2,1)S(1)}, u32[]{:S(2)}, u32[]{:S(2)}) %collective-permute-start.18) | collective-permute-done | bytes 262176 | tf_op jit(solution)/shard_map/ppermute | solution.py:35
  173.4 2.7 %collective-permute-start.23 = (bf16[4,4,16,512]{3,2,1,0:T(8,128)(2,1)}, bf16[4,4,16,512]{3,2,1,0:T(8,128)(2,1)}, u32[]{:S(2)}, u32[]{:S(2)}) collective-permute-start(bf16[4,4,16,512]{3,2,1,0:T(8,128)(2,1)} %collective-permute-done.22.refs_21_), channel_id=1, source_target_pairs={{0,224},{32,0},{64,32},{96,64},{128,96},{160,128},{192,160},{224,1... | collective-permute-start | bytes 786440 | tf_op jit(solution)/shard_map/ppermute | solution.py:35
  176.1 5.2 %collective-permute-done.19.refs_16_ = bf16[4,4,16,512]{3,2,1,0:T(8,128)(2,1)} collective-permute-done((bf16[4,4,16,512]{3,2,1,0:T(8,128)(2,1)S(1)}, bf16[4,4,16,512]{3,2,1,0:T(8,128)(2,1)}, u32[]{:S(2)}, u32[]{:S(2)}) %collective-permute-start.19) | collective-permute-done | bytes 262176 | tf_op jit(solution)/shard_map/ppermute | solution.py:35
  181.7 2.6 %collective-permute-start.26 = (bf16[8,4,16,512]{3,2,1,0:T(8,128)(2,1)S(1)}, bf16[8,4,16,512]{3,2,1,0:T(8,128)(2,1)S(1)}, u32[]{:S(2)}, u32[]{:S(2)}) collective-permute-start(bf16[8,4,16,512]{3,2,1,0:T(8,128)(2,1)S(1)} %all-to-all-done.3.refs_22_), channel_id=1, source_target_pairs={{0,16},{8,24},{16,0},{24,8},{1,17},{9,25},{17,1},{25,9},{2,18},{10... | collective-permute-start | bytes 1572872 | tf_op jit(solution)/shard_map/ppermute | solution.py:35
  185.0 2.6 %collective-permute-start.24 = (bf16[4,4,16,512]{3,2,1,0:T(8,128)(2,1)}, bf16[4,4,16,512]{3,2,1,0:T(8,128)(2,1)S(1)}, u32[]{:S(2)}, u32[]{:S(2)}) collective-permute-start(bf16[4,4,16,512]{3,2,1,0:T(8,128)(2,1)} %collective-permute-done.23.refs_20_), channel_id=1, source_target_pairs={{0,224},{32,0},{64,32},{96,64},{128,96},{160,128},{192,160},{224,1... | collective-permute-start | bytes 786440 | tf_op jit(solution)/shard_map/ppermute | solution.py:35
  187.6 1.0 collective-permute-done.20.refs_17_
  188.6 2.6 %collective-permute-done.24.refs_19_ = bf16[4,4,16,512]{3,2,1,0:T(8,128)(2,1)S(1)} collective-permute-done((bf16[4,4,16,512]{3,2,1,0:T(8,128)(2,1)}, bf16[4,4,16,512]{3,2,1,0:T(8,128)(2,1)S(1)}, u32[]{:S(2)}, u32[]{:S(2)}) %collective-permute-start.24) | collective-permute-done | bytes 262176 | tf_op jit(solution)/shard_map/ppermute | solution.py:35
  191.2 4.3 %collective-permute-done.21.refs_18_ = bf16[4,4,16,512]{3,2,1,0:T(8,128)(2,1)S(1)} collective-permute-done((bf16[4,4,16,512]{3,2,1,0:T(8,128)(2,1)}, bf16[4,4,16,512]{3,2,1,0:T(8,128)(2,1)S(1)}, u32[]{:S(2)}, u32[]{:S(2)}) %collective-permute-start.21) | collective-permute-done | bytes 262176 | tf_op jit(solution)/shard_map/ppermute | solution.py:35
  195.5 10.3 %collective-permute-done.26.refs_24_ = bf16[8,4,16,512]{3,2,1,0:T(8,128)(2,1)S(1)} collective-permute-done((bf16[8,4,16,512]{3,2,1,0:T(8,128)(2,1)S(1)}, bf16[8,4,16,512]{3,2,1,0:T(8,128)(2,1)S(1)}, u32[]{:S(2)}, u32[]{:S(2)}) %collective-permute-start.26) | collective-permute-done | bytes 524320 | tf_op jit(solution)/shard_map/ppermute | solution.py:35
  205.8 1.4 collective-permute-done.27.refs_25_
  207.2 14.8 %logits.1 = f32[32,8,128]{2,1,0:T(8,128)} custom-call(s32[4]{0:T(128)S(1)} %pad_add_fusion.at_ref, bf16[512,2048]{1,0:T(8,128)(2,1)} %refs_0_.3, bf16[256,2048]{1,0:T(8,128)(2,1)} %collective-permute-done.refs_1_, bf16[256,2048]{1,0:T(8,128)(2,1)} %collective-permute-done.1.refs_2_, bf16[256,2048]{1,0:T(8,128)(2,1)} %collective-permute-done.2.refs_3_, ...), custom_call_target="tpu_custom_call" | custom-call | flops 8589934592 | bytes 20971520 | tf_op jit(solution)/shard_map/logits/pallas_call | solution.py:297
  222.0 8.9 %all-to-all-start.4 = ((f32[32,8,128]{2,1,0:T(8,128)}), f32[32,8,128]{2,1,0:T(8,128)S(1)}, u32[]{:S(2)}, u32[]{:S(2)}) async-start(f32[32,8,128]{2,1,0:T(8,128)} %logits.1), calls=%async_computation.4 | async-start | bytes 262144 | tf_op jit(solution)/shard_map/all_to_all | solution.py:454
  231.7 8.7 %all-to-all-done.4.got_ref = f32[32,8,128]{2,1,0:T(8,128)S(1)} async-done(((f32[32,8,128]{2,1,0:T(8,128)}), f32[32,8,128]{2,1,0:T(8,128)S(1)}, u32[]{:S(2)}, u32[]{:S(2)}) %all-to-all-start.4) | async-done | bytes 131104 | tf_op jit(solution)/shard_map/all_to_all | solution.py:454
  240.3 0.8 shard_map.179
  241.1 5.3 %all-to-all-start.5 = ((f32[8,8,128]{2,1,0:T(8,128)}), f32[8,8,128]{2,1,0:T(8,128)S(1)}, u32[]{:S(2)}, u32[]{:S(2)}) async-start(f32[8,8,128]{2,1,0:T(8,128)} %get-tuple-element.22), calls=%async_computation.5 | async-start | bytes 65536 | tf_op jit(solution)/shard_map/all_to_all | solution.py:459
  247.0 4.2 %all-to-all-done.5.sums_ref = f32[8,8,128]{2,1,0:T(8,128)S(1)} async-done(((f32[8,8,128]{2,1,0:T(8,128)}), f32[8,8,128]{2,1,0:T(8,128)S(1)}, u32[]{:S(2)}, u32[]{:S(2)}) %all-to-all-start.5) | async-done | bytes 32800 | tf_op jit(solution)/shard_map/all_to_all | solution.py:459
  (81 shorter events, 6.7 us)
Async XLA Ops:
  2.4 24.7 %all-to-all-start = ((bf16[32,5,8,128]{3,2,1,0:T(8,128)(2,1)}), bf16[32,5,8,128]{3,2,1,0:T(8,128)(2,1)S(1)}, u32[]{:S(2)}, u32[]{:S(2)}) async-start(bf16[32,5,8,128]{3,2,1,0:T(8,128)(2,1)} %shard_map.175), calls=%async_computation | async-start | bytes 655360 | tf_op jit(solution)/shard_map/all_to_all | solution.py:373
  14.5 5.9 %copy-start.9 = (s32[32]{0:T(128)S(1)}, s32[32]{0:T(128)}, u32[]{:S(2)}) copy-start(s32[32]{0:T(128)} %param.19) | copy-start | bytes 388
  14.5 65.3 %copy-start = (bf16[4096,128]{1,0:T(8,128)(2,1)S(1)}, bf16[4096,128]{1,0:T(8,128)(2,1)}, u32[]{:S(2)}) copy-start(bf16[4096,128]{1,0:T(8,128)(2,1)} %refs_1_.1) | copy-start | bytes 3145732
  14.5 65.2 %copy-start.1 = (bf16[4096,128]{1,0:T(8,128)(2,1)S(1)}, bf16[4096,128]{1,0:T(8,128)(2,1)}, u32[]{:S(2)}) copy-start(bf16[4096,128]{1,0:T(8,128)(2,1)} %refs_2_.1) | copy-start | bytes 3145732
  14.5 65.2 %copy-start.4 = (f32[128,128]{1,0:T(8,128)S(1)}, f32[128,128]{1,0:T(8,128)}, u32[]{:S(2)}) copy-start(f32[128,128]{1,0:T(8,128)} %constant.95.clone.cos) | copy-start | bytes 196612
  14.5 65.2 %copy-start.5 = (f32[128,128]{1,0:T(8,128)S(1)}, f32[128,128]{1,0:T(8,128)}, u32[]{:S(2)}) copy-start(f32[128,128]{1,0:T(8,128)} %constant.96.clone.sin) | copy-start | bytes 196612
  14.5 65.2 %copy-start.6 = (f32[4096]{0:T(1024)S(1)}, f32[4096]{0:T(1024)}, u32[]{:S(2)}) copy-start(f32[4096]{0:T(1024)} %param.21) | copy-start | bytes 49156
  17.8 59.5 %collective-permute-start.3 = (bf16[256,2048]{1,0:T(8,128)(2,1)}, bf16[256,2048]{1,0:T(8,128)(2,1)}, u32[]{:S(2)}, u32[]{:S(2)}) collective-permute-start(bf16[256,2048]{1,0:T(8,128)(2,1)} %get-tuple-element.29), channel_id=1, source_target_pairs={{0,6},{2,0},{4,2},{6,4},{1,7},{3,1},{5,3},{7,5},{8,14},{10,8},{12,... | collective-permute-start | bytes 3145736 | tf_op jit(solution)/shard_map/ppermute | solution.py:35
  20.3 58.2 %collective-permute-start = (bf16[256,2048]{1,0:T(8,128)(2,1)}, bf16[256,2048]{1,0:T(8,128)(2,1)}, u32[]{:S(2)}, u32[]{:S(2)}) collective-permute-start(bf16[256,2048]{1,0:T(8,128)(2,1)} %get-tuple-element.30), channel_id=1, source_target_pairs={{0,2},{2,4},{4,6},{6,0},{1,3},{3,5},{5,7},{7,1},{8,10},{10,12},{12... | collective-permute-start | bytes 3145736 | tf_op jit(solution)/shard_map/ppermute | solution.py:35
  27.2 76.0 %copy-start.8 = (bf16[32,8,128]{2,1,0:T(8,128)(2,1)}, bf16[32,8,128]{2,1,0:T(8,128)(2,1)S(1)}, u32[]{:S(2)}) copy-start(bf16[32,8,128]{2,1,0:T(8,128)(2,1)S(1)} %slice_bitcast_fusion) | copy-start | bytes 196612
  28.9 14.2 %all-to-all-start.1 = ((bf16[32,16,128]{2,1,0:T(8,128)(2,1)}), bf16[32,16,128]{2,1,0:T(8,128)(2,1)S(1)}, u32[]{:S(2)}, u32[]{:S(2)}) async-start(bf16[32,16,128]{2,1,0:T(8,128)(2,1)} %bitcast.8), calls=%async_computation.1 | async-start | bytes 262144 | tf_op jit(solution)/shard_map/all_to_all | solution.py:383
  33.7 52.2 %collective-permute-start.5 = (bf16[256,2048]{1,0:T(8,128)(2,1)}, bf16[256,2048]{1,0:T(8,128)(2,1)}, u32[]{:S(2)}, u32[]{:S(2)}) collective-permute-start(bf16[256,2048]{1,0:T(8,128)(2,1)} %get-tuple-element.30), channel_id=1, source_target_pairs={{0,6},{2,0},{4,2},{6,4},{1,7},{3,1},{5,3},{7,5},{8,14},{10,8},{12,... | collective-permute-start | bytes 3145736 | tf_op jit(solution)/shard_map/ppermute | solution.py:35
  72.0 6.9 %collective-permute-start.13 = (bf16[4,32,16,128]{3,2,1,0:T(8,128)(2,1)S(1)}, bf16[4,32,16,128]{3,2,1,0:T(8,128)(2,1)S(1)}, u32[]{:S(2)}, u32[]{:S(2)}) collective-permute-start(bf16[4,32,16,128]{3,2,1,0:T(8,128)(2,1)S(1)} %bitcast.28), channel_id=1, source_target_pairs={{0,1},{1,0},{2,3},{3,2},{4,5},{5,4},{6,7},{7,6},{8,9},{9,8},{10,11... | collective-permute-start | bytes 1572872 | tf_op jit(solution)/shard_map/ppermute | solution.py:35
  75.3 27.1 %collective-permute-start.1 = (bf16[256,2048]{1,0:T(8,128)(2,1)}, bf16[256,2048]{1,0:T(8,128)(2,1)}, u32[]{:S(2)}, u32[]{:S(2)}) collective-permute-start(bf16[256,2048]{1,0:T(8,128)(2,1)} %get-tuple-element.29), channel_id=1, source_target_pairs={{0,2},{2,4},{4,6},{6,0},{1,3},{3,5},{5,7},{7,1},{8,10},{10,12},{12... | collective-permute-start | bytes 3145736 | tf_op jit(solution)/shard_map/ppermute | solution.py:35
  77.3 25.8 %collective-permute-start.4 = (bf16[256,2048]{1,0:T(8,128)(2,1)}, bf16[256,2048]{1,0:T(8,128)(2,1)}, u32[]{:S(2)}, u32[]{:S(2)}) collective-permute-start(bf16[256,2048]{1,0:T(8,128)(2,1)} %collective-permute-done.3.refs_6_), channel_id=1, source_target_pairs={{0,6},{2,0},{4,2},{6,4},{1,7},{3,1},{5,3},{7,5},{8,14},{10,8},{12,... | collective-permute-start | bytes 3145736 | tf_op jit(solution)/shard_map/ppermute | solution.py:35
  78.6 46.3 %collective-permute-start.2 = (bf16[256,2048]{1,0:T(8,128)(2,1)}, bf16[256,2048]{1,0:T(8,128)(2,1)}, u32[]{:S(2)}, u32[]{:S(2)}) collective-permute-start(bf16[256,2048]{1,0:T(8,128)(2,1)} %collective-permute-done.refs_1_), channel_id=1, source_target_pairs={{0,2},{2,4},{4,6},{6,0},{1,3},{3,5},{5,7},{7,1},{8,10},{10,12},{12... | collective-permute-start | bytes 3145736 | tf_op jit(solution)/shard_map/ppermute | solution.py:35
  78.9 0.8 copy-start.2
  79.8 1.0 copy-start.3
  84.9 54.5 %copy-start.7 = (f32[4096]{0:T(1024)S(1)}, f32[4096]{0:T(1024)}, u32[]{:S(2)}) copy-start(f32[4096]{0:T(1024)} %param.26) | copy-start | bytes 49156
  84.9 18.2 %collective-permute-start.14 = (bf16[4,8,16,512]{3,2,1,0:T(8,128)(2,1)S(1)}, bf16[4,8,16,512]{3,2,1,0:T(8,128)(2,1)S(1)}, u32[]{:S(2)}, u32[]{:S(2)}) collective-permute-start(bf16[4,8,16,512]{3,2,1,0:T(8,128)(2,1)S(1)} %get-tuple-element.16), channel_id=1, source_target_pairs={{0,1},{1,0},{2,3},{3,2},{4,5},{5,4},{6,7},{7,6},{8,9},{9,8},{10,11... | collective-permute-start | bytes 1572872 | tf_op jit(solution)/shard_map/ppermute | solution.py:35
  85.9 44.2 %collective-permute-start.12 = (bf16[256,2048]{1,0:T(8,128)(2,1)}, bf16[256,2048]{1,0:T(8,128)(2,1)S(1)}, u32[]{:S(2)}, u32[]{:S(2)}) collective-permute-start(bf16[256,2048]{1,0:T(8,128)(2,1)} %collective-permute-done.3.refs_6_), channel_id=1, source_target_pairs={{0,1},{1,0},{2,3},{3,2},{4,5},{5,4},{6,7},{7,6},{8,9},{9,8},{10,11... | collective-permute-start | bytes 3145736 | tf_op jit(solution)/shard_map/ppermute | solution.py:35
  102.4 78.9 %collective-permute-start.6 = (bf16[512,2048]{1,0:T(8,128)(2,1)}, bf16[512,2048]{1,0:T(8,128)(2,1)}, u32[]{:S(2)}, u32[]{:S(2)}) collective-permute-start(bf16[512,2048]{1,0:T(8,128)(2,1)} %refs_0_.3), channel_id=1, source_target_pairs={{0,1},{1,0},{2,3},{3,2},{4,5},{5,4},{6,7},{7,6},{8,9},{9,8},{10,11... | collective-permute-start | bytes 6291464 | tf_op jit(solution)/shard_map/ppermute | solution.py:35
  103.2 37.9 %collective-permute-start.7 = (bf16[256,2048]{1,0:T(8,128)(2,1)}, bf16[256,2048]{1,0:T(8,128)(2,1)}, u32[]{:S(2)}, u32[]{:S(2)}) collective-permute-start(bf16[256,2048]{1,0:T(8,128)(2,1)} %collective-permute-done.refs_1_), channel_id=1, source_target_pairs={{0,1},{1,0},{2,3},{3,2},{4,5},{5,4},{6,7},{7,6},{8,9},{9,8},{10,11... | collective-permute-start | bytes 3145736 | tf_op jit(solution)/shard_map/ppermute | solution.py:35
  103.2 26.8 %slice-start = ((bf16[32,8,128]{2,1,0:T(8,128)(2,1)}), bf16[32,4,128]{2,1,0:T(4,128)(2,1)S(1)}, s32[]{:S(2)}) async-start(bf16[32,8,128]{2,1,0:T(8,128)(2,1)} %copy-done.8), calls=%async_computation.6 | async-start | bytes 65536 | tf_op jit(solution)/shard_map/slice | solution.py:417
  103.2 57.1 %collective-permute-start.11 = (bf16[256,2048]{1,0:T(8,128)(2,1)}, bf16[256,2048]{1,0:T(8,128)(2,1)}, u32[]{:S(2)}, u32[]{:S(2)}) collective-permute-start(bf16[256,2048]{1,0:T(8,128)(2,1)} %collective-permute-done.5.refs_5_), channel_id=1, source_target_pairs={{0,1},{1,0},{2,3},{3,2},{4,5},{5,4},{6,7},{7,6},{8,9},{9,8},{10,11... | collective-permute-start | bytes 3145736 | tf_op jit(solution)/shard_map/ppermute | solution.py:35
  124.9 37.1 %collective-permute-start.8 = (bf16[256,2048]{1,0:T(8,128)(2,1)}, bf16[256,2048]{1,0:T(8,128)(2,1)}, u32[]{:S(2)}, u32[]{:S(2)}) collective-permute-start(bf16[256,2048]{1,0:T(8,128)(2,1)} %collective-permute-done.1.refs_2_), channel_id=1, source_target_pairs={{0,1},{1,0},{2,3},{3,2},{4,5},{5,4},{6,7},{7,6},{8,9},{9,8},{10,11... | collective-permute-start | bytes 3145736 | tf_op jit(solution)/shard_map/ppermute | solution.py:35
  126.4 13.0 %all-to-all-start.2 = ((bf16[4,8,16,512]{3,2,1,0:T(8,128)(2,1)}), bf16[4,8,16,512]{3,2,1,0:T(8,128)(2,1)S(1)}, u32[]{:S(2)}, u32[]{:S(2)}) async-start(bf16[4,8,16,512]{3,2,1,0:T(8,128)(2,1)} %add_convert_fusion), calls=%async_computation.2 | async-start | bytes 1048576 | tf_op jit(solution)/shard_map/all_to_all | solution.py:406
  130.1 54.2 %collective-permute-start.10 = (bf16[256,2048]{1,0:T(8,128)(2,1)}, bf16[256,2048]{1,0:T(8,128)(2,1)S(1)}, u32[]{:S(2)}, u32[]{:S(2)}) collective-permute-start(bf16[256,2048]{1,0:T(8,128)(2,1)} %collective-permute-done.4.refs_4_), channel_id=1, source_target_pairs={{0,1},{1,0},{2,3},{3,2},{4,5},{5,4},{6,7},{7,6},{8,9},{9,8},{10,11... | collective-permute-start | bytes 3145736 | tf_op jit(solution)/shard_map/ppermute | solution.py:35
  141.0 4.3 %collective-permute-start.15 = (bf16[4,16,512]{2,1,0:T(8,128)(2,1)S(1)}, bf16[4,16,512]{2,1,0:T(8,128)(2,1)S(1)}, u32[]{:S(2)}, u32[]{:S(2)}) collective-permute-start(bf16[4,16,512]{2,1,0:T(8,128)(2,1)S(1)} %get-tuple-element.18), channel_id=1, source_target_pairs={{0,8},{8,16},{16,24},{24,0},{1,9},{9,17},{17,25},{25,1},{2,10},{10... | collective-permute-start | bytes 196616 | tf_op jit(solution)/shard_map/ppermute | solution.py:35
  145.4 7.9 %collective-permute-start.16 = (bf16[4,16,512]{2,1,0:T(8,128)(2,1)S(1)}, bf16[4,16,512]{2,1,0:T(8,128)(2,1)S(1)}, u32[]{:S(2)}, u32[]{:S(2)}) collective-permute-start(bf16[4,16,512]{2,1,0:T(8,128)(2,1)S(1)} %get-tuple-element.18), channel_id=1, source_target_pairs={{0,16},{8,24},{16,0},{24,8},{1,17},{9,25},{17,1},{25,9},{2,18},{10... | collective-permute-start | bytes 196616 | tf_op jit(solution)/shard_map/ppermute | solution.py:35
  146.9 34.4 %all-to-all-start.3 = ((bf16[8,4,16,512]{3,2,1,0:T(8,128)(2,1)}), bf16[8,4,16,512]{3,2,1,0:T(8,128)(2,1)S(1)}, u32[]{:S(2)}, u32[]{:S(2)}) async-start(bf16[8,4,16,512]{3,2,1,0:T(8,128)(2,1)} %get-tuple-element.19), calls=%async_computation.3 | async-start | bytes 1048576 | tf_op jit(solution)/shard_map/all_to_all | solution.py:440
  153.3 3.2 %collective-permute-start.17 = (bf16[4,16,512]{2,1,0:T(8,128)(2,1)S(1)}, bf16[4,16,512]{2,1,0:T(8,128)(2,1)S(1)}, u32[]{:S(2)}, u32[]{:S(2)}) collective-permute-start(bf16[4,16,512]{2,1,0:T(8,128)(2,1)S(1)} %get-tuple-element.18), channel_id=1, source_target_pairs={{0,24},{8,0},{16,8},{24,16},{1,25},{9,1},{17,9},{25,17},{2,26},{10... | collective-permute-start | bytes 196616 | tf_op jit(solution)/shard_map/ppermute | solution.py:35
  156.5 28.5 %collective-permute-start.9 = (bf16[256,2048]{1,0:T(8,128)(2,1)}, bf16[256,2048]{1,0:T(8,128)(2,1)}, u32[]{:S(2)}, u32[]{:S(2)}) collective-permute-start(bf16[256,2048]{1,0:T(8,128)(2,1)} %collective-permute-done.2.refs_3_), channel_id=1, source_target_pairs={{0,1},{1,0},{2,3},{3,2},{4,5},{5,4},{6,7},{7,6},{8,9},{9,8},{10,11... | collective-permute-start | bytes 3145736 | tf_op jit(solution)/shard_map/ppermute | solution.py:35
  160.2 70.8 %copy-start.10 = (f32[22]{0:T(128)S(1)}, f32[22]{0:T(128)}, u32[]{:S(2)}) copy-start(f32[22]{0:T(128)} %param.29) | copy-start | bytes 268
  160.2 70.8 %copy-start.11 = (f32[22]{0:T(128)S(1)}, f32[22]{0:T(128)}, u32[]{:S(2)}) copy-start(f32[22]{0:T(128)} %param.28) | copy-start | bytes 268
  160.3 13.1 %collective-permute-start.18 = (bf16[4,4,16,512]{3,2,1,0:T(8,128)(2,1)S(1)}, bf16[4,4,16,512]{3,2,1,0:T(8,128)(2,1)S(1)}, u32[]{:S(2)}, u32[]{:S(2)}) collective-permute-start(bf16[4,4,16,512]{3,2,1,0:T(8,128)(2,1)S(1)} %pad_maximum_fusion.refs_14_), channel_id=1, source_target_pairs={{0,32},{32,64},{64,96},{96,128},{128,160},{160,192},{192,224},{224... | collective-permute-start | bytes 786440 | tf_op jit(solution)/shard_map/ppermute | solution.py:35
  162.0 11.4 %collective-permute-start.22 = (bf16[4,4,16,512]{3,2,1,0:T(8,128)(2,1)S(1)}, bf16[4,4,16,512]{3,2,1,0:T(8,128)(2,1)}, u32[]{:S(2)}, u32[]{:S(2)}) collective-permute-start(bf16[4,4,16,512]{3,2,1,0:T(8,128)(2,1)S(1)} %pad_maximum_fusion.refs_14_), channel_id=1, source_target_pairs={{0,224},{32,0},{64,32},{96,64},{128,96},{160,128},{192,160},{224,1... | collective-permute-start | bytes 786440 | tf_op jit(solution)/shard_map/ppermute | solution.py:35
  173.4 7.9 %collective-permute-start.19 = (bf16[4,4,16,512]{3,2,1,0:T(8,128)(2,1)S(1)}, bf16[4,4,16,512]{3,2,1,0:T(8,128)(2,1)}, u32[]{:S(2)}, u32[]{:S(2)}) collective-permute-start(bf16[4,4,16,512]{3,2,1,0:T(8,128)(2,1)S(1)} %collective-permute-done.18.refs_15_), channel_id=1, source_target_pairs={{0,32},{32,64},{64,96},{96,128},{128,160},{160,192},{192,224},{224... | collective-permute-start | bytes 786440 | tf_op jit(solution)/shard_map/ppermute | solution.py:35
  173.4 8.3 %collective-permute-start.23 = (bf16[4,4,16,512]{3,2,1,0:T(8,128)(2,1)}, bf16[4,4,16,512]{3,2,1,0:T(8,128)(2,1)}, u32[]{:S(2)}, u32[]{:S(2)}) collective-permute-start(bf16[4,4,16,512]{3,2,1,0:T(8,128)(2,1)} %collective-permute-done.22.refs_21_), channel_id=1, source_target_pairs={{0,224},{32,0},{64,32},{96,64},{128,96},{160,128},{192,160},{224,1... | collective-permute-start | bytes 786440 | tf_op jit(solution)/shard_map/ppermute | solution.py:35
  181.3 7.3 %collective-permute-start.20 = (bf16[4,4,16,512]{3,2,1,0:T(8,128)(2,1)}, bf16[4,4,16,512]{3,2,1,0:T(8,128)(2,1)}, u32[]{:S(2)}, u32[]{:S(2)}) collective-permute-start(bf16[4,4,16,512]{3,2,1,0:T(8,128)(2,1)} %collective-permute-done.19.refs_16_), channel_id=1, source_target_pairs={{0,32},{32,64},{64,96},{96,128},{128,160},{160,192},{192,224},{224... | collective-permute-start | bytes 786440 | tf_op jit(solution)/shard_map/ppermute | solution.py:35
  181.3 14.2 %collective-permute-start.25 = (bf16[8,4,16,512]{3,2,1,0:T(8,128)(2,1)S(1)}, bf16[8,4,16,512]{3,2,1,0:T(8,128)(2,1)S(1)}, u32[]{:S(2)}, u32[]{:S(2)}) collective-permute-start(bf16[8,4,16,512]{3,2,1,0:T(8,128)(2,1)S(1)} %all-to-all-done.3.refs_22_), channel_id=1, source_target_pairs={{0,8},{8,16},{16,24},{24,0},{1,9},{9,17},{17,25},{25,1},{2,10},{10... | collective-permute-start | bytes 1572872 | tf_op jit(solution)/shard_map/ppermute | solution.py:35
  181.7 24.1 %collective-permute-start.26 = (bf16[8,4,16,512]{3,2,1,0:T(8,128)(2,1)S(1)}, bf16[8,4,16,512]{3,2,1,0:T(8,128)(2,1)S(1)}, u32[]{:S(2)}, u32[]{:S(2)}) collective-permute-start(bf16[8,4,16,512]{3,2,1,0:T(8,128)(2,1)S(1)} %all-to-all-done.3.refs_22_), channel_id=1, source_target_pairs={{0,16},{8,24},{16,0},{24,8},{1,17},{9,25},{17,1},{25,9},{2,18},{10... | collective-permute-start | bytes 1572872 | tf_op jit(solution)/shard_map/ppermute | solution.py:35
  184.3 23.0 %collective-permute-start.27 = (bf16[8,4,16,512]{3,2,1,0:T(8,128)(2,1)S(1)}, bf16[8,4,16,512]{3,2,1,0:T(8,128)(2,1)S(1)}, u32[]{:S(2)}, u32[]{:S(2)}) collective-permute-start(bf16[8,4,16,512]{3,2,1,0:T(8,128)(2,1)S(1)} %all-to-all-done.3.refs_22_), channel_id=1, source_target_pairs={{0,24},{8,0},{16,8},{24,16},{1,25},{9,1},{17,9},{25,17},{2,26},{10... | collective-permute-start | bytes 1572872 | tf_op jit(solution)/shard_map/ppermute | solution.py:35
  185.0 6.2 %collective-permute-start.24 = (bf16[4,4,16,512]{3,2,1,0:T(8,128)(2,1)}, bf16[4,4,16,512]{3,2,1,0:T(8,128)(2,1)S(1)}, u32[]{:S(2)}, u32[]{:S(2)}) collective-permute-start(bf16[4,4,16,512]{3,2,1,0:T(8,128)(2,1)} %collective-permute-done.23.refs_20_), channel_id=1, source_target_pairs={{0,224},{32,0},{64,32},{96,64},{128,96},{160,128},{192,160},{224,1... | collective-permute-start | bytes 786440 | tf_op jit(solution)/shard_map/ppermute | solution.py:35
  188.6 6.9 %collective-permute-start.21 = (bf16[4,4,16,512]{3,2,1,0:T(8,128)(2,1)}, bf16[4,4,16,512]{3,2,1,0:T(8,128)(2,1)S(1)}, u32[]{:S(2)}, u32[]{:S(2)}) collective-permute-start(bf16[4,4,16,512]{3,2,1,0:T(8,128)(2,1)} %collective-permute-done.20.refs_17_), channel_id=1, source_target_pairs={{0,32},{32,64},{64,96},{96,128},{128,160},{160,192},{192,224},{224... | collective-permute-start | bytes 786440 | tf_op jit(solution)/shard_map/ppermute | solution.py:35
  222.0 18.3 %all-to-all-start.4 = ((f32[32,8,128]{2,1,0:T(8,128)}), f32[32,8,128]{2,1,0:T(8,128)S(1)}, u32[]{:S(2)}, u32[]{:S(2)}) async-start(f32[32,8,128]{2,1,0:T(8,128)} %logits.1), calls=%async_computation.4 | async-start | bytes 262144 | tf_op jit(solution)/shard_map/all_to_all | solution.py:454
  241.1 10.1 %all-to-all-start.5 = ((f32[8,8,128]{2,1,0:T(8,128)}), f32[8,8,128]{2,1,0:T(8,128)S(1)}, u32[]{:S(2)}, u32[]{:S(2)}) async-start(f32[8,8,128]{2,1,0:T(8,128)} %get-tuple-element.22), calls=%async_computation.5 | async-start | bytes 65536 | tf_op jit(solution)/shard_map/all_to_all | solution.py:459

commit v6 on v5

--- a/solution.py
+++ b/solution.py
@@ -232,10 +232,8 @@
             for p, ref in enumerate(pieces)
         ]
 
-    @pl.loop(0, BLOCKS)
-    def _(j):
-        for copy in copies(j):
-            copy.start()
+    for copy in copies(0):
+        copy.start()
 
     eye = lax.broadcasted_iota(i32, (128, 128), 0) == lax.broadcasted_iota(i32, (128, 128), 1)
     for q in range(4):
@@ -255,6 +253,9 @@
             for k in range(4):
                 rows_ref[a_rows, k * 512 : k * 512 + 512] = rows_a[dz][dy, k]
                 rows_ref[b_rows, 2048 + k * 512 : 2560 + k * 512] = rows_b[dy][dz, k]
+
+    for copy in copies(1):
+        copy.start()
 
     def multiply(j):
         for copy in copies(j):
@@ -276,6 +277,11 @@
 
     @pl.loop(1, BLOCKS)
     def _(j):
+        @pl.when(j + 1 < BLOCKS)
+        def _():
+            for copy in copies(j + 1):
+                copy.start()
+
         logits = multiply(j)
         reduce(j - 1, logit_ref[lax.rem(j - 1, 2)])
         logit_ref[lax.rem(j, 2)] = logits

time: 252 us -> 253 us (level)
  no operation moved by 1% of the time
where the time goes in v6:
time: 253 us; the launch traced here: 252 us
  waiting for transfers between devices  113 us (45%)
  starting transfers between devices  75.2 us (30%)
  blocking collectives  28.9 us (11%)
  Pallas kernels  25.2 us (10%)
  local copies, waits for them, and re-layouts  6.91 us (3%)
    ppermute x28, waiting for transfers between devices, shift(): return lax.ppermute(array, axis, [(i, (i + by) % n) for i in range(n)])  77.9 us
    ppermute x28, starting transfers between devices, shift(): return lax.ppermute(array, axis, [(i, (i + by) % n) for i in range(n)])  34.3 us
    all_gather x1, blocking collectives, program(): same = lax.all_gather(block, 'x', axis=0, tiled=False)  28.9 us
    pallas_call x1, Pallas kernels, logits_call(): pl.pallas_call(logits_kernel, out_shape=sds((32, 8, 128), f32), in_specs=...  14.9 us
    all_to_all x1, starting transfers between devices, program(): got = lax.all_to_all(packed, DP, 0, 0, tiled=True)  12 us
    pallas_call x6, Pallas kernels, call(): pl.pallas_call(kernel, out_shape=out_shape, in_specs=([pl.BlockSpec(memor...  10.3 us
    all_to_all x1, waiting for transfers between devices, program(): sums = lax.all_to_all(pair, 'x', 0, 0, tiled=True)  8.96 us
    all_to_all x1, starting transfers between devices, program(): merged = lax.all_to_all(pieces, DP, 0, 0, tiled=True)  8.91 us
  transfers between devices with their start and end apart: 34, of which 16 were waited for; matrix products, arithmetic and copies ran while one was open for 3% of the time, Pallas kernels for 3%

profile of v6, /device:TPU:1, one launch (start us, length us, event | category | flops | bytes accessed | tf_op | source)
XLA Modules:
  0.0 252.0 jit_solution(12031602304873340229)
XLA Ops:
  0.6 1.8 shard_map.175
  2.4 12.0 %all-to-all-start = ((bf16[32,5,8,128]{3,2,1,0:T(8,128)(2,1)}), bf16[32,5,8,128]{3,2,1,0:T(8,128)(2,1)S(1)}, u32[]{:S(2)}, u32[]{:S(2)}) async-start(bf16[32,5,8,128]{3,2,1,0:T(8,128)(2,1)} %shard_map.175), calls=%async_computation | async-start | bytes 655360 | tf_op jit(solution)/shard_map/all_to_all | solution.py:379
  14.5 3.3 %fusion.10 = (bf16[256,2048]{1,0:T(8,128)(2,1)}, bf16[256,2048]{1,0:T(8,128)(2,1)}) fusion(bf16[512,2048]{1,0:T(8,128)(2,1)} %refs_0_.3), kind=kLoop, calls=%fused_computation.33 | loop fusion | bytes 4194304 | tf_op jit(solution)/shard_map/slice | solution.py:414
  17.8 2.5 collective-permute-start.3
  20.5 6.6 %all-to-all-done = bf16[32,5,8,128]{3,2,1,0:T(8,128)(2,1)S(1)} async-done(((bf16[32,5,8,128]{3,2,1,0:T(8,128)(2,1)}), bf16[32,5,8,128]{3,2,1,0:T(8,128)(2,1)S(1)}, u32[]{:S(2)}, u32[]{:S(2)}) %all-to-all-start) | async-done | bytes 327712 | tf_op jit(solution)/shard_map/all_to_all | solution.py:379
  27.6 1.3 shard_map.176
  28.9 4.8 %all-to-all-start.1 = ((bf16[32,16,128]{2,1,0:T(8,128)(2,1)}), bf16[32,16,128]{2,1,0:T(8,128)(2,1)S(1)}, u32[]{:S(2)}, u32[]{:S(2)}) async-start(bf16[32,16,128]{2,1,0:T(8,128)(2,1)} %bitcast.8), calls=%async_computation.1 | async-start | bytes 262144 | tf_op jit(solution)/shard_map/all_to_all | solution.py:389
  33.7 2.6 %collective-permute-start.5 = (bf16[256,2048]{1,0:T(8,128)(2,1)}, bf16[256,2048]{1,0:T(8,128)(2,1)}, u32[]{:S(2)}, u32[]{:S(2)}) collective-permute-start(bf16[256,2048]{1,0:T(8,128)(2,1)} %get-tuple-element.30), channel_id=1, source_target_pairs={{0,6},{2,0},{4,2},{6,4},{1,7},{3,1},{5,3},{7,5},{8,14},{10,8},{12,... | collective-permute-start | bytes 3145736 | tf_op jit(solution)/shard_map/ppermute | solution.py:35
  36.3 6.8 %all-to-all-done.1 = bf16[32,16,128]{2,1,0:T(8,128)(2,1)S(1)} async-done(((bf16[32,16,128]{2,1,0:T(8,128)(2,1)}), bf16[32,16,128]{2,1,0:T(8,128)(2,1)S(1)}, u32[]{:S(2)}, u32[]{:S(2)}) %all-to-all-start.1) | async-done | bytes 131104 | tf_op jit(solution)/shard_map/all_to_all | solution.py:389
  43.1 28.9 %all-gather = bf16[128,16,128]{2,1,0:T(8,128)(2,1)S(1)} all-gather(bf16[32,16,128]{2,1,0:T(8,128)(2,1)S(1)} %all-to-all-done.1), channel_id=2, replica_groups=mesh['z'=8,'y'=4,'x'=4,'c'=2] {'x'}, dimensions={0}, use_global_device_ids=true | all-gather | bytes 655360 | tf_op jit(solution)/shard_map/all_gather | solution.py:391
  72.0 3.3 %collective-permute-start.13 = (bf16[4,32,16,128]{3,2,1,0:T(8,128)(2,1)S(1)}, bf16[4,32,16,128]{3,2,1,0:T(8,128)(2,1)S(1)}, u32[]{:S(2)}, u32[]{:S(2)}) collective-permute-start(bf16[4,32,16,128]{3,2,1,0:T(8,128)(2,1)S(1)} %bitcast.28), channel_id=1, source_target_pairs={{0,1},{1,0},{2,3},{3,2},{4,5},{5,4},{6,7},{7,6},{8,9},{9,8},{10,11... | collective-permute-start | bytes 1572872 | tf_op jit(solution)/shard_map/ppermute | solution.py:35
  75.3 2.0 collective-permute-start.1
  77.3 1.2 collective-permute-start.4
  78.9 0.8 copy-done.2
  79.8 1.0 copy-done.3
  80.8 4.1 %shard_map.177 = (bf16[4,8,16,512]{3,2,1,0:T(8,128)(2,1)S(1)}, bf16[4,8,16,512]{3,2,1,0:T(8,128)(2,1)S(1)}, bf16[8,16,512]{2,1,0:T(8,128)(2,1)S(1)}) custom-call(s32[4]{0:T(128)S(1)} %pad_add_fusion.at_ref, bf16[4,32,16,128]{3,2,1,0:T(8,128)(2,1)S(1)} %bitcast.29, bf16[4,32,16,128]{3,2,1,0:T(8,128)(2,1)S(1)} %copy-done.3, f32[8,1,512]{2,1,0:T(1,128)S(1)} %bitcast.32, ...), custom_call_target="tpu_custom_call" | custom-call | flops 1073741824 | tf_op jit(solution)/shard_map/pallas_call | solution.py:41
  84.9 0.9 collective-permute-start.14
  86.0 16.4 %collective-permute-done.1.refs_2_ = bf16[256,2048]{1,0:T(8,128)(2,1)} collective-permute-done((bf16[256,2048]{1,0:T(8,128)(2,1)}, bf16[256,2048]{1,0:T(8,128)(2,1)}, u32[]{:S(2)}, u32[]{:S(2)}) %collective-permute-start.1) | collective-permute-done | bytes 1048608 | tf_op jit(solution)/shard_map/ppermute | solution.py:35
  103.8 21.1 %collective-permute-done.2.refs_3_ = bf16[256,2048]{1,0:T(8,128)(2,1)} collective-permute-done((bf16[256,2048]{1,0:T(8,128)(2,1)}, bf16[256,2048]{1,0:T(8,128)(2,1)}, u32[]{:S(2)}, u32[]{:S(2)}) %collective-permute-start.2) | collective-permute-done | bytes 1048608 | tf_op jit(solution)/shard_map/ppermute | solution.py:35
  125.4 1.0 add_convert_fusion
  126.4 3.5 %all-to-all-start.2 = ((bf16[4,8,16,512]{3,2,1,0:T(8,128)(2,1)}), bf16[4,8,16,512]{3,2,1,0:T(8,128)(2,1)S(1)}, u32[]{:S(2)}, u32[]{:S(2)}) async-start(bf16[4,8,16,512]{3,2,1,0:T(8,128)(2,1)} %add_convert_fusion), calls=%async_computation.2 | async-start | bytes 1048576 | tf_op jit(solution)/shard_map/all_to_all | solution.py:412
  130.5 9.0 %all-to-all-done.2.sums = bf16[4,8,16,512]{3,2,1,0:T(8,128)(2,1)S(1)} async-done(((bf16[4,8,16,512]{3,2,1,0:T(8,128)(2,1)}), bf16[4,8,16,512]{3,2,1,0:T(8,128)(2,1)S(1)}, u32[]{:S(2)}, u32[]{:S(2)}) %all-to-all-start.2) | async-done | bytes 524320 | tf_op jit(solution)/shard_map/all_to_all | solution.py:412
  139.5 1.6 shard_map.178
  141.0 1.2 collective-permute-start.15
  142.3 3.1 %collective-permute-done.15 = bf16[4,16,512]{2,1,0:T(8,128)(2,1)S(1)} collective-permute-done((bf16[4,16,512]{2,1,0:T(8,128)(2,1)S(1)}, bf16[4,16,512]{2,1,0:T(8,128)(2,1)S(1)}, u32[]{:S(2)}, u32[]{:S(2)}) %collective-permute-start.15) | collective-permute-done | bytes 65568 | tf_op jit(solution)/shard_map/ppermute | solution.py:35
  145.4 1.5 collective-permute-start.16
  146.9 6.4 %all-to-all-start.3 = ((bf16[8,4,16,512]{3,2,1,0:T(8,128)(2,1)}), bf16[8,4,16,512]{3,2,1,0:T(8,128)(2,1)S(1)}, u32[]{:S(2)}, u32[]{:S(2)}) async-start(bf16[8,4,16,512]{3,2,1,0:T(8,128)(2,1)} %get-tuple-element.19), calls=%async_computation.3 | async-start | bytes 1048576 | tf_op jit(solution)/shard_map/all_to_all | solution.py:446
  153.3 1.0 collective-permute-start.17
  154.2 2.2 collective-permute-done.17
  156.5 3.7 %collective-permute-start.9 = (bf16[256,2048]{1,0:T(8,128)(2,1)}, bf16[256,2048]{1,0:T(8,128)(2,1)}, u32[]{:S(2)}, u32[]{:S(2)}) collective-permute-start(bf16[256,2048]{1,0:T(8,128)(2,1)} %collective-permute-done.2.refs_3_), channel_id=1, source_target_pairs={{0,1},{1,0},{2,3},{3,2},{4,5},{5,4},{6,7},{7,6},{8,9},{9,8},{10,11... | collective-permute-start | bytes 3145736 | tf_op jit(solution)/shard_map/ppermute | solution.py:35
  160.3 1.7 collective-permute-start.18
  162.0 1.3 collective-permute-start.22
  163.3 10.1 %collective-permute-done.18.refs_15_ = bf16[4,4,16,512]{3,2,1,0:T(8,128)(2,1)S(1)} collective-permute-done((bf16[4,4,16,512]{3,2,1,0:T(8,128)(2,1)S(1)}, bf16[4,4,16,512]{3,2,1,0:T(8,128)(2,1)S(1)}, u32[]{:S(2)}, u32[]{:S(2)}) %collective-permute-start.18) | collective-permute-done | bytes 262176 | tf_op jit(solution)/shard_map/ppermute | solution.py:35
  173.4 2.7 %collective-permute-start.23 = (bf16[4,4,16,512]{3,2,1,0:T(8,128)(2,1)}, bf16[4,4,16,512]{3,2,1,0:T(8,128)(2,1)}, u32[]{:S(2)}, u32[]{:S(2)}) collective-permute-start(bf16[4,4,16,512]{3,2,1,0:T(8,128)(2,1)} %collective-permute-done.22.refs_21_), channel_id=1, source_target_pairs={{0,224},{32,0},{64,32},{96,64},{128,96},{160,128},{192,160},{224,1... | collective-permute-start | bytes 786440 | tf_op jit(solution)/shard_map/ppermute | solution.py:35
  176.1 5.2 %collective-permute-done.19.refs_16_ = bf16[4,4,16,512]{3,2,1,0:T(8,128)(2,1)} collective-permute-done((bf16[4,4,16,512]{3,2,1,0:T(8,128)(2,1)S(1)}, bf16[4,4,16,512]{3,2,1,0:T(8,128)(2,1)}, u32[]{:S(2)}, u32[]{:S(2)}) %collective-permute-start.19) | collective-permute-done | bytes 262176 | tf_op jit(solution)/shard_map/ppermute | solution.py:35
  181.7 2.6 %collective-permute-start.26 = (bf16[8,4,16,512]{3,2,1,0:T(8,128)(2,1)S(1)}, bf16[8,4,16,512]{3,2,1,0:T(8,128)(2,1)S(1)}, u32[]{:S(2)}, u32[]{:S(2)}) collective-permute-start(bf16[8,4,16,512]{3,2,1,0:T(8,128)(2,1)S(1)} %all-to-all-done.3.refs_22_), channel_id=1, source_target_pairs={{0,16},{8,24},{16,0},{24,8},{1,17},{9,25},{17,1},{25,9},{2,18},{10... | collective-permute-start | bytes 1572872 | tf_op jit(solution)/shard_map/ppermute | solution.py:35
  185.0 2.6 %collective-permute-start.24 = (bf16[4,4,16,512]{3,2,1,0:T(8,128)(2,1)}, bf16[4,4,16,512]{3,2,1,0:T(8,128)(2,1)S(1)}, u32[]{:S(2)}, u32[]{:S(2)}) collective-permute-start(bf16[4,4,16,512]{3,2,1,0:T(8,128)(2,1)} %collective-permute-done.23.refs_20_), channel_id=1, source_target_pairs={{0,224},{32,0},{64,32},{96,64},{128,96},{160,128},{192,160},{224,1... | collective-permute-start | bytes 786440 | tf_op jit(solution)/shard_map/ppermute | solution.py:35
  187.6 1.0 collective-permute-done.20.refs_17_
  188.6 2.6 %collective-permute-done.24.refs_19_ = bf16[4,4,16,512]{3,2,1,0:T(8,128)(2,1)S(1)} collective-permute-done((bf16[4,4,16,512]{3,2,1,0:T(8,128)(2,1)}, bf16[4,4,16,512]{3,2,1,0:T(8,128)(2,1)S(1)}, u32[]{:S(2)}, u32[]{:S(2)}) %collective-permute-start.24) | collective-permute-done | bytes 262176 | tf_op jit(solution)/shard_map/ppermute | solution.py:35
  191.2 4.3 %collective-permute-done.21.refs_18_ = bf16[4,4,16,512]{3,2,1,0:T(8,128)(2,1)S(1)} collective-permute-done((bf16[4,4,16,512]{3,2,1,0:T(8,128)(2,1)}, bf16[4,4,16,512]{3,2,1,0:T(8,128)(2,1)S(1)}, u32[]{:S(2)}, u32[]{:S(2)}) %collective-permute-start.21) | collective-permute-done | bytes 262176 | tf_op jit(solution)/shard_map/ppermute | solution.py:35
  195.5 10.3 %collective-permute-done.26.refs_24_ = bf16[8,4,16,512]{3,2,1,0:T(8,128)(2,1)S(1)} collective-permute-done((bf16[8,4,16,512]{3,2,1,0:T(8,128)(2,1)S(1)}, bf16[8,4,16,512]{3,2,1,0:T(8,128)(2,1)S(1)}, u32[]{:S(2)}, u32[]{:S(2)}) %collective-permute-start.26) | collective-permute-done | bytes 524320 | tf_op jit(solution)/shard_map/ppermute | solution.py:35
  205.8 1.4 collective-permute-done.27.refs_25_
  207.2 14.9 %logits.1 = f32[32,8,128]{2,1,0:T(8,128)} custom-call(s32[4]{0:T(128)S(1)} %pad_add_fusion.at_ref, bf16[512,2048]{1,0:T(8,128)(2,1)} %refs_0_.3, bf16[256,2048]{1,0:T(8,128)(2,1)} %collective-permute-done.refs_1_, bf16[256,2048]{1,0:T(8,128)(2,1)} %collective-permute-done.1.refs_2_, bf16[256,2048]{1,0:T(8,128)(2,1)} %collective-permute-done.2.refs_3_, ...), custom_call_target="tpu_custom_call" | custom-call | flops 8589934592 | bytes 20971520 | tf_op jit(solution)/shard_map/logits/pallas_call | solution.py:303
  222.2 8.9 %all-to-all-start.4 = ((f32[32,8,128]{2,1,0:T(8,128)}), f32[32,8,128]{2,1,0:T(8,128)S(1)}, u32[]{:S(2)}, u32[]{:S(2)}) async-start(f32[32,8,128]{2,1,0:T(8,128)} %logits.1), calls=%async_computation.4 | async-start | bytes 262144 | tf_op jit(solution)/shard_map/all_to_all | solution.py:460
  231.8 8.7 %all-to-all-done.4.got_ref = f32[32,8,128]{2,1,0:T(8,128)S(1)} async-done(((f32[32,8,128]{2,1,0:T(8,128)}), f32[32,8,128]{2,1,0:T(8,128)S(1)}, u32[]{:S(2)}, u32[]{:S(2)}) %all-to-all-start.4) | async-done | bytes 131104 | tf_op jit(solution)/shard_map/all_to_all | solution.py:460
  240.4 0.8 shard_map.179
  241.2 5.3 %all-to-all-start.5 = ((f32[8,8,128]{2,1,0:T(8,128)}), f32[8,8,128]{2,1,0:T(8,128)S(1)}, u32[]{:S(2)}, u32[]{:S(2)}) async-start(f32[8,8,128]{2,1,0:T(8,128)} %get-tuple-element.22), calls=%async_computation.5 | async-start | bytes 65536 | tf_op jit(solution)/shard_map/all_to_all | solution.py:465
  247.1 4.2 %all-to-all-done.5.sums_ref = f32[8,8,128]{2,1,0:T(8,128)S(1)} async-done(((f32[8,8,128]{2,1,0:T(8,128)}), f32[8,8,128]{2,1,0:T(8,128)S(1)}, u32[]{:S(2)}, u32[]{:S(2)}) %all-to-all-start.5) | async-done | bytes 32800 | tf_op jit(solution)/shard_map/all_to_all | solution.py:465
  (81 shorter events, 6.7 us)
Async XLA Ops:
  2.4 24.7 %all-to-all-start = ((bf16[32,5,8,128]{3,2,1,0:T(8,128)(2,1)}), bf16[32,5,8,128]{3,2,1,0:T(8,128)(2,1)S(1)}, u32[]{:S(2)}, u32[]{:S(2)}) async-start(bf16[32,5,8,128]{3,2,1,0:T(8,128)(2,1)} %shard_map.175), calls=%async_computation | async-start | bytes 655360 | tf_op jit(solution)/shard_map/all_to_all | solution.py:379
  14.5 5.9 %copy-start.9 = (s32[32]{0:T(128)S(1)}, s32[32]{0:T(128)}, u32[]{:S(2)}) copy-start(s32[32]{0:T(128)} %param.19) | copy-start | bytes 388
  14.5 65.3 %copy-start = (bf16[4096,128]{1,0:T(8,128)(2,1)S(1)}, bf16[4096,128]{1,0:T(8,128)(2,1)}, u32[]{:S(2)}) copy-start(bf16[4096,128]{1,0:T(8,128)(2,1)} %refs_1_.1) | copy-start | bytes 3145732
  14.5 65.2 %copy-start.1 = (bf16[4096,128]{1,0:T(8,128)(2,1)S(1)}, bf16[4096,128]{1,0:T(8,128)(2,1)}, u32[]{:S(2)}) copy-start(bf16[4096,128]{1,0:T(8,128)(2,1)} %refs_2_.1) | copy-start | bytes 3145732
  14.5 65.2 %copy-start.4 = (f32[128,128]{1,0:T(8,128)S(1)}, f32[128,128]{1,0:T(8,128)}, u32[]{:S(2)}) copy-start(f32[128,128]{1,0:T(8,128)} %constant.95.clone.cos) | copy-start | bytes 196612
  14.5 65.2 %copy-start.5 = (f32[128,128]{1,0:T(8,128)S(1)}, f32[128,128]{1,0:T(8,128)}, u32[]{:S(2)}) copy-start(f32[128,128]{1,0:T(8,128)} %constant.96.clone.sin) | copy-start | bytes 196612
  14.5 65.2 %copy-start.6 = (f32[4096]{0:T(1024)S(1)}, f32[4096]{0:T(1024)}, u32[]{:S(2)}) copy-start(f32[4096]{0:T(1024)} %param.21) | copy-start | bytes 49156
  17.8 59.5 %collective-permute-start.3 = (bf16[256,2048]{1,0:T(8,128)(2,1)}, bf16[256,2048]{1,0:T(8,128)(2,1)}, u32[]{:S(2)}, u32[]{:S(2)}) collective-permute-start(bf16[256,2048]{1,0:T(8,128)(2,1)} %get-tuple-element.29), channel_id=1, source_target_pairs={{0,6},{2,0},{4,2},{6,4},{1,7},{3,1},{5,3},{7,5},{8,14},{10,8},{12,... | collective-permute-start | bytes 3145736 | tf_op jit(solution)/shard_map/ppermute | solution.py:35
  20.3 58.2 %collective-permute-start = (bf16[256,2048]{1,0:T(8,128)(2,1)}, bf16[256,2048]{1,0:T(8,128)(2,1)}, u32[]{:S(2)}, u32[]{:S(2)}) collective-permute-start(bf16[256,2048]{1,0:T(8,128)(2,1)} %get-tuple-element.30), channel_id=1, source_target_pairs={{0,2},{2,4},{4,6},{6,0},{1,3},{3,5},{5,7},{7,1},{8,10},{10,12},{12... | collective-permute-start | bytes 3145736 | tf_op jit(solution)/shard_map/ppermute | solution.py:35
  27.2 76.0 %copy-start.8 = (bf16[32,8,128]{2,1,0:T(8,128)(2,1)}, bf16[32,8,128]{2,1,0:T(8,128)(2,1)S(1)}, u32[]{:S(2)}) copy-start(bf16[32,8,128]{2,1,0:T(8,128)(2,1)S(1)} %slice_bitcast_fusion) | copy-start | bytes 196612
  28.9 14.2 %all-to-all-start.1 = ((bf16[32,16,128]{2,1,0:T(8,128)(2,1)}), bf16[32,16,128]{2,1,0:T(8,128)(2,1)S(1)}, u32[]{:S(2)}, u32[]{:S(2)}) async-start(bf16[32,16,128]{2,1,0:T(8,128)(2,1)} %bitcast.8), calls=%async_computation.1 | async-start | bytes 262144 | tf_op jit(solution)/shard_map/all_to_all | solution.py:389
  33.7 52.2 %collective-permute-start.5 = (bf16[256,2048]{1,0:T(8,128)(2,1)}, bf16[256,2048]{1,0:T(8,128)(2,1)}, u32[]{:S(2)}, u32[]{:S(2)}) collective-permute-start(bf16[256,2048]{1,0:T(8,128)(2,1)} %get-tuple-element.30), channel_id=1, source_target_pairs={{0,6},{2,0},{4,2},{6,4},{1,7},{3,1},{5,3},{7,5},{8,14},{10,8},{12,... | collective-permute-start | bytes 3145736 | tf_op jit(solution)/shard_map/ppermute | solution.py:35
  72.0 6.9 %collective-permute-start.13 = (bf16[4,32,16,128]{3,2,1,0:T(8,128)(2,1)S(1)}, bf16[4,32,16,128]{3,2,1,0:T(8,128)(2,1)S(1)}, u32[]{:S(2)}, u32[]{:S(2)}) collective-permute-start(bf16[4,32,16,128]{3,2,1,0:T(8,128)(2,1)S(1)} %bitcast.28), channel_id=1, source_target_pairs={{0,1},{1,0},{2,3},{3,2},{4,5},{5,4},{6,7},{7,6},{8,9},{9,8},{10,11... | collective-permute-start | bytes 1572872 | tf_op jit(solution)/shard_map/ppermute | solution.py:35
  75.3 27.1 %collective-permute-start.1 = (bf16[256,2048]{1,0:T(8,128)(2,1)}, bf16[256,2048]{1,0:T(8,128)(2,1)}, u32[]{:S(2)}, u32[]{:S(2)}) collective-permute-start(bf16[256,2048]{1,0:T(8,128)(2,1)} %get-tuple-element.29), channel_id=1, source_target_pairs={{0,2},{2,4},{4,6},{6,0},{1,3},{3,5},{5,7},{7,1},{8,10},{10,12},{12... | collective-permute-start | bytes 3145736 | tf_op jit(solution)/shard_map/ppermute | solution.py:35
  77.3 25.8 %collective-permute-start.4 = (bf16[256,2048]{1,0:T(8,128)(2,1)}, bf16[256,2048]{1,0:T(8,128)(2,1)}, u32[]{:S(2)}, u32[]{:S(2)}) collective-permute-start(bf16[256,2048]{1,0:T(8,128)(2,1)} %collective-permute-done.3.refs_6_), channel_id=1, source_target_pairs={{0,6},{2,0},{4,2},{6,4},{1,7},{3,1},{5,3},{7,5},{8,14},{10,8},{12,... | collective-permute-start | bytes 3145736 | tf_op jit(solution)/shard_map/ppermute | solution.py:35
  78.6 46.3 %collective-permute-start.2 = (bf16[256,2048]{1,0:T(8,128)(2,1)}, bf16[256,2048]{1,0:T(8,128)(2,1)}, u32[]{:S(2)}, u32[]{:S(2)}) collective-permute-start(bf16[256,2048]{1,0:T(8,128)(2,1)} %collective-permute-done.refs_1_), channel_id=1, source_target_pairs={{0,2},{2,4},{4,6},{6,0},{1,3},{3,5},{5,7},{7,1},{8,10},{10,12},{12... | collective-permute-start | bytes 3145736 | tf_op jit(solution)/shard_map/ppermute | solution.py:35
  78.9 0.8 copy-start.2
  79.8 1.0 copy-start.3
  84.9 54.5 %copy-start.7 = (f32[4096]{0:T(1024)S(1)}, f32[4096]{0:T(1024)}, u32[]{:S(2)}) copy-start(f32[4096]{0:T(1024)} %param.26) | copy-start | bytes 49156
  84.9 18.2 %collective-permute-start.14 = (bf16[4,8,16,512]{3,2,1,0:T(8,128)(2,1)S(1)}, bf16[4,8,16,512]{3,2,1,0:T(8,128)(2,1)S(1)}, u32[]{:S(2)}, u32[]{:S(2)}) collective-permute-start(bf16[4,8,16,512]{3,2,1,0:T(8,128)(2,1)S(1)} %get-tuple-element.16), channel_id=1, source_target_pairs={{0,1},{1,0},{2,3},{3,2},{4,5},{5,4},{6,7},{7,6},{8,9},{9,8},{10,11... | collective-permute-start | bytes 1572872 | tf_op jit(solution)/shard_map/ppermute | solution.py:35
  85.9 44.2 %collective-permute-start.12 = (bf16[256,2048]{1,0:T(8,128)(2,1)}, bf16[256,2048]{1,0:T(8,128)(2,1)S(1)}, u32[]{:S(2)}, u32[]{:S(2)}) collective-permute-start(bf16[256,2048]{1,0:T(8,128)(2,1)} %collective-permute-done.3.refs_6_), channel_id=1, source_target_pairs={{0,1},{1,0},{2,3},{3,2},{4,5},{5,4},{6,7},{7,6},{8,9},{9,8},{10,11... | collective-permute-start | bytes 3145736 | tf_op jit(solution)/shard_map/ppermute | solution.py:35
  102.4 78.9 %collective-permute-start.6 = (bf16[512,2048]{1,0:T(8,128)(2,1)}, bf16[512,2048]{1,0:T(8,128)(2,1)}, u32[]{:S(2)}, u32[]{:S(2)}) collective-permute-start(bf16[512,2048]{1,0:T(8,128)(2,1)} %refs_0_.3), channel_id=1, source_target_pairs={{0,1},{1,0},{2,3},{3,2},{4,5},{5,4},{6,7},{7,6},{8,9},{9,8},{10,11... | collective-permute-start | bytes 6291464 | tf_op jit(solution)/shard_map/ppermute | solution.py:35
  103.2 37.9 %collective-permute-start.7 = (bf16[256,2048]{1,0:T(8,128)(2,1)}, bf16[256,2048]{1,0:T(8,128)(2,1)}, u32[]{:S(2)}, u32[]{:S(2)}) collective-permute-start(bf16[256,2048]{1,0:T(8,128)(2,1)} %collective-permute-done.refs_1_), channel_id=1, source_target_pairs={{0,1},{1,0},{2,3},{3,2},{4,5},{5,4},{6,7},{7,6},{8,9},{9,8},{10,11... | collective-permute-start | bytes 3145736 | tf_op jit(solution)/shard_map/ppermute | solution.py:35
  103.2 26.8 %slice-start = ((bf16[32,8,128]{2,1,0:T(8,128)(2,1)}), bf16[32,4,128]{2,1,0:T(4,128)(2,1)S(1)}, s32[]{:S(2)}) async-start(bf16[32,8,128]{2,1,0:T(8,128)(2,1)} %copy-done.8), calls=%async_computation.6 | async-start | bytes 65536 | tf_op jit(solution)/shard_map/slice | solution.py:423
  103.2 57.1 %collective-permute-start.11 = (bf16[256,2048]{1,0:T(8,128)(2,1)}, bf16[256,2048]{1,0:T(8,128)(2,1)}, u32[]{:S(2)}, u32[]{:S(2)}) collective-permute-start(bf16[256,2048]{1,0:T(8,128)(2,1)} %collective-permute-done.5.refs_5_), channel_id=1, source_target_pairs={{0,1},{1,0},{2,3},{3,2},{4,5},{5,4},{6,7},{7,6},{8,9},{9,8},{10,11... | collective-permute-start | bytes 3145736 | tf_op jit(solution)/shard_map/ppermute | solution.py:35
  124.9 37.1 %collective-permute-start.8 = (bf16[256,2048]{1,0:T(8,128)(2,1)}, bf16[256,2048]{1,0:T(8,128)(2,1)}, u32[]{:S(2)}, u32[]{:S(2)}) collective-permute-start(bf16[256,2048]{1,0:T(8,128)(2,1)} %collective-permute-done.1.refs_2_), channel_id=1, source_target_pairs={{0,1},{1,0},{2,3},{3,2},{4,5},{5,4},{6,7},{7,6},{8,9},{9,8},{10,11... | collective-permute-start | bytes 3145736 | tf_op jit(solution)/shard_map/ppermute | solution.py:35
  126.4 13.0 %all-to-all-start.2 = ((bf16[4,8,16,512]{3,2,1,0:T(8,128)(2,1)}), bf16[4,8,16,512]{3,2,1,0:T(8,128)(2,1)S(1)}, u32[]{:S(2)}, u32[]{:S(2)}) async-start(bf16[4,8,16,512]{3,2,1,0:T(8,128)(2,1)} %add_convert_fusion), calls=%async_computation.2 | async-start | bytes 1048576 | tf_op jit(solution)/shard_map/all_to_all | solution.py:412
  130.1 54.2 %collective-permute-start.10 = (bf16[256,2048]{1,0:T(8,128)(2,1)}, bf16[256,2048]{1,0:T(8,128)(2,1)S(1)}, u32[]{:S(2)}, u32[]{:S(2)}) collective-permute-start(bf16[256,2048]{1,0:T(8,128)(2,1)} %collective-permute-done.4.refs_4_), channel_id=1, source_target_pairs={{0,1},{1,0},{2,3},{3,2},{4,5},{5,4},{6,7},{7,6},{8,9},{9,8},{10,11... | collective-permute-start | bytes 3145736 | tf_op jit(solution)/shard_map/ppermute | solution.py:35
  141.0 4.3 %collective-permute-start.15 = (bf16[4,16,512]{2,1,0:T(8,128)(2,1)S(1)}, bf16[4,16,512]{2,1,0:T(8,128)(2,1)S(1)}, u32[]{:S(2)}, u32[]{:S(2)}) collective-permute-start(bf16[4,16,512]{2,1,0:T(8,128)(2,1)S(1)} %get-tuple-element.18), channel_id=1, source_target_pairs={{0,8},{8,16},{16,24},{24,0},{1,9},{9,17},{17,25},{25,1},{2,10},{10... | collective-permute-start | bytes 196616 | tf_op jit(solution)/shard_map/ppermute | solution.py:35
  145.4 7.9 %collective-permute-start.16 = (bf16[4,16,512]{2,1,0:T(8,128)(2,1)S(1)}, bf16[4,16,512]{2,1,0:T(8,128)(2,1)S(1)}, u32[]{:S(2)}, u32[]{:S(2)}) collective-permute-start(bf16[4,16,512]{2,1,0:T(8,128)(2,1)S(1)} %get-tuple-element.18), channel_id=1, source_target_pairs={{0,16},{8,24},{16,0},{24,8},{1,17},{9,25},{17,1},{25,9},{2,18},{10... | collective-permute-start | bytes 196616 | tf_op jit(solution)/shard_map/ppermute | solution.py:35
  146.9 34.4 %all-to-all-start.3 = ((bf16[8,4,16,512]{3,2,1,0:T(8,128)(2,1)}), bf16[8,4,16,512]{3,2,1,0:T(8,128)(2,1)S(1)}, u32[]{:S(2)}, u32[]{:S(2)}) async-start(bf16[8,4,16,512]{3,2,1,0:T(8,128)(2,1)} %get-tuple-element.19), calls=%async_computation.3 | async-start | bytes 1048576 | tf_op jit(solution)/shard_map/all_to_all | solution.py:446
  153.3 3.2 %collective-permute-start.17 = (bf16[4,16,512]{2,1,0:T(8,128)(2,1)S(1)}, bf16[4,16,512]{2,1,0:T(8,128)(2,1)S(1)}, u32[]{:S(2)}, u32[]{:S(2)}) collective-permute-start(bf16[4,16,512]{2,1,0:T(8,128)(2,1)S(1)} %get-tuple-element.18), channel_id=1, source_target_pairs={{0,24},{8,0},{16,8},{24,16},{1,25},{9,1},{17,9},{25,17},{2,26},{10... | collective-permute-start | bytes 196616 | tf_op jit(solution)/shard_map/ppermute | solution.py:35
  156.5 28.5 %collective-permute-start.9 = (bf16[256,2048]{1,0:T(8,128)(2,1)}, bf16[256,2048]{1,0:T(8,128)(2,1)}, u32[]{:S(2)}, u32[]{:S(2)}) collective-permute-start(bf16[256,2048]{1,0:T(8,128)(2,1)} %collective-permute-done.2.refs_3_), channel_id=1, source_target_pairs={{0,1},{1,0},{2,3},{3,2},{4,5},{5,4},{6,7},{7,6},{8,9},{9,8},{10,11... | collective-permute-start | bytes 3145736 | tf_op jit(solution)/shard_map/ppermute | solution.py:35
  160.2 70.9 %copy-start.10 = (f32[22]{0:T(128)S(1)}, f32[22]{0:T(128)}, u32[]{:S(2)}) copy-start(f32[22]{0:T(128)} %param.29) | copy-start | bytes 268
  160.2 70.9 %copy-start.11 = (f32[22]{0:T(128)S(1)}, f32[22]{0:T(128)}, u32[]{:S(2)}) copy-start(f32[22]{0:T(128)} %param.28) | copy-start | bytes 268
  160.3 13.1 %collective-permute-start.18 = (bf16[4,4,16,512]{3,2,1,0:T(8,128)(2,1)S(1)}, bf16[4,4,16,512]{3,2,1,0:T(8,128)(2,1)S(1)}, u32[]{:S(2)}, u32[]{:S(2)}) collective-permute-start(bf16[4,4,16,512]{3,2,1,0:T(8,128)(2,1)S(1)} %pad_maximum_fusion.refs_14_), channel_id=1, source_target_pairs={{0,32},{32,64},{64,96},{96,128},{128,160},{160,192},{192,224},{224... | collective-permute-start | bytes 786440 | tf_op jit(solution)/shard_map/ppermute | solution.py:35
  162.0 11.4 %collective-permute-start.22 = (bf16[4,4,16,512]{3,2,1,0:T(8,128)(2,1)S(1)}, bf16[4,4,16,512]{3,2,1,0:T(8,128)(2,1)}, u32[]{:S(2)}, u32[]{:S(2)}) collective-permute-start(bf16[4,4,16,512]{3,2,1,0:T(8,128)(2,1)S(1)} %pad_maximum_fusion.refs_14_), channel_id=1, source_target_pairs={{0,224},{32,0},{64,32},{96,64},{128,96},{160,128},{192,160},{224,1... | collective-permute-start | bytes 786440 | tf_op jit(solution)/shard_map/ppermute | solution.py:35
  173.4 7.9 %collective-permute-start.19 = (bf16[4,4,16,512]{3,2,1,0:T(8,128)(2,1)S(1)}, bf16[4,4,16,512]{3,2,1,0:T(8,128)(2,1)}, u32[]{:S(2)}, u32[]{:S(2)}) collective-permute-start(bf16[4,4,16,512]{3,2,1,0:T(8,128)(2,1)S(1)} %collective-permute-done.18.refs_15_), channel_id=1, source_target_pairs={{0,32},{32,64},{64,96},{96,128},{128,160},{160,192},{192,224},{224... | collective-permute-start | bytes 786440 | tf_op jit(solution)/shard_map/ppermute | solution.py:35
  173.4 8.3 %collective-permute-start.23 = (bf16[4,4,16,512]{3,2,1,0:T(8,128)(2,1)}, bf16[4,4,16,512]{3,2,1,0:T(8,128)(2,1)}, u32[]{:S(2)}, u32[]{:S(2)}) collective-permute-start(bf16[4,4,16,512]{3,2,1,0:T(8,128)(2,1)} %collective-permute-done.22.refs_21_), channel_id=1, source_target_pairs={{0,224},{32,0},{64,32},{96,64},{128,96},{160,128},{192,160},{224,1... | collective-permute-start | bytes 786440 | tf_op jit(solution)/shard_map/ppermute | solution.py:35
  181.3 7.3 %collective-permute-start.20 = (bf16[4,4,16,512]{3,2,1,0:T(8,128)(2,1)}, bf16[4,4,16,512]{3,2,1,0:T(8,128)(2,1)}, u32[]{:S(2)}, u32[]{:S(2)}) collective-permute-start(bf16[4,4,16,512]{3,2,1,0:T(8,128)(2,1)} %collective-permute-done.19.refs_16_), channel_id=1, source_target_pairs={{0,32},{32,64},{64,96},{96,128},{128,160},{160,192},{192,224},{224... | collective-permute-start | bytes 786440 | tf_op jit(solution)/shard_map/ppermute | solution.py:35
  181.3 14.2 %collective-permute-start.25 = (bf16[8,4,16,512]{3,2,1,0:T(8,128)(2,1)S(1)}, bf16[8,4,16,512]{3,2,1,0:T(8,128)(2,1)S(1)}, u32[]{:S(2)}, u32[]{:S(2)}) collective-permute-start(bf16[8,4,16,512]{3,2,1,0:T(8,128)(2,1)S(1)} %all-to-all-done.3.refs_22_), channel_id=1, source_target_pairs={{0,8},{8,16},{16,24},{24,0},{1,9},{9,17},{17,25},{25,1},{2,10},{10... | collective-permute-start | bytes 1572872 | tf_op jit(solution)/shard_map/ppermute | solution.py:35
  181.7 24.1 %collective-permute-start.26 = (bf16[8,4,16,512]{3,2,1,0:T(8,128)(2,1)S(1)}, bf16[8,4,16,512]{3,2,1,0:T(8,128)(2,1)S(1)}, u32[]{:S(2)}, u32[]{:S(2)}) collective-permute-start(bf16[8,4,16,512]{3,2,1,0:T(8,128)(2,1)S(1)} %all-to-all-done.3.refs_22_), channel_id=1, source_target_pairs={{0,16},{8,24},{16,0},{24,8},{1,17},{9,25},{17,1},{25,9},{2,18},{10... | collective-permute-start | bytes 1572872 | tf_op jit(solution)/shard_map/ppermute | solution.py:35
  184.3 23.0 %collective-permute-start.27 = (bf16[8,4,16,512]{3,2,1,0:T(8,128)(2,1)S(1)}, bf16[8,4,16,512]{3,2,1,0:T(8,128)(2,1)S(1)}, u32[]{:S(2)}, u32[]{:S(2)}) collective-permute-start(bf16[8,4,16,512]{3,2,1,0:T(8,128)(2,1)S(1)} %all-to-all-done.3.refs_22_), channel_id=1, source_target_pairs={{0,24},{8,0},{16,8},{24,16},{1,25},{9,1},{17,9},{25,17},{2,26},{10... | collective-permute-start | bytes 1572872 | tf_op jit(solution)/shard_map/ppermute | solution.py:35
  185.0 6.2 %collective-permute-start.24 = (bf16[4,4,16,512]{3,2,1,0:T(8,128)(2,1)}, bf16[4,4,16,512]{3,2,1,0:T(8,128)(2,1)S(1)}, u32[]{:S(2)}, u32[]{:S(2)}) collective-permute-start(bf16[4,4,16,512]{3,2,1,0:T(8,128)(2,1)} %collective-permute-done.23.refs_20_), channel_id=1, source_target_pairs={{0,224},{32,0},{64,32},{96,64},{128,96},{160,128},{192,160},{224,1... | collective-permute-start | bytes 786440 | tf_op jit(solution)/shard_map/ppermute | solution.py:35
  188.6 6.9 %collective-permute-start.21 = (bf16[4,4,16,512]{3,2,1,0:T(8,128)(2,1)}, bf16[4,4,16,512]{3,2,1,0:T(8,128)(2,1)S(1)}, u32[]{:S(2)}, u32[]{:S(2)}) collective-permute-start(bf16[4,4,16,512]{3,2,1,0:T(8,128)(2,1)} %collective-permute-done.20.refs_17_), channel_id=1, source_target_pairs={{0,32},{32,64},{64,96},{96,128},{128,160},{160,192},{192,224},{224... | collective-permute-start | bytes 786440 | tf_op jit(solution)/shard_map/ppermute | solution.py:35
  222.2 18.3 %all-to-all-start.4 = ((f32[32,8,128]{2,1,0:T(8,128)}), f32[32,8,128]{2,1,0:T(8,128)S(1)}, u32[]{:S(2)}, u32[]{:S(2)}) async-start(f32[32,8,128]{2,1,0:T(8,128)} %logits.1), calls=%async_computation.4 | async-start | bytes 262144 | tf_op jit(solution)/shard_map/all_to_all | solution.py:460
  241.2 10.1 %all-to-all-start.5 = ((f32[8,8,128]{2,1,0:T(8,128)}), f32[8,8,128]{2,1,0:T(8,128)S(1)}, u32[]{:S(2)}, u32[]{:S(2)}) async-start(f32[8,8,128]{2,1,0:T(8,128)} %get-tuple-element.22), calls=%async_computation.5 | async-start | bytes 65536 | tf_op jit(solution)/shard_map/all_to_all | solution.py:465
